TPU v7x, 32 devices: a whole 2x2x4 slice. The times are simulated.
32 devices in a mesh: grp: 8 (over z, y), blk: 4 (over x, core).
Axes of the slice: x: 2, y: 2, z: 4, core: 2. Of those that a mesh axis runs over, the one named last changes fastest.
Arguments:
- query: bfloat16 [4096, 512], P(('grp', 'blk')), may hold values from -6 to 6
- key: bfloat16 [4096, 512], P(('grp', 'blk')), may hold values from -6 to 6
- value: bfloat16 [4096, 512], P(('grp', 'blk')), may hold values from -6 to 6
- gate_u: bfloat16 [4096, 512], P(('grp', 'blk')), may hold values from -6 to 6
- out_grad: bfloat16 [4096, 1024], P(('grp', 'blk')), may hold values from -6 to 6
- lengths: int32 [8], P('grp'), may hold values from 32 to 512
- norm_gain: float32 [512], replicated, may hold values from 0.1 to 1.9
- out_weight: bfloat16 [512, 1024], replicated, may hold values from -0.25 to 0.25
Outputs:
- layer_out: bfloat16 [4096, 1024], P(('grp', 'blk'))
- grad_query: bfloat16 [4096, 512], P(('grp', 'blk'))
- grad_key: bfloat16 [4096, 512], P(('grp', 'blk'))
- grad_value: bfloat16 [4096, 512], P(('grp', 'blk'))
- grad_gate: bfloat16 [4096, 512], P(('grp', 'blk'))
- grad_weight: float32 [512, 1024], P(None, 'blk')
Inputs may be any that keep to these rules, and one draw needn't show every extreme that they name: `lengths`: events of a user at or past its length are padding.
All inputs are finite; a program needn't handle non-finite values.
Results may differ from a plain program's by a relative error of at most 0.009.
Values may be sent and summed in bfloat16 or wider, within the bound.
No kernel may reach another device: no remote copies, remote signals or barrier semaphores. Data moves between devices by JAX's collectives and lax.ppermute only.
A program may use at most 64 MiB of HBM per device.

v0:
```python
import math

import jax
import jax.numpy as jnp
from jax import lax
from jax.sharding import PartitionSpec as P

HEADS = 8
HEAD = 64


EPS = 1e-05


def causal_mask(query_pos, key_pos, length):
    return (
        (key_pos[None, :] <= query_pos[:, None])
        & (query_pos[:, None] < length)
        & (key_pos[None, :] < length)
    )


def over_blocks(total_rows, step_fn, initial):
    size = math.gcd(total_rows, 512)

    def advance(index, carry):
        return step_fn(carry, index * size, size)

    return lax.fori_loop(0, total_rows // size, advance, initial)


def shards(query, key, value, gate_u, out_grad, lengths, norm_gain, out_weight):
    rows = query.shape[0]
    scale = HEAD ** (-0.5)
    length = lengths[0]
    lanes = lax.axis_size("blk")
    position = lax.axis_index("blk")
    first_row = position * rows
    row_pos = first_row + jnp.arange(rows, dtype=jnp.int32)
    total_len = rows * lanes
    query_heads = query.reshape(rows, HEADS, HEAD)
    key_heads = key.reshape(rows, HEADS, HEAD)
    value_heads = value.reshape(rows, HEADS, HEAD)
    zeros = jnp.zeros((rows, HEADS, HEAD), jnp.float32)
    keys_all, values_all = (
        lax.all_gather(key, "blk", axis=0, tiled=True),
        lax.all_gather(value, "blk", axis=0, tiled=True),
    )

    def forward_step(carry, begin, size):
        key_block = lax.dynamic_slice_in_dim(keys_all, begin, size, 0).reshape(size, HEADS, HEAD)
        value_block = lax.dynamic_slice_in_dim(values_all, begin, size, 0).reshape(
            size, HEADS, HEAD
        )
        scores = (
            jnp.einsum("rhd,nhd->hrn", query_heads, key_block, preferred_element_type=jnp.float32)
            * scale
        )
        mask = causal_mask(row_pos, begin + jnp.arange(size, dtype=jnp.int32), length)
        weights = (jax.nn.silu(scores) * mask[None]).astype(jnp.bfloat16)
        return carry + jnp.einsum(
            "hrn,nhd->rhd", weights, value_block, preferred_element_type=jnp.float32
        )

    attended = over_blocks(total_len, forward_step, zeros).reshape(rows, HEADS * HEAD)
    centre = attended - jnp.mean(attended, axis=1, keepdims=True)
    inv_std = lax.rsqrt(jnp.mean(centre * centre, axis=1, keepdims=True) + EPS)
    normed = centre * inv_std
    scaled = normed * norm_gain
    gates = gate_u.astype(jnp.float32)
    mixed = (scaled * gates).astype(jnp.bfloat16)
    layer_out = jnp.dot(mixed, out_weight, preferred_element_type=jnp.float32).astype(jnp.bfloat16)
    mixed_grad = lax.dot_general(
        out_grad, out_weight, (((1,), (1,)), ((), ())), preferred_element_type=jnp.float32
    )
    grad_gate = (mixed_grad * scaled).astype(jnp.bfloat16)
    normed_grad = mixed_grad * gates * norm_gain
    attended_grad = inv_std * (
        normed_grad
        - jnp.mean(normed_grad, axis=1, keepdims=True)
        - normed * jnp.mean(normed_grad * normed, axis=1, keepdims=True)
    )
    attended_grad = attended_grad.astype(jnp.bfloat16)
    grad_heads = attended_grad.reshape(rows, HEADS, HEAD)
    weight_term = lax.dot_general(
        mixed, out_grad, (((0,), (0,)), ((), ())), preferred_element_type=jnp.float32
    )

    def query_step(carry, begin, size):
        key_block = lax.dynamic_slice_in_dim(keys_all, begin, size, 0).reshape(size, HEADS, HEAD)
        value_block = lax.dynamic_slice_in_dim(values_all, begin, size, 0).reshape(
            size, HEADS, HEAD
        )
        scores = (
            jnp.einsum("rhd,nhd->hrn", query_heads, key_block, preferred_element_type=jnp.float32)
            * scale
        )
        mask = causal_mask(row_pos, begin + jnp.arange(size, dtype=jnp.int32), length)
        sigma = jax.nn.sigmoid(scores)
        prob_grad = jnp.einsum(
            "rhd,nhd->hrn", grad_heads, value_block, preferred_element_type=jnp.float32
        )
        score_grad = (prob_grad * sigma * (1.0 + scores * (1.0 - sigma)) * mask[None]).astype(
            jnp.bfloat16
        )
        return carry + jnp.einsum(
            "hrn,nhd->rhd", score_grad, key_block, preferred_element_type=jnp.float32
        )

    grad_query = (
        (over_blocks(total_len, query_step, zeros) * scale)
        .reshape(rows, HEADS * HEAD)
        .astype(jnp.bfloat16)
    )
    query_piece = lax.all_gather(query, "blk", axis=0, tiled=True)
    grad_piece = lax.all_gather(attended_grad, "blk", axis=0, tiled=True)
    count = query_piece.shape[0]

    def inner(acc, begin, size):
        key_acc, value_acc = acc
        query_block = lax.dynamic_slice_in_dim(query_piece, begin, size, 0).reshape(
            size, HEADS, HEAD
        )
        grad_block = lax.dynamic_slice_in_dim(grad_piece, begin, size, 0).reshape(size, HEADS, HEAD)
        scores = (
            jnp.einsum("nhd,rhd->hnr", query_block, key_heads, preferred_element_type=jnp.float32)
            * scale
        )
        mask = causal_mask(begin + jnp.arange(size, dtype=jnp.int32), row_pos, length)
        weights = (jax.nn.silu(scores) * mask[None]).astype(jnp.bfloat16)
        sigma = jax.nn.sigmoid(scores)
        prob_grad = jnp.einsum(
            "nhd,rhd->hnr", grad_block, value_heads, preferred_element_type=jnp.float32
        )
        score_grad = (prob_grad * sigma * (1.0 + scores * (1.0 - sigma)) * mask[None]).astype(
            jnp.bfloat16
        )
        key_acc = key_acc + jnp.einsum(
            "hnr,nhd->rhd", score_grad, query_block, preferred_element_type=jnp.float32
        )
        value_acc = value_acc + jnp.einsum(
            "hnr,nhd->rhd", weights, grad_block, preferred_element_type=jnp.float32
        )
        return (key_acc, value_acc)

    key_acc, value_acc = over_blocks(count, inner, (zeros, zeros))
    grad_key = (key_acc * scale).reshape(rows, HEADS * HEAD).astype(jnp.bfloat16)
    grad_value = value_acc.reshape(rows, HEADS * HEAD).astype(jnp.bfloat16)
    column_part = lax.psum_scatter(weight_term, "blk", scatter_dimension=1, tiled=True)
    grad_weight = lax.psum(column_part, "grp")
    return (layer_out, grad_query, grad_key, grad_value, grad_gate, grad_weight)


def solution(mesh):
    return jax.shard_map(
        shards,
        mesh=mesh,
        in_specs=(
            P(("grp", "blk"), None),
            P(("grp", "blk"), None),
            P(("grp", "blk"), None),
            P(("grp", "blk"), None),
            P(("grp", "blk"), None),
            P("grp"),
            P(),
            P(),
        ),
        out_specs=(
            P(("grp", "blk"), None),
            P(("grp", "blk"), None),
            P(("grp", "blk"), None),
            P(("grp", "blk"), None),
            P(("grp", "blk"), None),
            P(None, "blk"),
        ),
        check_vma=False,
    )
```

profile of v0, /device:TPU:0, one launch (start us, length us, event | category | flops | bytes accessed | tf_op | source)
XLA Modules:
  0.0 158.3 jit_solution(8994347896110078273)
XLA Ops:
  7.2 9.0 %all_gather.13 = bf16[512,512]{1,0:T(8,128)(2,1)S(1)} all-gather(bf16[128,512]{1,0:T(8,128)(2,1)} %param.10), channel_id=1, replica_groups=mesh['grp'=8,'blk'=4] {'blk'}, dimensions={0}, use_global_device_ids=true | all-gather | bytes 655360 | tf_op jit(solution)/shard_map/all_gather | solution.py:47
  16.2 1.0 copy.26
  17.2 1.0 copy.24
  18.3 7.5 %all_gather.12 = bf16[512,512]{1,0:T(8,128)(2,1)S(1)} all-gather(bf16[128,512]{1,0:T(8,128)(2,1)} %param.9), channel_id=1, replica_groups=mesh['grp'=8,'blk'=4] {'blk'}, dimensions={0}, use_global_device_ids=true | all-gather | bytes 655360 | tf_op jit(solution)/shard_map/all_gather | solution.py:46
  25.7 1.0 copy.25
  27.5 1.5 fusion.33
  29.0 0.1 fusion.19
  29.1 2.0 %fusion.32 = (f32[128]{0:T(128)S(1)}, f32[8,128,64]{1,2,0:T(8,128)S(1)}) fusion(bf16[512,8,64]{0,2,1:T(8,128)(2,1)} %bitcast.51, f32[8,128,512]{2,1,0:T(8,128)S(1)} %fusion.33, f32[128,512]{1,0:T(8,128)S(1)} %fusion.19), kind=kOutput, calls=%fused_computation.56 | convolution fusion | flops 70844288 | bytes 3146240 | tf_op jit(solution)/shard_map/while/body/eval_jaxpr/hrn,nhd->rhd/dot_general | solution.py:61
  31.3 0.5 add_rsqrt_fusion
  31.9 1.1 copy.27
  33.0 1.6 %fusion.23 = (f32[128]{0:T(128)S(1)}, f32[128]{0:T(128)S(1)}, f32[128,512]{1,0:T(8,128)S(1)}) fusion(f32[512]{0:T(512)S(1)} %copy-done.12, bf16[128,512]{1,0:T(8,128)(2,1)S(1)} %copy-done.9, f32[128]{0:T(128)} %add_rsqrt_fusion, f32[128,512]{1,0:T(8,128)S(1)} %copy.27, f32[128]{0:T(128)S(1)} %broadcast_multiply_fusion.2, bf16[128,1024]{1,0:T(8,128)(2,1)} %param.12, ...), kind=kOutput, calls=%fused_computation.40 | convolution fusion | flops 134741760 | bytes 1970176 | tf_op jit(solution)/shard_map/dot_general | solution.py:73
  34.6 1.8 %multiply_convert_fusion.6 = (bf16[128,512]{1,0:T(8,128)(2,1)}, bf16[128,512]{1,0:T(8,128)(2,1)S(1)}, bf16[128,512]{1,0:T(8,128)(2,1)S(1)}) fusion(f32[128,512]{1,0:T(8,128)S(1)} %get-tuple-element.96, f32[128,512]{1,0:T(8,128)S(1)} %copy.27, f32[512]{0:T(512)S(1)} %copy-done.12, f32[128]{0:T(128)} %add_rsqrt_fusion, f32[128]{0:T(128)S(1)} %broadcast_multiply_fusion.2, ...), kind=kLoop, calls=%fused_computation.28 | loop fusion | flops 983040 | bytes 1052672 | tf_op jit(solution)/shard_map/convert_element_type | solution.py:76
  36.4 0.6 copy-done.1
  37.0 1.8 %fusion.35 = f32[512,1024]{1,0:T(8,128)} fusion(bf16[128,512]{1,0:T(8,128)(2,1)S(1)} %get-tuple-element.93, bf16[128,1024]{1,0:T(8,128)(2,1)S(1)} %copy-done.3), kind=kOutput, calls=%fused_computation.59 | convolution fusion | flops 134217728 | bytes 2490368 | tf_op jit(solution)/shard_map/dot_general | solution.py:85
  38.9 0.8 copy.32
  39.7 0.7 copy.30
  40.6 3.3 %fusion.5 = bf16[8,128,64]{1,2,0:T(8,128)(2,1)} fusion(bf16[512,8,64]{0,2,1:T(8,128)(2,1)} %bitcast.47, f32[8,128,512]{2,1,0:T(8,128)S(1)} %fusion.33, bf16[128,8,64]{0,2,1:T(8,128)(2,1)S(1)} %bitcast.59, bf16[512,8,64]{0,2,1:T(8,128)(2,1)} %bitcast.52, f32[128,512]{1,0:T(8,128)} %copy-done.10), kind=kOutput, calls=%fused_computation.12 | convolution fusion | flops 140115968 | bytes 3670016 | tf_op jit(solution)/shard_map/while/body/eval_jaxpr/hrn,nhd->rhd/dot_general | solution.py:106
  43.9 1.7 %copy.33 = bf16[128,512]{1,0:T(8,128)(2,1)} copy(bf16[128,512]{0,1:T(8,128)(2,1)} %bitcast.58) | data formatting | bytes 262144
  45.6 7.3 %all_gather.15 = bf16[512,512]{1,0:T(8,128)(2,1)S(1)} all-gather(bf16[128,512]{1,0:T(8,128)(2,1)S(1)} %copy-done.7), channel_id=1, replica_groups=mesh['grp'=8,'blk'=4] {'blk'}, dimensions={0}, use_global_device_ids=true | all-gather | bytes 655360 | tf_op jit(solution)/shard_map/all_gather | solution.py:115
  52.8 1.0 copy.31
  53.8 9.5 %all_gather.14 = bf16[512,512]{1,0:T(8,128)(2,1)S(1)} all-gather(bf16[128,512]{1,0:T(8,128)(2,1)S(1)} %get-tuple-element.92), channel_id=1, replica_groups=mesh['grp'=8,'blk'=4] {'blk'}, dimensions={0}, use_global_device_ids=true | all-gather | bytes 655360 | tf_op jit(solution)/shard_map/all_gather | solution.py:116
  63.3 1.0 copy.29
  64.3 0.1 fusion.22
  64.5 1.6 %fusion.34 = f32[8,512,128]{2,1,0:T(8,128)S(1)} fusion(bf16[512,8,64]{0,2,1:T(8,128)(2,1)} %bitcast.48, bf16[128,8,64]{0,2,1:T(8,128)(2,1)S(1)} %bitcast.55), kind=kOutput, calls=%fused_computation.58 | convolution fusion | flops 67108864 | bytes 2752512 | tf_op jit(solution)/shard_map/while/body/eval_jaxpr/nhd,rhd->hnr/dot_general | solution.py:126
  66.2 2.6 %fusion.4 = bf16[8,128,64]{1,2,0:T(8,128)(2,1)S(1)} fusion(bf16[512,8,64]{0,2,1:T(8,128)(2,1)} %bitcast.49, f32[8,512,128]{2,1,0:T(8,128)S(1)} %fusion.34, bf16[512,8,64]{0,2,1:T(8,128)(2,1)} %bitcast.53, bf16[128,8,64]{0,2,1:T(8,128)(2,1)} %bitcast.57, f32[512,128]{1,0:T(8,128)S(1)} %fusion.22), kind=kOutput, calls=%fused_computation.11 | convolution fusion | flops 140115968 | bytes 3670016 | tf_op jit(solution)/shard_map/while/body/eval_jaxpr/hnr,nhd->rhd/dot_general | solution.py:138
  68.8 0.8 copy.34
  69.5 3.2 %reduce-scatter.2.cloned.1.call-done = f32[512,256]{1,0:T(8,128)} async-done(((f32[512,1024]{1,0:T(8,128)}), f32[512,256]{1,0:T(8,128)}) %reduce-scatter.2.cloned.1.call-update) | async-done | bytes 524304 | tf_op jit(solution)/shard_map/reduce_scatter | solution.py:149
  72.7 2.0 %convolution_convert_fusion.1 = bf16[8,64,128]{2,1,0:T(8,128)(2,1)S(1)} fusion(bf16[512,8,64]{0,2,1:T(8,128)(2,1)} %bitcast.54, f32[8,512,128]{2,1,0:T(8,128)S(1)} %fusion.34, f32[512,128]{1,0:T(8,128)} %copy-done.11), kind=kOutput, calls=%fused_computation.13 | convolution fusion | flops 70844416 | bytes 3014656 | tf_op jit(solution)/shard_map/while/body/eval_jaxpr/hnr,nhd->rhd/dot_general | solution.py:141
  74.7 0.8 copy.35
  75.5 1.0 convolution_convert_fusion
  76.5 73.1 %all-reduce.2.cloned.1.call-done = f32[512,256]{1,0:T(8,128)} async-done(((f32[512,256]{1,0:T(8,128)}), f32[512,256]{1,0:T(8,128)}) %all-reduce.2.cloned.1.call-update) | async-done | bytes 524304 | tf_op jit(solution)/shard_map/psum | solution.py:150
  149.6 1.9 %copy.38 = f32[512,256]{1,0:T(8,128)} copy(f32[512,256]{1,0:T(8,128)} %all-reduce.2.cloned.1.call-done) | data formatting | bytes 1048576
  (40 shorter events, 0.5 us)
Async XLA Ops:
  7.2 25.8 %copy-start = (bf16[512,1024]{1,0:T(8,128)(2,1)S(1)}, bf16[512,1024]{1,0:T(8,128)(2,1)}, u32[]{:S(2)}) copy-start(bf16[512,1024]{1,0:T(8,128)(2,1)} %param.15) | copy-start | bytes 3145732
  7.2 65.5 %reduce-scatter.2.cloned.1.call-start = ((), (), s32[]{:S(2)}) async-start(), calls=%async_computation.1 | async-start | bytes 2621440 | tf_op jit(solution)/shard_map/reduce_scatter | solution.py:149
  27.4 3.7 %copy-start.13 = (pred[512]{0:T(512)(128)(4,1)}, pred[512]{0:T(512)(128)(4,1)S(1)}, u32[]{:S(2)}) copy-start(pred[512]{0:T(512)(128)(4,1)S(1)} %iota_compare_fusion.2) | copy-start | bytes 1540
  29.1 2.1 %copy-start.10 = (f32[128,512]{1,0:T(8,128)}, f32[128,512]{1,0:T(8,128)S(1)}, u32[]{:S(2)}) copy-start(f32[128,512]{1,0:T(8,128)S(1)} %fusion.19) | copy-start | bytes 786436
  29.1 3.9 %copy-start.9 = (bf16[128,512]{1,0:T(8,128)(2,1)S(1)}, bf16[128,512]{1,0:T(8,128)(2,1)}, u32[]{:S(2)}) copy-start(bf16[128,512]{1,0:T(8,128)(2,1)} %param.11) | copy-start | bytes 393220
  29.1 3.9 %copy-start.12 = (f32[512]{0:T(512)S(1)}, f32[512]{0:T(512)}, u32[]{:S(2)}) copy-start(f32[512]{0:T(512)} %param.14) | copy-start | bytes 6148
  31.2 0.7 copy-start.4
  33.0 4.0 %copy-start.3 = (bf16[128,1024]{1,0:T(8,128)(2,1)S(1)}, bf16[128,1024]{1,0:T(8,128)(2,1)}, u32[]{:S(2)}) copy-start(bf16[128,1024]{1,0:T(8,128)(2,1)} %param.12) | copy-start | bytes 786436
  36.4 0.6 copy-start.1
  37.0 1.9 %copy-start.5 = (bf16[128,512]{1,0:T(8,128)(2,1)S(1)}, bf16[128,512]{1,0:T(8,128)(2,1)}, u32[]{:S(2)}) copy-start(bf16[128,512]{1,0:T(8,128)(2,1)} %param.9) | copy-start | bytes 393220
  37.0 2.7 %copy-start.6 = (bf16[128,512]{1,0:T(8,128)(2,1)S(1)}, bf16[128,512]{1,0:T(8,128)(2,1)}, u32[]{:S(2)}) copy-start(bf16[128,512]{1,0:T(8,128)(2,1)} %param.10) | copy-start | bytes 393220
  38.9 110.8 %all-reduce.2.cloned.1.call-start = ((), (), s32[]{:S(2)}) async-start(), calls=%async_computation.2 | async-start | bytes 1048576 | tf_op jit(solution)/shard_map/psum | solution.py:150
  40.6 5.0 %copy-start.7 = (bf16[128,512]{1,0:T(8,128)(2,1)S(1)}, bf16[128,512]{1,0:T(8,128)(2,1)}, u32[]{:S(2)}) copy-start(bf16[128,512]{1,0:T(8,128)(2,1)} %param.8) | copy-start | bytes 393220
  43.9 20.5 %copy-start.14 = (pred[512]{0:T(512)(128)(4,1)S(1)}, pred[512]{0:T(512)(128)(4,1)}, u32[]{:S(2)}) copy-start(pred[512]{0:T(512)(128)(4,1)} %copy-done.13) | copy-start | bytes 1540
  43.9 20.6 %copy-start.8 = (bf16[128,512]{0,1:T(8,128)(2,1)S(1)}, bf16[128,512]{0,1:T(8,128)(2,1)}, u32[]{:S(2)}) copy-start(bf16[128,512]{0,1:T(8,128)(2,1)} %copy.32) | copy-start | bytes 393220
  64.5 4.3 %copy-start.11 = (f32[512,128]{1,0:T(8,128)}, f32[512,128]{1,0:T(8,128)S(1)}, u32[]{:S(2)}) copy-start(f32[512,128]{1,0:T(8,128)S(1)} %fusion.22) | copy-start | bytes 786436
  72.7 2.8 %copy-start.2 = (bf16[128,512]{1,0:T(8,128)(2,1)S(1)}, bf16[128,512]{1,0:T(8,128)(2,1)}, u32[]{:S(2)}) copy-start(bf16[128,512]{1,0:T(8,128)(2,1)} %copy-done.1) | copy-start | bytes 393220
Sparse Core Ops, SparseCore 0:
  39.0 33.6 reduce-scatter.1
  76.1 73.4 all-reduce.1
where the time goes:
time: 159 us; the launch traced here: 158 us
  waiting for transfers between devices  76.3 us (48%)
  blocking collectives  33.2 us (21%)
  matrix products  17.5 us (11%)
  between operations  14.9 us (9%)
  local copies, waits for them, and re-layouts  13.7 us (9%)
  other arithmetic  2.64 us (2%)
    psum x1, waiting for transfers between devices, shards(): grad_weight = lax.psum(column_part, 'grp')  73.1 us
    all_gather x1, blocking collectives, shards(): grad_piece = lax.all_gather(attended_grad, 'blk', axis=0, tiled=True)  9.49 us
    all_gather x1, blocking collectives, shards(): lax.all_gather(value, 'blk', axis=0, tiled=True)  8.99 us
    unnamed x37, local copies, waits for them, and re-layouts  8.42 us
    all_gather x1, blocking collectives, shards(): lax.all_gather(key, 'blk', axis=0, tiled=True)  7.49 us
    all_gather x1, blocking collectives, shards(): query_piece = lax.all_gather(query, 'blk', axis=0, tiled=True)  7.27 us
    dot_general x1, matrix products, query_step(): jnp.einsum('hrn,nhd->rhd', score_grad, key_block, preferred_element_type=...  3.29 us
  transfers between devices with their start and end apart: 2, of which 2 were waited for; matrix products, arithmetic and copies ran while one was open for 11% of the time, Pallas kernels for 0%

commit v1 on v0

v1 whole, which is shorter than its diff:
```python
import functools

import jax
import jax.numpy as jnp
from jax import lax
from jax.experimental import pallas as pl
from jax.experimental.pallas import tpu as pltpu
from jax.sharding import PartitionSpec as P

HEADS = 8
HEAD = 64
PAIR = 2 * HEAD
EPS = 1e-05
F32 = jnp.float32
BF16 = jnp.bfloat16
CORES = 2

NT = (((1,), (1,)), ((), ()))
NN = (((1,), (0,)), ((), ()))


def dot(a, b, dims=NN):
    return lax.dot_general(a, b, dims, preferred_element_type=F32)


def call(kernel, outs, *args, scalars=0, scratch=(), flops=0):
    smem = pl.BlockSpec(memory_space=pltpu.SMEM)
    vmem = pl.BlockSpec(memory_space=pltpu.VMEM)
    return pl.pallas_call(
        kernel,
        out_shape=[jax.ShapeDtypeStruct(s, d) for s, d in outs],
        in_specs=[smem] * scalars + [vmem] * (len(args) - scalars),
        out_specs=[vmem] * len(outs),
        scratch_shapes=list(scratch),
        cost_estimate=pl.CostEstimate(flops=flops, transcendentals=0, bytes_accessed=0),
    )(*args)


def partner(index, k, size):
    if size & (size - 1) == 0:
        return index ^ k
    return (index + k) % size


def source(index, k, size):
    if size & (size - 1) == 0:
        return index ^ k
    return (index - k) % size if isinstance(index, int) else lax.rem(index - k + size, size)


def target(index, k, size):
    if size & (size - 1) == 0:
        return index ^ k
    return lax.rem(index + k, size)


def swap_core(x, lanes, down=None):
    pairs = [(i, i ^ 1) for i in range(lanes)]
    if down is not None:
        pairs = [(s, d) for s, d in pairs if (d < s) == down]
    return lax.ppermute(x, "blk", pairs)


def over_chips(x, lanes, k, down):
    step = -k * CORES if down else k * CORES
    pairs = [(i, i + step) for i in range(lanes) if 0 <= i + step < lanes]
    return lax.ppermute(x, "blk", pairs)


def digits(groups):
    out, stride = [], 1
    for size in (2, 4):
        if groups // stride > 1 and (groups // stride) % size == 0:
            out.append((stride, size))
            stride *= size
    if groups // stride > 1:
        out.append((stride, groups // stride))
    return out


def over_digit(x, groups, digit, k):
    stride, size = digit
    pairs = []
    for i in range(groups):
        d = (i // stride) % size
        pairs.append((i, i + (partner(d, k, size) - d) * stride))
    return lax.ppermute(x, "grp", pairs)


def digit_of(digit):
    stride, size = digit
    return lax.rem(lax.div(lax.axis_index("grp"), jnp.int32(stride)), jnp.int32(size))


def low_lanes(shape):
    return lax.broadcasted_iota(jnp.int32, shape, 1) < HEAD


def two_heads(x):
    low = low_lanes(x.shape)
    zero = jnp.zeros_like(x)
    return jnp.concatenate([jnp.where(low, x, zero), jnp.where(low, zero, x)], axis=0)


def one_pair(x):
    rows = x.shape[0] // 2
    top, bottom = x[:rows], x[rows:]
    return jnp.where(low_lanes(top.shape), top, bottom)


def store_blocks(dst, refs, lanes, later):
    pos = lax.axis_index("blk")
    rows = refs[0].shape[0]
    chips = lanes // CORES
    chip, core = lax.div(pos, CORES), lax.rem(pos, CORES)
    for n, ref in enumerate(refs):
        step, other = n // 2, n % 2
        move = step if later else chips - step
        block = lax.rem(chip + move, chips) * CORES + lax.rem(core + other, CORES)
        dst[pl.ds(pl.multiple_of(block * rows, rows), rows), :] = ref[...]


def limits(length, shape, rows):
    pos = lax.axis_index("blk")
    local = lax.rem(lax.broadcasted_iota(jnp.int32, shape, 0), rows)
    row = local + pos * rows
    return jnp.where(row < length, row, -1)


def mixed_grad_kernel(og_ref, w_ref, mg_ref):
    mg_ref[...] = dot(og_ref[...], w_ref[...], NT)


def forward_kernel(lanes, *refs):
    count = lanes
    len_ref, q_ref = refs[:2]
    k_refs = refs[2 : 2 + count]
    v_refs = refs[2 + count : 2 + 2 * count]
    gate_ref, gain_ref, mg_ref = refs[2 + 2 * count : 5 + 2 * count]
    mixed_ref, mixed_t_ref, ag_ref, gg_ref, kall, vall = refs[5 + 2 * count : 11 + 2 * count]
    att = refs[-1]
    length = len_ref[0]
    rows, feats = q_ref.shape
    total = kall.shape[0]
    tile = min(total, 512)
    store_blocks(kall, k_refs, lanes, False)
    store_blocks(vall, v_refs, lanes, False)
    limit = limits(length, (2 * rows, tile), rows)
    key = lax.broadcasted_iota(jnp.int32, (2 * rows, tile), 1)
    for p in range(feats // PAIR):
        cols = slice(p * PAIR, (p + 1) * PAIR)
        lhs = two_heads(q_ref[:, cols] * BF16(HEAD ** -0.5 / 2))

        def step(t, acc, lhs=lhs, cols=cols):
            at = pl.ds(pl.multiple_of(t * tile, tile), tile)
            half = dot(lhs, kall[at, cols], NT)
            weight = jnp.where(key + t * tile <= limit, half + half * jnp.tanh(half), 0.0)
            return acc + dot(weight.astype(BF16), vall[at, cols])

        zero = jnp.zeros((2 * rows, PAIR), F32)
        acc = step(0, zero) if total == tile else lax.fori_loop(0, total // tile, step, zero)
        att[:, cols] = one_pair(acc)
    attended = att[...]
    centre = attended - jnp.mean(attended, axis=1, keepdims=True)
    inv_std = lax.rsqrt(jnp.mean(centre * centre, axis=1, keepdims=True) + EPS)
    normed = centre * inv_std
    gain = gain_ref[...]
    scaled = normed * gain
    gates = gate_ref[...].astype(F32)
    mixed = scaled * gates
    mixed_ref[...] = mixed.astype(BF16)
    mixed_t_ref[...] = mixed.T.astype(BF16)
    mixed_grad = mg_ref[...]
    gg_ref[...] = (mixed_grad * scaled).astype(BF16)
    normed_grad = mixed_grad * gates * gain
    grad = inv_std * (
        normed_grad
        - jnp.mean(normed_grad, axis=1, keepdims=True)
        - normed * jnp.mean(normed_grad * normed, axis=1, keepdims=True)
    )
    ag_ref[...] = grad.astype(BF16)


def query_kernel(len_ref, q_ref, kall, vall, ag_ref, mixed_ref, w_ref, lo_ref, dq_ref):
    length = len_ref[0]
    rows, feats = q_ref.shape
    total = kall.shape[0]
    tile = min(total, 512)
    lo_ref[...] = dot(mixed_ref[...], w_ref[...]).astype(BF16)
    limit = limits(length, (2 * rows, tile), rows)
    key = lax.broadcasted_iota(jnp.int32, (2 * rows, tile), 1)
    for p in range(feats // PAIR):
        cols = slice(p * PAIR, (p + 1) * PAIR)
        lhs = two_heads(q_ref[:, cols] * BF16(HEAD ** -0.5 / 2))
        grad = two_heads(ag_ref[:, cols])

        def step(t, acc, lhs=lhs, grad=grad, cols=cols):
            at = pl.ds(pl.multiple_of(t * tile, tile), tile)
            half = dot(lhs, kall[at, cols], NT)
            prob_grad = dot(grad, vall[at, cols], NT)
            th = jnp.tanh(half)
            slope = (0.5 + 0.5 * th) * (1.0 + half * (1.0 - th))
            score_grad = jnp.where(key + t * tile <= limit, prob_grad * slope, 0.0)
            return acc + dot(score_grad.astype(BF16), kall[at, cols])

        zero = jnp.zeros((2 * rows, PAIR), F32)
        acc = step(0, zero) if total == tile else lax.fori_loop(0, total // tile, step, zero)
        dq_ref[:, cols] = (one_pair(acc) * HEAD ** -0.5).astype(BF16)


def key_kernel(lanes, *refs):
    count = lanes
    len_ref, k_ref, v_ref = refs[:3]
    q_refs = refs[3 : 3 + count]
    g_refs = refs[3 + count : 3 + 2 * count]
    dk_ref, dv_ref, qall, gall = refs[3 + 2 * count :]
    length = len_ref[0]
    rows, feats = k_ref.shape
    total = qall.shape[0]
    tile = min(total, 512)
    store_blocks(qall, q_refs, lanes, True)
    store_blocks(gall, g_refs, lanes, True)
    pos = lax.axis_index("blk")
    mine = lax.rem(lax.broadcasted_iota(jnp.int32, (2 * rows, tile), 0), rows) + pos * rows
    query = lax.broadcasted_iota(jnp.int32, (2 * rows, tile), 1)
    for p in range(feats // PAIR):
        cols = slice(p * PAIR, (p + 1) * PAIR)
        lhs = two_heads(k_ref[:, cols] * BF16(HEAD ** -0.5 / 2))
        val = two_heads(v_ref[:, cols])

        def step(t, carry, lhs=lhs, val=val, cols=cols):
            dk, dv = carry
            at = pl.ds(pl.multiple_of(t * tile, tile), tile)
            half = dot(lhs, qall[at, cols], NT)
            prob_grad = dot(val, gall[at, cols], NT)
            where = query + t * tile
            live = (mine <= where) & (where < length)
            th = jnp.tanh(half)
            weight = jnp.where(live, half + half * th, 0.0)
            slope = (0.5 + 0.5 * th) * (1.0 + half * (1.0 - th))
            score_grad = jnp.where(live, prob_grad * slope, 0.0)
            dk = dk + dot(score_grad.astype(BF16), qall[at, cols])
            dv = dv + dot(weight.astype(BF16), gall[at, cols])
            return dk, dv

        zero = jnp.zeros((2 * rows, PAIR), F32)
        carry = (zero, zero)
        carry = step(0, carry) if total == tile else lax.fori_loop(0, total // tile, step, carry)
        dk_ref[:, cols] = (one_pair(carry[0]) * HEAD ** -0.5).astype(BF16)
        dv_ref[:, cols] = one_pair(carry[1]).astype(BF16)


def split(total_ref, digit, keep_ref, send_refs):
    size = 1 + len(send_refs)
    part = keep_ref.shape[0]
    mine = digit_of(digit)
    keep_ref[...] = total_ref[pl.ds(pl.multiple_of(mine * part, part), part), :]
    for k, ref in enumerate(send_refs, 1):
        at = target(mine, k, size)
        ref[...] = total_ref[pl.ds(pl.multiple_of(at * part, part), part), :].astype(BF16)


def product_kernel(lanes, digit, *refs):
    m_refs, o_refs = refs[:lanes], refs[lanes : 2 * lanes]
    outs, acc = refs[2 * lanes : -1], refs[-1]
    acc[...] = sum(dot(m[...], o[...]) for m, o in zip(m_refs, o_refs))
    split(acc, digit, outs[0], outs[1:])


def sum_split_kernel(count, whole, digit, *refs):
    outs, acc = refs[1 + count : -1], refs[-1]
    if whole is None:
        total = refs[0][...]
        for ref in refs[1 : 1 + count]:
            total = total + ref[...].astype(F32)
    else:
        mine, size = digit_of(whole), whole[1]
        rows = refs[0].shape[0]
        for k, ref in enumerate(refs[: 1 + count]):
            at = source(mine, k, size) * rows
            acc[pl.ds(pl.multiple_of(at, rows), rows), :] = ref[...].astype(F32)
        total = acc[:rows, :]
        for k in range(1, size):
            total = total + acc[k * rows : (k + 1) * rows, :]
        acc = acc.at[:rows, :]
    acc[...] = total
    if digit is None:
        outs[0][...] = total.astype(outs[0].dtype)
    else:
        split(acc, digit, outs[0], outs[1:])


def join_kernel(digit, *refs):
    parts, out = refs[:-1], refs[-1]
    size, part = len(parts), parts[0].shape[0]
    mine = digit_of(digit)
    for k, ref in enumerate(parts):
        at = source(mine, k, size)
        out[pl.ds(pl.multiple_of(at * part, part), part), :] = ref[...].astype(out.dtype)


def shards(query, key, value, gate_u, out_grad, lengths, norm_gain, out_weight):
    rows, feats = query.shape
    model = out_grad.shape[1]
    lanes = lax.axis_size("blk")
    groups = lax.axis_size("grp")
    chips = lanes // CORES
    pos = lax.axis_index("blk")
    total = rows * lanes
    width = model // lanes

    def spread(x, later):
        cross = [over_chips(x, lanes, k, later) for k in range(1, chips)]
        pieces = [x, swap_core(x, lanes, later)]
        for c in cross:
            pieces += [c, swap_core(c, lanes)]
        return pieces

    keys = spread(key, False)
    values = spread(value, False)
    columns = [
        lax.dynamic_slice_in_dim(out_grad, target(pos, k, lanes) * width, width, 1)
        for k in range(lanes)
    ]
    blk_pairs = [[(i, partner(i, k, lanes)) for i in range(lanes)] for k in range(lanes)]
    columns = columns[:1] + [lax.ppermute(columns[k], "blk", blk_pairs[k]) for k in range(1, lanes)]
    queries = spread(query, True)

    (mixed_grad,) = call(
        mixed_grad_kernel, [((rows, feats), F32)], out_grad, out_weight, flops=2 * rows * feats * model
    )
    attention_flops = 4 * rows * total * feats
    mixed, mixed_t, att_grad, grad_gate, kall, vall = call(
        functools.partial(forward_kernel, lanes),
        [
            ((rows, feats), BF16),
            ((feats, rows), BF16),
            ((rows, feats), BF16),
            ((rows, feats), BF16),
            ((total, feats), BF16),
            ((total, feats), BF16),
        ],
        lengths,
        query,
        *keys,
        *values,
        gate_u,
        norm_gain.reshape(1, feats),
        mixed_grad,
        scalars=1,
        scratch=[pltpu.VMEM((rows, feats), F32)],
        flops=attention_flops,
    )
    mixes = [mixed_t] + [lax.ppermute(mixed_t, "blk", blk_pairs[k]) for k in range(1, lanes)]
    grads = spread(att_grad, True)

    stages = digits(groups)
    size = feats
    plan = []
    for digit in stages:
        parts = digit[1] if size % (16 * digit[1]) == 0 else 1
        size //= parts
        plan.append((digit, parts, size))

    layer_out, grad_query = call(
        query_kernel,
        [((rows, model), BF16), ((rows, feats), BF16)],
        lengths,
        query,
        kall,
        vall,
        att_grad,
        mixed,
        out_weight,
        scalars=1,
        flops=attention_flops,
    )
    grad_key, grad_value = call(
        functools.partial(key_kernel, lanes),
        [((rows, feats), BF16), ((rows, feats), BF16)],
        lengths,
        key,
        value,
        *queries,
        *grads,
        scalars=1,
        scratch=[pltpu.VMEM((total, feats), BF16), pltpu.VMEM((total, feats), BF16)],
        flops=2 * attention_flops,
    )

    def pieces_of(parts, part):
        return [((part, width), F32)] + [((part, width), BF16)] * (parts - 1)

    held = call(
        functools.partial(product_kernel, lanes, plan[0][0]),
        pieces_of(plan[0][1], plan[0][2]),
        *mixes,
        *columns,
        scratch=[pltpu.VMEM((feats, width), F32)],
        flops=2 * total * feats * width,
    )
    for n, (digit, parts, part) in enumerate(plan):
        if parts > 1:
            received = [over_digit(held[k], groups, digit, k) for k in range(1, parts)]
        else:
            held = [held[0].astype(BF16)]
            received = [over_digit(held[0], groups, digit, k) for k in range(1, digit[1])]
        last = n + 1 == len(plan)
        nxt = None if last else plan[n + 1]
        split_next = not last and nxt[1] > 1
        held = call(
            functools.partial(
                sum_split_kernel,
                len(received),
                None if parts > 1 else digit,
                nxt[0] if split_next else None,
            ),
            [((part, width), BF16 if last else F32)] if not split_next else pieces_of(nxt[1], nxt[2]),
            held[0],
            *received,
            scratch=[pltpu.VMEM((part if parts > 1 else part * digit[1], width), F32)],
        )
    piece = held[0]
    gathers = [entry for entry in plan[::-1] if entry[1] > 1]
    for n, (digit, parts, part) in enumerate(gathers):
        received = [over_digit(piece, groups, digit, k) for k in range(1, parts)]
        (piece,) = call(
            functools.partial(join_kernel, digit),
            [((part * parts, width), F32 if n + 1 == len(gathers) else BF16)],
            piece,
            *received,
        )
    return (layer_out, grad_query, grad_key, grad_value, grad_gate, piece.astype(F32))


def solution(mesh):
    rows = P(("grp", "blk"), None)
    return jax.shard_map(
        shards,
        mesh=mesh,
        in_specs=(rows, rows, rows, rows, rows, P("grp"), P(), P()),
        out_specs=(rows, rows, rows, rows, rows, P(None, "blk")),
        check_vma=False,
    )
```

time: 159 us -> 82.3 us (0.52)
  waiting for transfers between devices: 76.3 us -> 16.9 us
  blocking collectives: 33.2 us -> 0 us
  starting transfers between devices: 0.08 us -> 33.1 us
  Pallas kernels: 0 us -> 23.1 us
  matrix products: 17.5 us -> 0 us
  between operations: 14.9 us -> 1.59 us
  local copies, waits for them, and re-layouts: 13.7 us -> 6.96 us
  other arithmetic: 2.64 us -> 0 us
    psum x1 -> x0, waiting for transfers between devices: 73.1 us -> none  [shards(): grad_weight = lax.psum(column_part, 'grp')]
    all_gather x4 -> x0, blocking collectives: 33.2 us -> none  [the longest x1 9.49 us: shards(): grad_piece = lax.all_gather(attended_grad, 'blk', axis=0, tiled=True)]
    ppermute x0 -> x26, starting transfers between devices: none -> 33.1 us  [the longest x8 11.9 us: over_digit(): return lax.ppermute(x, 'grp', pairs)]
    pallas_call x0 -> x9, Pallas kernels: none -> 23.1 us  [call(): pl.pallas_call(kernel, out_shape=[jax.ShapeDtypeStruct(s, d) for s, d in...]
    dot_general x9 -> x0, matrix products: 17.5 us -> none  [the longest x1 3.29 us: query_step(): jnp.einsum('hrn,nhd->rhd', score_grad, key_block, preferred_element_type=...]
    ppermute x0 -> x26, waiting for transfers between devices: none -> 16.9 us  [the longest x3 7.84 us: shards(): lax.ppermute(columns[k], 'blk', blk_pairs[k])]
    all_gather x4 -> x0, local copies, waits for them, and re-layouts: 4.04 us -> none  [the longest x1 1.02 us: shards(): lax.all_gather(key, 'blk', axis=0, tiled=True)]
    reduce_scatter x1 -> x0, waiting for transfers between devices: 3.17 us -> none  [shards(): lax.psum_scatter(weight_term, 'blk', scatter_dimension=1, tiled=True)]
  transfers between devices with their start and end apart: 2 -> 26, of which waited for: 2 -> 7; matrix products, arithmetic and copies ran while one was open for 11% -> 2% of each run, Pallas kernels for 0% -> 23%
where the time goes in v1:
time: 82.3 us; the launch traced here: 81.6 us
  starting transfers between devices  33.1 us (40%)
  Pallas kernels  23.1 us (28%)
  waiting for transfers between devices  16.9 us (21%)
  local copies, waits for them, and re-layouts  6.96 us (8%)
  between operations  1.59 us (2%)
    pallas_call x9, Pallas kernels, call(): pl.pallas_call(kernel, out_shape=[jax.ShapeDtypeStruct(s, d) for s, d in...  23.1 us
    ppermute x8, starting transfers between devices, over_digit(): return lax.ppermute(x, 'grp', pairs)  11.9 us
    ppermute x4, starting transfers between devices, over_chips(): return lax.ppermute(x, 'blk', pairs)  8.75 us
    ppermute x3, waiting for transfers between devices, shards(): lax.ppermute(columns[k], 'blk', blk_pairs[k])  7.84 us
    ppermute x8, starting transfers between devices, swap_core(): return lax.ppermute(x, 'blk', pairs)  7.75 us
    ppermute x8, waiting for transfers between devices, over_digit(): return lax.ppermute(x, 'grp', pairs)  7.29 us
    unnamed x56, local copies, waits for them, and re-layouts  5.34 us
    ppermute x3, starting transfers between devices, shards(): lax.ppermute(mixed_t, 'blk', blk_pairs[k])  2.5 us
  transfers between devices with their start and end apart: 26, of which 7 were waited for; matrix products, arithmetic and copies ran while one was open for 2% of the time, Pallas kernels for 23%

profile of v1, /device:TPU:0, one launch (start us, length us, event | category | flops | bytes accessed | tf_op | source)
XLA Modules:
  0.0 81.6 jit_solution(1601626831885209271)
XLA Ops:
  0.6 4.9 %collective-permute-start.1 = (bf16[128,512]{1,0:T(8,128)(2,1)}, bf16[128,512]{1,0:T(8,128)(2,1)S(1)}, u32[]{:S(2)}, u32[]{:S(2)}) collective-permute-start(bf16[128,512]{1,0:T(8,128)(2,1)} %refs_1_.3), channel_id=1, source_target_pairs={{0,2},{1,3},{4,6},{5,7},{8,10},{9,11},{12,14},{13,15},{16,18},{17,... | collective-permute-start | bytes 393224 | tf_op jit(solution)/shard_map/ppermute | solution.py:67
  5.5 1.3 %collective-permute-start.4 = (bf16[128,512]{1,0:T(8,128)(2,1)}, bf16[128,512]{1,0:T(8,128)(2,1)S(1)}, u32[]{:S(2)}, u32[]{:S(2)}) collective-permute-start(bf16[128,512]{1,0:T(8,128)(2,1)} %refs_2_.3), channel_id=1, source_target_pairs={{0,2},{1,3},{4,6},{5,7},{8,10},{9,11},{12,14},{13,15},{16,18},{17,... | collective-permute-start | bytes 393224 | tf_op jit(solution)/shard_map/ppermute | solution.py:67
  6.8 1.5 %collective-permute-start = (bf16[128,512]{1,0:T(8,128)(2,1)}, bf16[128,512]{1,0:T(8,128)(2,1)S(1)}, u32[]{:S(2)}, u32[]{:S(2)}) collective-permute-start(bf16[128,512]{1,0:T(8,128)(2,1)} %refs_1_.3), channel_id=1, source_target_pairs={{0,1},{2,3},{4,5},{6,7},{8,9},{10,11},{12,13},{14,15},{16,17},{18,... | collective-permute-start | bytes 393224 | tf_op jit(solution)/shard_map/ppermute | solution.py:61
  8.3 1.3 %collective-permute-start.3 = (bf16[128,512]{1,0:T(8,128)(2,1)}, bf16[128,512]{1,0:T(8,128)(2,1)S(1)}, u32[]{:S(2)}, u32[]{:S(2)}) collective-permute-start(bf16[128,512]{1,0:T(8,128)(2,1)} %refs_2_.3), channel_id=1, source_target_pairs={{0,1},{2,3},{4,5},{6,7},{8,9},{10,11},{12,13},{14,15},{16,17},{18,... | collective-permute-start | bytes 393224 | tf_op jit(solution)/shard_map/ppermute | solution.py:61
  9.7 1.6 %collective-permute-done.4.refs_8_ = bf16[128,512]{1,0:T(8,128)(2,1)S(1)} collective-permute-done((bf16[128,512]{1,0:T(8,128)(2,1)}, bf16[128,512]{1,0:T(8,128)(2,1)S(1)}, u32[]{:S(2)}, u32[]{:S(2)}) %collective-permute-start.4) | collective-permute-done | bytes 131104 | tf_op jit(solution)/shard_map/ppermute | solution.py:67
  11.4 1.6 %constant_dynamic-slice_fusion = (bf16[128,256]{1,0:T(8,128)(2,1)S(1)}, bf16[128,256]{1,0:T(8,128)(2,1)S(1)}, bf16[128,256]{1,0:T(8,128)(2,1)}, bf16[128,256]{1,0:T(8,128)(2,1)S(1)}) fusion(bf16[128,1024]{1,0:T(8,128)(2,1)} %og_ref.1, s32[]{:T(128)S(6)} %select_n.15, s32[]{:T(128)S(6)} %select_n.13, s32[]{:T(128)S(6)} %select_n.12, s32[]{:T(128)S(6)} %select_n.14), kind=kLoop, calls=%fused_computation | loop fusion | bytes 524304 | tf_op jit(solution)/shard_map/dynamic_slice | solution.py:322
  14.1 2.5 %shard_map.127.refs_12_ = f32[128,512]{1,0:T(8,128)} custom-call(bf16[128,1024]{1,0:T(8,128)(2,1)} %og_ref.1, bf16[512,1024]{1,0:T(8,128)(2,1)} %w_ref.3), custom_call_target="tpu_custom_call" | custom-call | flops 134217728 | tf_op jit(solution)/shard_map/pallas_call | solution.py:29
  17.4 3.9 %shard_map.128 = (bf16[128,512]{1,0:T(8,128)(2,1)}, bf16[512,128]{1,0:T(8,128)(2,1)}, bf16[128,512]{1,0:T(8,128)(2,1)}, bf16[128,512]{1,0:T(8,128)(2,1)}, bf16[5...) custom-call(s32[1]{0:T(128)S(6)} %copy.14.refs_0_.len_ref, bf16[128,512]{1,0:T(8,128)(2,1)} %refs_3_.1, ...), custom_call_target="tpu_custom_call" | custom-call | flops 134217728 | tf_op jit(solution)/shard_map/pallas_call | solution.py:29
  21.3 2.4 %collective-permute-start.13 = (bf16[512,128]{1,0:T(8,128)(2,1)}, bf16[512,128]{1,0:T(8,128)(2,1)S(1)}, u32[]{:S(2)}, u32[]{:S(2)}) collective-permute-start(bf16[512,128]{1,0:T(8,128)(2,1)} %get-tuple-element.31.refs_0_), channel_id=1, source_target_pairs={{0,2},{1,3},{2,0},{3,1},{4,6},{5,7},{6,4},{7,5},{8,10},{9,11},{10,... | collective-permute-start | bytes 393224 | tf_op jit(solution)/shard_map/ppermute | solution.py:354
  23.8 1.7 %collective-permute-start.16 = (bf16[128,256]{1,0:T(8,128)(2,1)S(1)}, bf16[128,256]{1,0:T(8,128)(2,1)S(1)}, u32[]{:S(2)}, u32[]{:S(2)}) collective-permute-start(bf16[128,256]{1,0:T(8,128)(2,1)S(1)} %get-tuple-element.41), channel_id=1, source_target_pairs={{0,2},{1,3},{2,0},{3,1},{4,6},{5,7},{6,4},{7,5},{8,10},{9,11},{10,... | collective-permute-start | bytes 196616 | tf_op jit(solution)/shard_map/ppermute | solution.py:326
  25.6 6.9 %collective-permute-done.16.refs_6_ = bf16[128,256]{1,0:T(8,128)(2,1)S(1)} collective-permute-done((bf16[128,256]{1,0:T(8,128)(2,1)S(1)}, bf16[128,256]{1,0:T(8,128)(2,1)S(1)}, u32[]{:S(2)}, u32[]{:S(2)}) %collective-permute-start.16) | collective-permute-done | bytes 65568 | tf_op jit(solution)/shard_map/ppermute | solution.py:326
  34.2 2.4 %shard_map.131 = (f32[256,256]{1,0:T(8,128)}, bf16[256,256]{1,0:T(8,128)(2,1)}) custom-call(bf16[512,128]{1,0:T(8,128)(2,1)} %get-tuple-element.31.refs_0_, bf16[512,128]{1,0:T(8,128)(2,1)} %copy-done.15, bf16[512,128]{1,0:T(8,128)(2,1)} %copy-done.16, bf16[512,128]{1,0:T(8,128)(2,1)} %copy-done.17, bf16[128,256]{1,0:T(8,128)(2,1)} %get-tuple-element.40.refs_4_, ...), custom_call_target="tpu_custom_call" | custom-call | flops 134217728 | tf_op jit(solution)/shard_map/pallas_call | solution.py:29
  36.6 1.5 %collective-permute-start.18 = (bf16[256,256]{1,0:T(8,128)(2,1)}, bf16[256,256]{1,0:T(8,128)(2,1)S(1)}, u32[]{:S(2)}, u32[]{:S(2)}) collective-permute-start(bf16[256,256]{1,0:T(8,128)(2,1)} %get-tuple-element.33), channel_id=1, source_target_pairs={{0,4},{4,0},{8,12},{12,8},{16,20},{20,16},{24,28},{28,24},{1,5},{5... | collective-permute-start | bytes 393224 | tf_op jit(solution)/shard_map/ppermute | solution.py:87
  38.1 1.3 %collective-permute-start.7 = (bf16[128,512]{1,0:T(8,128)(2,1)S(1)}, bf16[128,512]{1,0:T(8,128)(2,1)S(1)}, u32[]{:S(2)}, u32[]{:S(2)}) collective-permute-start(bf16[128,512]{1,0:T(8,128)(2,1)S(1)} %copy-done), channel_id=1, source_target_pairs={{2,0},{3,1},{6,4},{7,5},{10,8},{11,9},{14,12},{15,13},{18,16},{19,... | collective-permute-start | bytes 393224 | tf_op jit(solution)/shard_map/ppermute | solution.py:67
  39.4 1.3 %collective-permute-start.10 = (bf16[128,512]{1,0:T(8,128)(2,1)S(1)}, bf16[128,512]{1,0:T(8,128)(2,1)S(1)}, u32[]{:S(2)}, u32[]{:S(2)}) collective-permute-start(bf16[128,512]{1,0:T(8,128)(2,1)S(1)} %copy-done.1), channel_id=1, source_target_pairs={{2,0},{3,1},{6,4},{7,5},{10,8},{11,9},{14,12},{15,13},{18,16},{19,... | collective-permute-start | bytes 393224 | tf_op jit(solution)/shard_map/ppermute | solution.py:67
  40.7 1.6 %collective-permute-done.18.refs_1_ = bf16[256,256]{1,0:T(8,128)(2,1)S(1)} collective-permute-done((bf16[256,256]{1,0:T(8,128)(2,1)}, bf16[256,256]{1,0:T(8,128)(2,1)S(1)}, u32[]{:S(2)}, u32[]{:S(2)}) %collective-permute-start.18) | collective-permute-done | bytes 131104 | tf_op jit(solution)/shard_map/ppermute | solution.py:87
  43.0 1.7 %shard_map.132 = (f32[64,256]{1,0:T(8,128)}, bf16[64,256]{1,0:T(8,128)(2,1)}, bf16[64,256]{1,0:T(8,128)(2,1)}, bf16[64,256]{1,0:T(8,128)(2,1)}) custom-call(f32[256,256]{1,0:T(8,128)} %get-tuple-element.32.refs_0_, bf16[256,256]{1,0:T(8,128)(2,1)} %copy-done.14), custom_call_target="tpu_custom_call" | custom-call | tf_op jit(solution)/shard_map/pallas_call | solution.py:29
  44.6 1.6 %collective-permute-start.19 = (bf16[64,256]{1,0:T(8,128)(2,1)}, bf16[64,256]{1,0:T(8,128)(2,1)S(1)}, u32[]{:S(2)}, u32[]{:S(2)}) collective-permute-start(bf16[64,256]{1,0:T(8,128)(2,1)} %get-tuple-element.35), channel_id=1, source_target_pairs={{0,8},{4,12},{8,0},{12,4},{16,24},{20,28},{24,16},{28,20},{1,9},{5... | collective-permute-start | bytes 98312 | tf_op jit(solution)/shard_map/ppermute | solution.py:87
  46.2 2.6 %collective-permute-start.20 = (bf16[64,256]{1,0:T(8,128)(2,1)}, bf16[64,256]{1,0:T(8,128)(2,1)S(1)}, u32[]{:S(2)}, u32[]{:S(2)}) collective-permute-start(bf16[64,256]{1,0:T(8,128)(2,1)} %get-tuple-element.36), channel_id=1, source_target_pairs={{0,16},{4,20},{8,24},{12,28},{16,0},{20,4},{24,8},{28,12},{1,17},{... | collective-permute-start | bytes 98312 | tf_op jit(solution)/shard_map/ppermute | solution.py:87
  49.0 2.5 %collective-permute-done.20.refs_2_ = bf16[64,256]{1,0:T(8,128)(2,1)S(1)} collective-permute-done((bf16[64,256]{1,0:T(8,128)(2,1)}, bf16[64,256]{1,0:T(8,128)(2,1)S(1)}, u32[]{:S(2)}, u32[]{:S(2)}) %collective-permute-start.20) | collective-permute-done | bytes 32800 | tf_op jit(solution)/shard_map/ppermute | solution.py:87
  51.5 3.2 %collective-permute-done.21.refs_3_ = bf16[64,256]{1,0:T(8,128)(2,1)S(1)} collective-permute-done((bf16[64,256]{1,0:T(8,128)(2,1)}, bf16[64,256]{1,0:T(8,128)(2,1)S(1)}, u32[]{:S(2)}, u32[]{:S(2)}) %collective-permute-start.21) | collective-permute-done | bytes 32800 | tf_op jit(solution)/shard_map/ppermute | solution.py:87
  55.3 1.5 %shard_map.133.refs_0_ = bf16[64,256]{1,0:T(8,128)(2,1)} custom-call(f32[64,256]{1,0:T(8,128)} %get-tuple-element.34.refs_0_, bf16[64,256]{1,0:T(8,128)(2,1)} %copy-done.22, bf16[64,256]{1,0:T(8,128)(2,1)} %copy-done.23, bf16[64,256]{1,0:T(8,128)(2,1)} %copy-done.24), custom_call_target="tpu_custom_call" | custom-call | tf_op jit(solution)/shard_map/pallas_call | solution.py:29
  57.7 3.5 %collective-permute-start.24 = (bf16[64,256]{1,0:T(8,128)(2,1)}, bf16[64,256]{1,0:T(8,128)(2,1)S(1)}, u32[]{:S(2)}, u32[]{:S(2)}) collective-permute-start(bf16[64,256]{1,0:T(8,128)(2,1)} %shard_map.133.refs_0_), channel_id=1, source_target_pairs={{0,24},{4,28},{8,16},{12,20},{16,8},{20,12},{24,0},{28,4},{1,25},{... | collective-permute-start | bytes 98312 | tf_op jit(solution)/shard_map/ppermute | solution.py:87
  61.2 1.3 %collective-permute-start.6 = (bf16[128,512]{1,0:T(8,128)(2,1)S(1)}, bf16[128,512]{1,0:T(8,128)(2,1)S(1)}, u32[]{:S(2)}, u32[]{:S(2)}) collective-permute-start(bf16[128,512]{1,0:T(8,128)(2,1)S(1)} %copy-done), channel_id=1, source_target_pairs={{1,0},{3,2},{5,4},{7,6},{9,8},{11,10},{13,12},{15,14},{17,16},{19,... | collective-permute-start | bytes 393224 | tf_op jit(solution)/shard_map/ppermute | solution.py:61
  62.5 1.2 %collective-permute-start.8 = (bf16[128,512]{1,0:T(8,128)(2,1)S(1)}, bf16[128,512]{1,0:T(8,128)(2,1)S(1)}, u32[]{:S(2)}, u32[]{:S(2)}) collective-permute-start(bf16[128,512]{1,0:T(8,128)(2,1)S(1)} %collective-permute-done.7.refs_5_), channel_id=1, source_target_pairs={{0,1},{1,0},{2,3},{3,2},{4,5},{5,4},{6,7},{7,6},{8,9},{9,8},{10,11... | collective-permute-start | bytes 393224 | tf_op jit(solution)/shard_map/ppermute | solution.py:61
  63.7 1.3 %collective-permute-start.9 = (bf16[128,512]{1,0:T(8,128)(2,1)S(1)}, bf16[128,512]{1,0:T(8,128)(2,1)S(1)}, u32[]{:S(2)}, u32[]{:S(2)}) collective-permute-start(bf16[128,512]{1,0:T(8,128)(2,1)S(1)} %copy-done.1), channel_id=1, source_target_pairs={{1,0},{3,2},{5,4},{7,6},{9,8},{11,10},{13,12},{15,14},{17,16},{19,... | collective-permute-start | bytes 393224 | tf_op jit(solution)/shard_map/ppermute | solution.py:61
  65.0 1.2 %collective-permute-start.11 = (bf16[128,512]{1,0:T(8,128)(2,1)S(1)}, bf16[128,512]{1,0:T(8,128)(2,1)S(1)}, u32[]{:S(2)}, u32[]{:S(2)}) collective-permute-start(bf16[128,512]{1,0:T(8,128)(2,1)S(1)} %collective-permute-done.10.refs_9_), channel_id=1, source_target_pairs={{0,1},{1,0},{2,3},{3,2},{4,5},{5,4},{6,7},{7,6},{8,9},{9,8},{10,11... | collective-permute-start | bytes 393224 | tf_op jit(solution)/shard_map/ppermute | solution.py:61
  66.8 1.5 %shard_map.134.refs_0_ = bf16[256,256]{1,0:T(8,128)(2,1)} custom-call(bf16[64,256]{1,0:T(8,128)(2,1)} %shard_map.133.refs_0_, bf16[64,256]{1,0:T(8,128)(2,1)} %copy-done.25, bf16[64,256]{1,0:T(8,128)(2,1)} %copy-done.26, bf16[64,256]{1,0:T(8,128)(2,1)} %copy-done.27), custom_call_target="tpu_custom_call" | custom-call | tf_op jit(solution)/shard_map/pallas_call | solution.py:29
  68.3 1.5 %collective-permute-start.25 = (bf16[256,256]{1,0:T(8,128)(2,1)}, bf16[256,256]{1,0:T(8,128)(2,1)S(1)}, u32[]{:S(2)}, u32[]{:S(2)}) collective-permute-start(bf16[256,256]{1,0:T(8,128)(2,1)} %shard_map.134.refs_0_), channel_id=1, source_target_pairs={{0,4},{4,0},{8,12},{12,8},{16,20},{20,16},{24,28},{28,24},{1,5},{5... | collective-permute-start | bytes 393224 | tf_op jit(solution)/shard_map/ppermute | solution.py:87
  69.9 4.0 %shard_map.129 = (bf16[128,1024]{1,0:T(8,128)(2,1)}, bf16[128,512]{1,0:T(8,128)(2,1)}) custom-call(s32[1]{0:T(128)S(6)} %copy.14.refs_0_.len_ref, bf16[128,512]{1,0:T(8,128)(2,1)} %refs_3_.1, bf16[512,512]{1,0:T(8,128)(2,1)} %get-tuple-element.22.kall, bf16[512,512]{1,0:T(8,128)(2,1)} %get-tuple-element.23.vall, ...), custom_call_target="tpu_custom_call" | custom-call | flops 134217728 | tf_op jit(solution)/shard_map/pallas_call | solution.py:29
  75.2 3.9 %shard_map.130 = (bf16[128,512]{1,0:T(8,128)(2,1)}, bf16[128,512]{1,0:T(8,128)(2,1)}) custom-call(s32[1]{0:T(128)S(6)} %copy.14.refs_0_.len_ref, bf16[128,512]{1,0:T(8,128)(2,1)} %refs_1_.3, bf16[128,512]{1,0:T(8,128)(2,1)} %refs_2_.3, bf16[128,512]{1,0:T(8,128)(2,1)} %refs_3_.1, bf16[128,512]{1,0:T(8,128)(2,1)} %copy-done.8, bf16[128,512]{1,0:T(8,128)(2,1)} %copy-done.2, ...), custom_call_target="tpu_custom_call" | custom-call | flops 268435456 | tf_op jit(solution)/shard_map/pallas_call | solution.py:29
  79.8 1.8 %shard_map.135 = f32[512,256]{1,0:T(8,128)} custom-call(bf16[256,256]{1,0:T(8,128)(2,1)} %shard_map.134.refs_0_, bf16[256,256]{1,0:T(8,128)(2,1)} %copy-done.18), custom_call_target="tpu_custom_call" | custom-call | tf_op jit(solution)/shard_map/pallas_call | solution.py:29
  (86 shorter events, 8.1 us)
Async XLA Ops:
  0.6 9.1 %collective-permute-start.1 = (bf16[128,512]{1,0:T(8,128)(2,1)}, bf16[128,512]{1,0:T(8,128)(2,1)S(1)}, u32[]{:S(2)}, u32[]{:S(2)}) collective-permute-start(bf16[128,512]{1,0:T(8,128)(2,1)} %refs_1_.3), channel_id=1, source_target_pairs={{0,2},{1,3},{4,6},{5,7},{8,10},{9,11},{12,14},{13,15},{16,18},{17,... | collective-permute-start | bytes 393224 | tf_op jit(solution)/shard_map/ppermute | solution.py:67
  5.5 5.9 %collective-permute-start.4 = (bf16[128,512]{1,0:T(8,128)(2,1)}, bf16[128,512]{1,0:T(8,128)(2,1)S(1)}, u32[]{:S(2)}, u32[]{:S(2)}) collective-permute-start(bf16[128,512]{1,0:T(8,128)(2,1)} %refs_2_.3), channel_id=1, source_target_pairs={{0,2},{1,3},{4,6},{5,7},{8,10},{9,11},{12,14},{13,15},{16,18},{17,... | collective-permute-start | bytes 393224 | tf_op jit(solution)/shard_map/ppermute | solution.py:67
  6.8 9.8 %collective-permute-start = (bf16[128,512]{1,0:T(8,128)(2,1)}, bf16[128,512]{1,0:T(8,128)(2,1)S(1)}, u32[]{:S(2)}, u32[]{:S(2)}) collective-permute-start(bf16[128,512]{1,0:T(8,128)(2,1)} %refs_1_.3), channel_id=1, source_target_pairs={{0,1},{2,3},{4,5},{6,7},{8,9},{10,11},{12,13},{14,15},{16,17},{18,... | collective-permute-start | bytes 393224 | tf_op jit(solution)/shard_map/ppermute | solution.py:61
  8.3 8.3 %collective-permute-start.3 = (bf16[128,512]{1,0:T(8,128)(2,1)}, bf16[128,512]{1,0:T(8,128)(2,1)S(1)}, u32[]{:S(2)}, u32[]{:S(2)}) collective-permute-start(bf16[128,512]{1,0:T(8,128)(2,1)} %refs_2_.3), channel_id=1, source_target_pairs={{0,1},{2,3},{4,5},{6,7},{8,9},{10,11},{12,13},{14,15},{16,17},{18,... | collective-permute-start | bytes 393224 | tf_op jit(solution)/shard_map/ppermute | solution.py:61
  9.7 6.9 %collective-permute-start.2 = (bf16[128,512]{1,0:T(8,128)(2,1)S(1)}, bf16[128,512]{1,0:T(8,128)(2,1)S(1)}, u32[]{:S(2)}, u32[]{:S(2)}) collective-permute-start(bf16[128,512]{1,0:T(8,128)(2,1)S(1)} %collective-permute-done.1.refs_4_), channel_id=1, source_target_pairs={{0,1},{1,0},{2,3},{3,2},{4,5},{5,4},{6,7},{7,6},{8,9},{9,8},{10,11... | collective-permute-start | bytes 393224 | tf_op jit(solution)/shard_map/ppermute | solution.py:61
  11.4 5.3 %collective-permute-start.5 = (bf16[128,512]{1,0:T(8,128)(2,1)S(1)}, bf16[128,512]{1,0:T(8,128)(2,1)S(1)}, u32[]{:S(2)}, u32[]{:S(2)}) collective-permute-start(bf16[128,512]{1,0:T(8,128)(2,1)S(1)} %collective-permute-done.4.refs_8_), channel_id=1, source_target_pairs={{0,1},{1,0},{2,3},{3,2},{4,5},{5,4},{6,7},{7,6},{8,9},{9,8},{10,11... | collective-permute-start | bytes 393224 | tf_op jit(solution)/shard_map/ppermute | solution.py:61
  13.0 12.5 %collective-permute-start.15 = (bf16[128,256]{1,0:T(8,128)(2,1)S(1)}, bf16[128,256]{1,0:T(8,128)(2,1)S(1)}, u32[]{:S(2)}, u32[]{:S(2)}) collective-permute-start(bf16[128,256]{1,0:T(8,128)(2,1)S(1)} %get-tuple-element.39), channel_id=1, source_target_pairs={{0,1},{1,0},{2,3},{3,2},{4,5},{5,4},{6,7},{7,6},{8,9},{9,8},{10,11... | collective-permute-start | bytes 196616 | tf_op jit(solution)/shard_map/ppermute | solution.py:326
  21.3 12.1 %collective-permute-start.12 = (bf16[512,128]{1,0:T(8,128)(2,1)}, bf16[512,128]{1,0:T(8,128)(2,1)S(1)}, u32[]{:S(2)}, u32[]{:S(2)}) collective-permute-start(bf16[512,128]{1,0:T(8,128)(2,1)} %get-tuple-element.31.refs_0_), channel_id=1, source_target_pairs={{0,1},{1,0},{2,3},{3,2},{4,5},{5,4},{6,7},{7,6},{8,9},{9,8},{10,11... | collective-permute-start | bytes 393224 | tf_op jit(solution)/shard_map/ppermute | solution.py:354
  21.3 12.1 %collective-permute-start.13 = (bf16[512,128]{1,0:T(8,128)(2,1)}, bf16[512,128]{1,0:T(8,128)(2,1)S(1)}, u32[]{:S(2)}, u32[]{:S(2)}) collective-permute-start(bf16[512,128]{1,0:T(8,128)(2,1)} %get-tuple-element.31.refs_0_), channel_id=1, source_target_pairs={{0,2},{1,3},{2,0},{3,1},{4,6},{5,7},{6,4},{7,5},{8,10},{9,11},{10,... | collective-permute-start | bytes 393224 | tf_op jit(solution)/shard_map/ppermute | solution.py:354
  23.7 9.7 %collective-permute-start.14 = (bf16[512,128]{1,0:T(8,128)(2,1)}, bf16[512,128]{1,0:T(8,128)(2,1)S(1)}, u32[]{:S(2)}, u32[]{:S(2)}) collective-permute-start(bf16[512,128]{1,0:T(8,128)(2,1)} %get-tuple-element.31.refs_0_), channel_id=1, source_target_pairs={{0,3},{1,2},{2,1},{3,0},{4,7},{5,6},{6,5},{7,4},{8,11},{9,10},{10,... | collective-permute-start | bytes 393224 | tf_op jit(solution)/shard_map/ppermute | solution.py:354
  23.8 8.7 %collective-permute-start.16 = (bf16[128,256]{1,0:T(8,128)(2,1)S(1)}, bf16[128,256]{1,0:T(8,128)(2,1)S(1)}, u32[]{:S(2)}, u32[]{:S(2)}) collective-permute-start(bf16[128,256]{1,0:T(8,128)(2,1)S(1)} %get-tuple-element.41), channel_id=1, source_target_pairs={{0,2},{1,3},{2,0},{3,1},{4,6},{5,7},{6,4},{7,5},{8,10},{9,11},{10,... | collective-permute-start | bytes 196616 | tf_op jit(solution)/shard_map/ppermute | solution.py:326
  25.5 7.9 %copy-start.19 = (bf16[128,256]{1,0:T(8,128)(2,1)}, bf16[128,256]{1,0:T(8,128)(2,1)S(1)}, u32[]{:S(2)}) copy-start(bf16[128,256]{1,0:T(8,128)(2,1)S(1)} %collective-permute-done.15.refs_5_) | copy-start | bytes 196612
  25.5 7.9 %collective-permute-start.17 = (bf16[128,256]{1,0:T(8,128)(2,1)S(1)}, bf16[128,256]{1,0:T(8,128)(2,1)S(1)}, u32[]{:S(2)}, u32[]{:S(2)}) collective-permute-start(bf16[128,256]{1,0:T(8,128)(2,1)S(1)} %get-tuple-element.38), channel_id=1, source_target_pairs={{0,3},{1,2},{2,1},{3,0},{4,7},{5,6},{6,5},{7,4},{8,11},{9,10},{10,... | collective-permute-start | bytes 196616 | tf_op jit(solution)/shard_map/ppermute | solution.py:326
  34.2 3.9 %copy-start = (bf16[128,512]{1,0:T(8,128)(2,1)S(1)}, bf16[128,512]{1,0:T(8,128)(2,1)}, u32[]{:S(2)}) copy-start(bf16[128,512]{1,0:T(8,128)(2,1)} %refs_3_.1) | copy-start | bytes 393220
  34.2 5.2 %copy-start.1 = (bf16[128,512]{1,0:T(8,128)(2,1)S(1)}, bf16[128,512]{1,0:T(8,128)(2,1)}, u32[]{:S(2)}) copy-start(bf16[128,512]{1,0:T(8,128)(2,1)} %get-tuple-element.24.ag_ref.refs_7_) | copy-start | bytes 393220
  36.6 5.7 %collective-permute-start.18 = (bf16[256,256]{1,0:T(8,128)(2,1)}, bf16[256,256]{1,0:T(8,128)(2,1)S(1)}, u32[]{:S(2)}, u32[]{:S(2)}) collective-permute-start(bf16[256,256]{1,0:T(8,128)(2,1)} %get-tuple-element.33), channel_id=1, source_target_pairs={{0,4},{4,0},{8,12},{12,8},{16,20},{20,16},{24,28},{28,24},{1,5},{5... | collective-permute-start | bytes 393224 | tf_op jit(solution)/shard_map/ppermute | solution.py:87
  38.1 23.1 %collective-permute-start.7 = (bf16[128,512]{1,0:T(8,128)(2,1)S(1)}, bf16[128,512]{1,0:T(8,128)(2,1)S(1)}, u32[]{:S(2)}, u32[]{:S(2)}) collective-permute-start(bf16[128,512]{1,0:T(8,128)(2,1)S(1)} %copy-done), channel_id=1, source_target_pairs={{2,0},{3,1},{6,4},{7,5},{10,8},{11,9},{14,12},{15,13},{18,16},{19,... | collective-permute-start | bytes 393224 | tf_op jit(solution)/shard_map/ppermute | solution.py:67
  39.4 23.1 %collective-permute-start.10 = (bf16[128,512]{1,0:T(8,128)(2,1)S(1)}, bf16[128,512]{1,0:T(8,128)(2,1)S(1)}, u32[]{:S(2)}, u32[]{:S(2)}) collective-permute-start(bf16[128,512]{1,0:T(8,128)(2,1)S(1)} %copy-done.1), channel_id=1, source_target_pairs={{2,0},{3,1},{6,4},{7,5},{10,8},{11,9},{14,12},{15,13},{18,16},{19,... | collective-permute-start | bytes 393224 | tf_op jit(solution)/shard_map/ppermute | solution.py:67
  44.6 4.4 %collective-permute-start.19 = (bf16[64,256]{1,0:T(8,128)(2,1)}, bf16[64,256]{1,0:T(8,128)(2,1)S(1)}, u32[]{:S(2)}, u32[]{:S(2)}) collective-permute-start(bf16[64,256]{1,0:T(8,128)(2,1)} %get-tuple-element.35), channel_id=1, source_target_pairs={{0,8},{4,12},{8,0},{12,4},{16,24},{20,28},{24,16},{28,20},{1,9},{5... | collective-permute-start | bytes 98312 | tf_op jit(solution)/shard_map/ppermute | solution.py:87
  46.2 5.3 %collective-permute-start.20 = (bf16[64,256]{1,0:T(8,128)(2,1)}, bf16[64,256]{1,0:T(8,128)(2,1)S(1)}, u32[]{:S(2)}, u32[]{:S(2)}) collective-permute-start(bf16[64,256]{1,0:T(8,128)(2,1)} %get-tuple-element.36), channel_id=1, source_target_pairs={{0,16},{4,20},{8,24},{12,28},{16,0},{20,4},{24,8},{28,12},{1,17},{... | collective-permute-start | bytes 98312 | tf_op jit(solution)/shard_map/ppermute | solution.py:87
  48.8 5.9 %collective-permute-start.21 = (bf16[64,256]{1,0:T(8,128)(2,1)}, bf16[64,256]{1,0:T(8,128)(2,1)S(1)}, u32[]{:S(2)}, u32[]{:S(2)}) collective-permute-start(bf16[64,256]{1,0:T(8,128)(2,1)} %get-tuple-element.37), channel_id=1, source_target_pairs={{0,24},{4,28},{8,16},{12,20},{16,8},{20,12},{24,0},{28,4},{1,25},{... | collective-permute-start | bytes 98312 | tf_op jit(solution)/shard_map/ppermute | solution.py:87
  49.0 5.7 %copy-start.22 = (bf16[64,256]{1,0:T(8,128)(2,1)}, bf16[64,256]{1,0:T(8,128)(2,1)S(1)}, u32[]{:S(2)}) copy-start(bf16[64,256]{1,0:T(8,128)(2,1)S(1)} %collective-permute-done.19.refs_1_) | copy-start | bytes 98308
  56.8 6.9 %collective-permute-start.22 = (bf16[64,256]{1,0:T(8,128)(2,1)}, bf16[64,256]{1,0:T(8,128)(2,1)S(1)}, u32[]{:S(2)}, u32[]{:S(2)}) collective-permute-start(bf16[64,256]{1,0:T(8,128)(2,1)} %shard_map.133.refs_0_), channel_id=1, source_target_pairs={{0,8},{4,12},{8,0},{12,4},{16,24},{20,28},{24,16},{28,20},{1,9},{5... | collective-permute-start | bytes 98312 | tf_op jit(solution)/shard_map/ppermute | solution.py:87
  56.8 8.2 %collective-permute-start.23 = (bf16[64,256]{1,0:T(8,128)(2,1)}, bf16[64,256]{1,0:T(8,128)(2,1)S(1)}, u32[]{:S(2)}, u32[]{:S(2)}) collective-permute-start(bf16[64,256]{1,0:T(8,128)(2,1)} %shard_map.133.refs_0_), channel_id=1, source_target_pairs={{0,16},{4,20},{8,24},{12,28},{16,0},{20,4},{24,8},{28,12},{1,17},{... | collective-permute-start | bytes 98312 | tf_op jit(solution)/shard_map/ppermute | solution.py:87
  57.7 8.5 %collective-permute-start.24 = (bf16[64,256]{1,0:T(8,128)(2,1)}, bf16[64,256]{1,0:T(8,128)(2,1)S(1)}, u32[]{:S(2)}, u32[]{:S(2)}) collective-permute-start(bf16[64,256]{1,0:T(8,128)(2,1)} %shard_map.133.refs_0_), channel_id=1, source_target_pairs={{0,24},{4,28},{8,16},{12,20},{16,8},{20,12},{24,0},{28,4},{1,25},{... | collective-permute-start | bytes 98312 | tf_op jit(solution)/shard_map/ppermute | solution.py:87
  61.2 7.1 %copy-start.2 = (bf16[128,512]{1,0:T(8,128)(2,1)}, bf16[128,512]{1,0:T(8,128)(2,1)S(1)}, u32[]{:S(2)}) copy-start(bf16[128,512]{1,0:T(8,128)(2,1)S(1)} %collective-permute-done.7.refs_5_) | copy-start | bytes 393220
  61.2 12.6 %collective-permute-start.6 = (bf16[128,512]{1,0:T(8,128)(2,1)S(1)}, bf16[128,512]{1,0:T(8,128)(2,1)S(1)}, u32[]{:S(2)}, u32[]{:S(2)}) collective-permute-start(bf16[128,512]{1,0:T(8,128)(2,1)S(1)} %copy-done), channel_id=1, source_target_pairs={{1,0},{3,2},{5,4},{7,6},{9,8},{11,10},{13,12},{15,14},{17,16},{19,... | collective-permute-start | bytes 393224 | tf_op jit(solution)/shard_map/ppermute | solution.py:61
  62.5 5.8 %copy-start.3 = (bf16[128,512]{1,0:T(8,128)(2,1)}, bf16[128,512]{1,0:T(8,128)(2,1)S(1)}, u32[]{:S(2)}) copy-start(bf16[128,512]{1,0:T(8,128)(2,1)S(1)} %collective-permute-done.10.refs_9_) | copy-start | bytes 393220
  62.5 11.3 %collective-permute-start.8 = (bf16[128,512]{1,0:T(8,128)(2,1)S(1)}, bf16[128,512]{1,0:T(8,128)(2,1)S(1)}, u32[]{:S(2)}, u32[]{:S(2)}) collective-permute-start(bf16[128,512]{1,0:T(8,128)(2,1)S(1)} %collective-permute-done.7.refs_5_), channel_id=1, source_target_pairs={{0,1},{1,0},{2,3},{3,2},{4,5},{5,4},{6,7},{7,6},{8,9},{9,8},{10,11... | collective-permute-start | bytes 393224 | tf_op jit(solution)/shard_map/ppermute | solution.py:61
  63.7 10.1 %collective-permute-start.9 = (bf16[128,512]{1,0:T(8,128)(2,1)S(1)}, bf16[128,512]{1,0:T(8,128)(2,1)S(1)}, u32[]{:S(2)}, u32[]{:S(2)}) collective-permute-start(bf16[128,512]{1,0:T(8,128)(2,1)S(1)} %copy-done.1), channel_id=1, source_target_pairs={{1,0},{3,2},{5,4},{7,6},{9,8},{11,10},{13,12},{15,14},{17,16},{19,... | collective-permute-start | bytes 393224 | tf_op jit(solution)/shard_map/ppermute | solution.py:61
  65.0 8.9 %collective-permute-start.11 = (bf16[128,512]{1,0:T(8,128)(2,1)S(1)}, bf16[128,512]{1,0:T(8,128)(2,1)S(1)}, u32[]{:S(2)}, u32[]{:S(2)}) collective-permute-start(bf16[128,512]{1,0:T(8,128)(2,1)S(1)} %collective-permute-done.10.refs_9_), channel_id=1, source_target_pairs={{0,1},{1,0},{2,3},{3,2},{4,5},{5,4},{6,7},{7,6},{8,9},{9,8},{10,11... | collective-permute-start | bytes 393224 | tf_op jit(solution)/shard_map/ppermute | solution.py:61
  68.3 10.8 %collective-permute-start.25 = (bf16[256,256]{1,0:T(8,128)(2,1)}, bf16[256,256]{1,0:T(8,128)(2,1)S(1)}, u32[]{:S(2)}, u32[]{:S(2)}) collective-permute-start(bf16[256,256]{1,0:T(8,128)(2,1)} %shard_map.134.refs_0_), channel_id=1, source_target_pairs={{0,4},{4,0},{8,12},{12,8},{16,20},{20,16},{24,28},{28,24},{1,5},{5... | collective-permute-start | bytes 393224 | tf_op jit(solution)/shard_map/ppermute | solution.py:87
  (22 other events, 23.6 us)

commit v2 on v1

--- a/solution.py
+++ b/solution.py
@@ -1,4 +1,5 @@
 import functools
+import math
 
 import jax
 import jax.numpy as jnp
@@ -7,13 +8,14 @@
 from jax.experimental.pallas import tpu as pltpu
 from jax.sharding import PartitionSpec as P
 
-HEADS = 8
+
 HEAD = 64
 PAIR = 2 * HEAD
 EPS = 1e-05
 F32 = jnp.float32
 BF16 = jnp.bfloat16
 CORES = 2
+WORK_BYTES = 8 << 20
 
 NT = (((1,), (1,)), ((), ()))
 NN = (((1,), (0,)), ((), ()))
@@ -21,11 +23,17 @@
 
 def dot(a, b, dims=NN):
     return lax.dot_general(a, b, dims, preferred_element_type=F32)
+
+
+def nbytes(shape, dtype):
+    return math.prod(shape) * jnp.dtype(dtype).itemsize
 
 
 def call(kernel, outs, *args, scalars=0, scratch=(), flops=0):
     smem = pl.BlockSpec(memory_space=pltpu.SMEM)
     vmem = pl.BlockSpec(memory_space=pltpu.VMEM)
+    held = sum(nbytes(x.shape, x.dtype) for x in args) + sum(nbytes(*o) for o in outs)
+    held += sum(nbytes(x.shape, x.dtype) for x in scratch)
     return pl.pallas_call(
         kernel,
         out_shape=[jax.ShapeDtypeStruct(s, d) for s, d in outs],
@@ -33,46 +41,40 @@
         out_specs=[vmem] * len(outs),
         scratch_shapes=list(scratch),
         cost_estimate=pl.CostEstimate(flops=flops, transcendentals=0, bytes_accessed=0),
+        compiler_params=pltpu.CompilerParams(vmem_limit_bytes=held + WORK_BYTES),
     )(*args)
 
 
-def partner(index, k, size):
-    if size & (size - 1) == 0:
+def is_pow2(size):
+    return size & (size - 1) == 0
+
+
+def target(index, k, size):
+    if is_pow2(size):
         return index ^ k
-    return (index + k) % size
+    return (index + k) % size if isinstance(index, int) else lax.rem(index + k, size)
 
 
 def source(index, k, size):
-    if size & (size - 1) == 0:
+    if is_pow2(size):
         return index ^ k
-    return (index - k) % size if isinstance(index, int) else lax.rem(index - k + size, size)
-
-
-def target(index, k, size):
-    if size & (size - 1) == 0:
-        return index ^ k
-    return lax.rem(index + k, size)
-
-
-def swap_core(x, lanes, down=None):
-    pairs = [(i, i ^ 1) for i in range(lanes)]
-    if down is not None:
-        pairs = [(s, d) for s, d in pairs if (d < s) == down]
-    return lax.ppermute(x, "blk", pairs)
-
-
-def over_chips(x, lanes, k, down):
-    step = -k * CORES if down else k * CORES
-    pairs = [(i, i + step) for i in range(lanes) if 0 <= i + step < lanes]
+    return (index - k) % size if isinstance(index, int) else lax.rem(index + size - k, size)
+
+
+def over_blk(x, lanes, step, other):
+    chips = lanes // CORES
+    pairs = []
+    for i in range(lanes):
+        chip, core = divmod(i, CORES)
+        pairs.append((i, target(chip, step, chips) * CORES + (core + other) % CORES))
     return lax.ppermute(x, "blk", pairs)
 
 
 def digits(groups):
     out, stride = [], 1
-    for size in (2, 4):
-        if groups // stride > 1 and (groups // stride) % size == 0:
-            out.append((stride, size))
-            stride *= size
+    while groups // stride % 2 == 0:
+        out.append((stride, 2))
+        stride *= 2
     if groups // stride > 1:
         out.append((stride, groups // stride))
     return out
@@ -83,7 +85,7 @@
     pairs = []
     for i in range(groups):
         d = (i // stride) % size
-        pairs.append((i, i + (partner(d, k, size) - d) * stride))
+        pairs.append((i, i + (target(d, k, size) - d) * stride))
     return lax.ppermute(x, "grp", pairs)
 
 
@@ -108,15 +110,14 @@
     return jnp.where(low_lanes(top.shape), top, bottom)
 
 
-def store_blocks(dst, refs, lanes, later):
+def store_blocks(dst, refs, lanes):
     pos = lax.axis_index("blk")
     rows = refs[0].shape[0]
     chips = lanes // CORES
     chip, core = lax.div(pos, CORES), lax.rem(pos, CORES)
     for n, ref in enumerate(refs):
-        step, other = n // 2, n % 2
-        move = step if later else chips - step
-        block = lax.rem(chip + move, chips) * CORES + lax.rem(core + other, CORES)
+        step, other = n // CORES, n % CORES
+        block = source(chip, step, chips) * CORES + lax.rem(core + other, CORES)
         dst[pl.ds(pl.multiple_of(block * rows, rows), rows), :] = ref[...]
 
 
@@ -127,8 +128,13 @@
     return jnp.where(row < length, row, -1)
 
 
-def mixed_grad_kernel(og_ref, w_ref, mg_ref):
+def mixed_grad_kernel(chips, og_ref, w_ref, mg_ref, *cols_refs):
     mg_ref[...] = dot(og_ref[...], w_ref[...], NT)
+    chip = lax.div(lax.axis_index("blk"), CORES)
+    width = cols_refs[0].shape[1]
+    for k, ref in enumerate(cols_refs):
+        at = target(chip, k, chips) * width
+        ref[...] = og_ref[:, pl.ds(pl.multiple_of(at, width), width)]
 
 
 def forward_kernel(lanes, *refs):
@@ -143,8 +149,8 @@
     rows, feats = q_ref.shape
     total = kall.shape[0]
     tile = min(total, 512)
-    store_blocks(kall, k_refs, lanes, False)
-    store_blocks(vall, v_refs, lanes, False)
+    store_blocks(kall, k_refs, lanes)
+    store_blocks(vall, v_refs, lanes)
     limit = limits(length, (2 * rows, tile), rows)
     key = lax.broadcasted_iota(jnp.int32, (2 * rows, tile), 1)
     for p in range(feats // PAIR):
@@ -218,8 +224,8 @@
     rows, feats = k_ref.shape
     total = qall.shape[0]
     tile = min(total, 512)
-    store_blocks(qall, q_refs, lanes, True)
-    store_blocks(gall, g_refs, lanes, True)
+    store_blocks(qall, q_refs, lanes)
+    store_blocks(gall, g_refs, lanes)
     pos = lax.axis_index("blk")
     mine = lax.rem(lax.broadcasted_iota(jnp.int32, (2 * rows, tile), 0), rows) + pos * rows
     query = lax.broadcasted_iota(jnp.int32, (2 * rows, tile), 1)
@@ -263,7 +269,16 @@
 def product_kernel(lanes, digit, *refs):
     m_refs, o_refs = refs[:lanes], refs[lanes : 2 * lanes]
     outs, acc = refs[2 * lanes : -1], refs[-1]
-    acc[...] = sum(dot(m[...], o[...]) for m, o in zip(m_refs, o_refs))
+    width = acc.shape[1]
+    first = lax.rem(lax.axis_index("blk"), CORES) == 0
+    total = None
+    for n in range(0, lanes, CORES):
+        lhs = jnp.concatenate([m[...] for m in m_refs[n : n + CORES]], axis=1)
+        rhs = jnp.concatenate([o[...] for o in o_refs[n : n + CORES]], axis=0)
+        rhs = jnp.where(first, rhs[:, :width], rhs[:, width:])
+        part = dot(lhs, rhs)
+        total = part if total is None else total + part
+    acc[...] = total
     split(acc, digit, outs[0], outs[1:])
 
 
@@ -299,36 +314,38 @@
         out[pl.ds(pl.multiple_of(at * part, part), part), :] = ref[...].astype(out.dtype)
 
 
-def shards(query, key, value, gate_u, out_grad, lengths, norm_gain, out_weight):
+def layer(query, key, value, gate_u, out_grad, lengths, norm_gain, out_weight):
     rows, feats = query.shape
     model = out_grad.shape[1]
     lanes = lax.axis_size("blk")
     groups = lax.axis_size("grp")
     chips = lanes // CORES
-    pos = lax.axis_index("blk")
     total = rows * lanes
     width = model // lanes
-
-    def spread(x, later):
-        cross = [over_chips(x, lanes, k, later) for k in range(1, chips)]
-        pieces = [x, swap_core(x, lanes, later)]
-        for c in cross:
-            pieces += [c, swap_core(c, lanes)]
-        return pieces
-
-    keys = spread(key, False)
-    values = spread(value, False)
-    columns = [
-        lax.dynamic_slice_in_dim(out_grad, target(pos, k, lanes) * width, width, 1)
-        for k in range(lanes)
-    ]
-    blk_pairs = [[(i, partner(i, k, lanes)) for i in range(lanes)] for k in range(lanes)]
-    columns = columns[:1] + [lax.ppermute(columns[k], "blk", blk_pairs[k]) for k in range(1, lanes)]
-    queries = spread(query, True)
-
-    (mixed_grad,) = call(
-        mixed_grad_kernel, [((rows, feats), F32)], out_grad, out_weight, flops=2 * rows * feats * model
-    )
+    steps = range(1, chips)
+
+    def cross(x):
+        return [over_blk(x, lanes, k, 0) for k in steps]
+
+    def cores(pieces):
+        out = []
+        for x in pieces:
+            out += [x, over_blk(x, lanes, 0, 1)]
+        return out
+
+    keys = cores([key] + cross(key))
+    values = cores([value] + cross(value))
+    mixed_grad, *columns = call(
+        functools.partial(mixed_grad_kernel, chips),
+        [((rows, feats), F32)] + [((rows, model // chips), BF16)] * chips,
+        out_grad,
+        out_weight,
+        flops=2 * rows * feats * model,
+    )
+    moved = [over_blk(columns[k], lanes, k, 0) for k in steps]
+    columns = cores([columns[0]] + moved)
+    queries = cores([query] + cross(query))
+
     attention_flops = 4 * rows * total * feats
     mixed, mixed_t, att_grad, grad_gate, kall, vall = call(
         functools.partial(forward_kernel, lanes),
@@ -351,14 +368,16 @@
         scratch=[pltpu.VMEM((rows, feats), F32)],
         flops=attention_flops,
     )
-    mixes = [mixed_t] + [lax.ppermute(mixed_t, "blk", blk_pairs[k]) for k in range(1, lanes)]
-    grads = spread(att_grad, True)
+    mixes = [mixed_t]
+    for n in range(1, lanes):
+        mixes.append(over_blk(mixed_t, lanes, n // CORES, n % CORES))
+    grads = cores([att_grad] + cross(att_grad))
 
     stages = digits(groups)
     size = feats
     plan = []
-    for digit in stages:
-        parts = digit[1] if size % (16 * digit[1]) == 0 else 1
+    for n, digit in enumerate(stages):
+        parts = digit[1] if n == 0 and size % (16 * digit[1]) == 0 else 1
         size //= parts
         plan.append((digit, parts, size))
 
@@ -415,7 +434,7 @@
                 None if parts > 1 else digit,
                 nxt[0] if split_next else None,
             ),
-            [((part, width), BF16 if last else F32)] if not split_next else pieces_of(nxt[1], nxt[2]),
+            [((part, width), BF16)] if not split_next else pieces_of(nxt[1], nxt[2]),
             held[0],
             *received,
             scratch=[pltpu.VMEM((part if parts > 1 else part * digit[1], width), F32)],
@@ -436,7 +455,7 @@
 def solution(mesh):
     rows = P(("grp", "blk"), None)
     return jax.shard_map(
-        shards,
+        layer,
         mesh=mesh,
         in_specs=(rows, rows, rows, rows, rows, P("grp"), P(), P()),
         out_specs=(rows, rows, rows, rows, rows, P(None, "blk")),

time: 82.3 us -> 51.1 us (0.62)
  Pallas kernels: 23.1 us -> 8.76 us
  starting transfers between devices: 33.1 us -> 18.9 us
  local copies, waits for them, and re-layouts: 6.96 us -> 2.2 us
  waiting for transfers between devices: 16.9 us -> 19.5 us
    pallas_call x9, Pallas kernels: 23.1 us -> 8.76 us  [call(): pl.pallas_call(kernel, out_shape=[jax.ShapeDtypeStruct(s, d) for s, d in...]
    ppermute x18, starting transfers between devices: 21.2 us -> 11 us  [over_blk(): return lax.ppermute(x, 'blk', pairs)]
    ppermute x8 -> x4, starting transfers between devices: 11.9 us -> 7.95 us  [over_digit(): return lax.ppermute(x, 'grp', pairs)]
    unnamed x56 -> x16, local copies, waits for them, and re-layouts: 5.34 us -> 2.2 us
    ppermute x8 -> x4, waiting for transfers between devices: 7.29 us -> 10.1 us  [over_digit(): return lax.ppermute(x, 'grp', pairs)]
    dynamic_slice x1 -> x0, local copies, waits for them, and re-layouts: 1.62 us -> none  [shards(): lax.dynamic_slice_in_dim(out_grad, target(pos, k, lanes) * width, width, 1)]
  transfers between devices with their start and end apart: 26 -> 22, of which waited for: 7 -> 8; matrix products, arithmetic and copies ran while one was open for 2% -> 0% of each run, Pallas kernels for 23% -> 15%
where the time goes in v2:
time: 51.1 us; the launch traced here: 50.9 us
  waiting for transfers between devices  19.5 us (38%)
  starting transfers between devices  18.9 us (37%)
  Pallas kernels  8.76 us (17%)
  local copies, waits for them, and re-layouts  2.2 us (4%)
  between operations  1.44 us (3%)
    ppermute x18, starting transfers between devices, over_blk(): return lax.ppermute(x, 'blk', pairs)  11 us
    ppermute x4, waiting for transfers between devices, over_digit(): return lax.ppermute(x, 'grp', pairs)  10.1 us
    ppermute x18, waiting for transfers between devices, over_blk(): return lax.ppermute(x, 'blk', pairs)  9.43 us
    pallas_call x9, Pallas kernels, call(): pl.pallas_call(kernel, out_shape=[jax.ShapeDtypeStruct(s, d) for s, d in...  8.76 us
    ppermute x4, starting transfers between devices, over_digit(): return lax.ppermute(x, 'grp', pairs)  7.95 us
    unnamed x16, local copies, waits for them, and re-layouts  2.2 us
  transfers between devices with their start and end apart: 22, of which 8 were waited for; matrix products, arithmetic and copies ran while one was open for 0% of the time, Pallas kernels for 15%

profile of v2, /device:TPU:0, one launch (start us, length us, event | category | flops | bytes accessed | tf_op | source)
XLA Modules:
  0.0 50.9 jit_solution(14941500329772950851)
XLA Ops:
  0.6 3.0 %collective-permute-start.1 = (bf16[128,512]{1,0:T(8,128)(2,1)}, bf16[128,512]{1,0:T(8,128)(2,1)S(1)}, u32[]{:S(2)}, u32[]{:S(2)}) collective-permute-start(bf16[128,512]{1,0:T(8,128)(2,1)} %refs_1_.3), channel_id=1, source_target_pairs={{0,2},{1,3},{2,0},{3,1},{4,6},{5,7},{6,4},{7,5},{8,10},{9,11},{10,... | collective-permute-start | bytes 393224 | tf_op jit(solution)/shard_map/ppermute | solution.py:70
  3.7 0.1 collective-permute-start.4
  3.7 0.5 collective-permute-start.3
  4.3 1.2 %copy-done = bf16[512,1024]{1,0:T(8,128)(2,1)S(1)} copy-done((bf16[512,1024]{1,0:T(8,128)(2,1)S(1)}, bf16[512,1024]{1,0:T(8,128)(2,1)}, u32[]{:S(2)}) %copy-start) | copy-done | bytes 1048600
  5.5 0.9 %copy-done.5 = bf16[128,1024]{1,0:T(8,128)(2,1)S(1)} copy-done((bf16[128,1024]{1,0:T(8,128)(2,1)S(1)}, bf16[128,1024]{1,0:T(8,128)(2,1)}, u32[]{:S(2)}) %copy-start.5) | copy-done | bytes 262168
  6.4 0.5 shard_map.127
  6.9 2.0 %collective-permute-start.16 = (bf16[128,512]{1,0:T(8,128)(2,1)S(1)}, bf16[128,512]{1,0:T(8,128)(2,1)S(1)}, u32[]{:S(2)}, u32[]{:S(2)}) collective-permute-start(bf16[128,512]{1,0:T(8,128)(2,1)S(1)} %get-tuple-element.33), channel_id=1, source_target_pairs={{0,2},{1,3},{2,0},{3,1},{4,6},{5,7},{6,4},{7,5},{8,10},{9,11},{10,... | collective-permute-start | bytes 393224 | tf_op jit(solution)/shard_map/ppermute | solution.py:70
  9.0 1.6 %collective-permute-done.4.refs_8_ = bf16[128,512]{1,0:T(8,128)(2,1)S(1)} collective-permute-done((bf16[128,512]{1,0:T(8,128)(2,1)}, bf16[128,512]{1,0:T(8,128)(2,1)S(1)}, u32[]{:S(2)}, u32[]{:S(2)}) %collective-permute-start.4) | collective-permute-done | bytes 131104 | tf_op jit(solution)/shard_map/ppermute | solution.py:70
  11.2 0.6 %collective-permute-start.15 = (bf16[128,512]{1,0:T(8,128)(2,1)S(1)}, bf16[128,512]{1,0:T(8,128)(2,1)S(1)}, u32[]{:S(2)}, u32[]{:S(2)}) collective-permute-start(bf16[128,512]{1,0:T(8,128)(2,1)S(1)} %get-tuple-element.32.refs_4_), channel_id=1, source_target_pairs={{0,1},{1,0},{2,3},{3,2},{4,5},{5,4},{6,7},{7,6},{8,9},{9,8},{10,11... | collective-permute-start | bytes 393224 | tf_op jit(solution)/shard_map/ppermute | solution.py:70
  11.8 1.2 %collective-permute-done.16.refs_6_ = bf16[128,512]{1,0:T(8,128)(2,1)S(1)} collective-permute-done((bf16[128,512]{1,0:T(8,128)(2,1)S(1)}, bf16[128,512]{1,0:T(8,128)(2,1)S(1)}, u32[]{:S(2)}, u32[]{:S(2)}) %collective-permute-start.16) | collective-permute-done | bytes 131104 | tf_op jit(solution)/shard_map/ppermute | solution.py:70
  13.1 2.0 %shard_map.128 = (bf16[128,512]{1,0:T(8,128)(2,1)S(1)}, bf16[512,128]{1,0:T(8,128)(2,1)S(1)}, bf16[128,512]{1,0:T(8,128)(2,1)S(1)}, bf16[128,512]{1,0:T(8,128)(2...) custom-call(s32[1]{0:T(128)S(6)} %copy.14.refs_0_.len_ref, bf16[128,512]{1,0:T(8,128)(2,1)S(1)} %copy-done.2, ...), custom_call_target="tpu_custom_call" | custom-call | flops 134217728 | tf_op jit(solution)/shard_map/pallas_call | solution.py:37
  15.1 0.5 collective-permute-start.12
  15.6 1.7 %collective-permute-start.13 = (bf16[512,128]{1,0:T(8,128)(2,1)S(1)}, bf16[512,128]{1,0:T(8,128)(2,1)S(1)}, u32[]{:S(2)}, u32[]{:S(2)}) collective-permute-start(bf16[512,128]{1,0:T(8,128)(2,1)S(1)} %get-tuple-element.31.refs_0_), channel_id=1, source_target_pairs={{0,2},{1,3},{2,0},{3,1},{4,6},{5,7},{6,4},{7,5},{8,10},{9,11},{10,... | collective-permute-start | bytes 393224 | tf_op jit(solution)/shard_map/ppermute | solution.py:70
  17.3 4.3 %collective-permute-done.13.refs_2_ = bf16[512,128]{1,0:T(8,128)(2,1)S(1)} collective-permute-done((bf16[512,128]{1,0:T(8,128)(2,1)S(1)}, bf16[512,128]{1,0:T(8,128)(2,1)S(1)}, u32[]{:S(2)}, u32[]{:S(2)}) %collective-permute-start.13) | collective-permute-done | bytes 131104 | tf_op jit(solution)/shard_map/ppermute | solution.py:70
  21.7 1.4 %collective-permute-done.14.refs_3_ = bf16[512,128]{1,0:T(8,128)(2,1)S(1)} collective-permute-done((bf16[512,128]{1,0:T(8,128)(2,1)S(1)}, bf16[512,128]{1,0:T(8,128)(2,1)S(1)}, u32[]{:S(2)}, u32[]{:S(2)}) %collective-permute-start.14) | collective-permute-done | bytes 131104 | tf_op jit(solution)/shard_map/ppermute | solution.py:70
  23.1 0.3 shard_map.131
  23.5 1.6 %collective-permute-start.18 = (bf16[256,256]{1,0:T(8,128)(2,1)S(1)}, bf16[256,256]{1,0:T(8,128)(2,1)S(1)}, u32[]{:S(2)}, u32[]{:S(2)}) collective-permute-start(bf16[256,256]{1,0:T(8,128)(2,1)S(1)} %get-tuple-element.35), channel_id=1, source_target_pairs={{0,4},{4,0},{8,12},{12,8},{16,20},{20,16},{24,28},{28,24},{1,5},{5... | collective-permute-start | bytes 393224 | tf_op jit(solution)/shard_map/ppermute | solution.py:89
  25.1 4.4 %collective-permute-done.18.refs_1_ = bf16[256,256]{1,0:T(8,128)(2,1)S(1)} collective-permute-done((bf16[256,256]{1,0:T(8,128)(2,1)S(1)}, bf16[256,256]{1,0:T(8,128)(2,1)S(1)}, u32[]{:S(2)}, u32[]{:S(2)}) %collective-permute-start.18) | collective-permute-done | bytes 131104 | tf_op jit(solution)/shard_map/ppermute | solution.py:89
  29.5 1.8 %collective-permute-start.19 = (bf16[256,256]{1,0:T(8,128)(2,1)S(1)}, bf16[256,256]{1,0:T(8,128)(2,1)S(1)}, u32[]{:S(2)}, u32[]{:S(2)}) collective-permute-start(bf16[256,256]{1,0:T(8,128)(2,1)S(1)} %shard_map.132.refs_0_), channel_id=1, source_target_pairs={{0,8},{4,12},{8,0},{12,4},{16,24},{20,28},{24,16},{28,20},{1,9},{5... | collective-permute-start | bytes 393224 | tf_op jit(solution)/shard_map/ppermute | solution.py:89
  31.4 1.5 %collective-permute-start.7 = (bf16[128,512]{1,0:T(8,128)(2,1)S(1)}, bf16[128,512]{1,0:T(8,128)(2,1)S(1)}, u32[]{:S(2)}, u32[]{:S(2)}) collective-permute-start(bf16[128,512]{1,0:T(8,128)(2,1)S(1)} %copy-done.2), channel_id=1, source_target_pairs={{0,2},{1,3},{2,0},{3,1},{4,6},{5,7},{6,4},{7,5},{8,10},{9,11},{10,... | collective-permute-start | bytes 393224 | tf_op jit(solution)/shard_map/ppermute | solution.py:70
  32.9 0.5 %collective-permute-start.10 = (bf16[128,512]{1,0:T(8,128)(2,1)S(1)}, bf16[128,512]{1,0:T(8,128)(2,1)S(1)}, u32[]{:S(2)}, u32[]{:S(2)}) collective-permute-start(bf16[128,512]{1,0:T(8,128)(2,1)S(1)} %get-tuple-element.24.ag_ref.refs_7_), channel_id=1, source_target_pairs={{0,2},{1,3},{2,0},{3,1},{4,6},{5,7},{6,4},{7,5},{8,10},{9,11},{10,... | collective-permute-start | bytes 393224 | tf_op jit(solution)/shard_map/ppermute | solution.py:70
  33.4 1.5 %collective-permute-done.19.refs_1_ = bf16[256,256]{1,0:T(8,128)(2,1)S(1)} collective-permute-done((bf16[256,256]{1,0:T(8,128)(2,1)S(1)}, bf16[256,256]{1,0:T(8,128)(2,1)S(1)}, u32[]{:S(2)}, u32[]{:S(2)}) %collective-permute-start.19) | collective-permute-done | bytes 131104 | tf_op jit(solution)/shard_map/ppermute | solution.py:89
  34.9 0.1 shard_map.133.refs_0_
  35.0 2.8 %collective-permute-start.20 = (bf16[256,256]{1,0:T(8,128)(2,1)S(1)}, bf16[256,256]{1,0:T(8,128)(2,1)S(1)}, u32[]{:S(2)}, u32[]{:S(2)}) collective-permute-start(bf16[256,256]{1,0:T(8,128)(2,1)S(1)} %shard_map.133.refs_0_), channel_id=1, source_target_pairs={{0,16},{4,20},{8,24},{12,28},{16,0},{20,4},{24,8},{28,12},{1,17},{... | collective-permute-start | bytes 393224 | tf_op jit(solution)/shard_map/ppermute | solution.py:89
  37.8 0.5 collective-permute-start.8
  38.4 0.8 %collective-permute-done.10.refs_9_ = bf16[128,512]{1,0:T(8,128)(2,1)S(1)} collective-permute-done((bf16[128,512]{1,0:T(8,128)(2,1)S(1)}, bf16[128,512]{1,0:T(8,128)(2,1)S(1)}, u32[]{:S(2)}, u32[]{:S(2)}) %collective-permute-start.10) | collective-permute-done | bytes 131104 | tf_op jit(solution)/shard_map/ppermute | solution.py:70
  39.2 4.1 %collective-permute-done.20.refs_1_ = bf16[256,256]{1,0:T(8,128)(2,1)S(1)} collective-permute-done((bf16[256,256]{1,0:T(8,128)(2,1)S(1)}, bf16[256,256]{1,0:T(8,128)(2,1)S(1)}, u32[]{:S(2)}, u32[]{:S(2)}) %collective-permute-start.20) | collective-permute-done | bytes 131104 | tf_op jit(solution)/shard_map/ppermute | solution.py:89
  43.3 0.1 shard_map.134.refs_0_
  43.4 1.7 %collective-permute-start.21 = (bf16[256,256]{1,0:T(8,128)(2,1)S(1)}, bf16[256,256]{1,0:T(8,128)(2,1)S(1)}, u32[]{:S(2)}, u32[]{:S(2)}) collective-permute-start(bf16[256,256]{1,0:T(8,128)(2,1)S(1)} %shard_map.134.refs_0_), channel_id=1, source_target_pairs={{0,4},{4,0},{8,12},{12,8},{16,20},{20,16},{24,28},{28,24},{1,5},{5... | collective-permute-start | bytes 393224 | tf_op jit(solution)/shard_map/ppermute | solution.py:89
  45.1 2.3 %shard_map.129 = (bf16[128,1024]{1,0:T(8,128)(2,1)}, bf16[128,512]{1,0:T(8,128)(2,1)}) custom-call(s32[1]{0:T(128)S(6)} %copy.14.refs_0_.len_ref, bf16[128,512]{1,0:T(8,128)(2,1)S(1)} %copy-done.2, bf16[512,512]{1,0:T(8,128)(2,1)S(1)} %get-tuple-element.22.kall, bf16[512,512]{1,0:T(8,128)(2,1)S(1)} %get-tuple-element.23.vall, ...), custom_call_target="tpu_custom_call" | custom-call | flops 134217728 | tf_op jit(solution)/shard_map/pallas_call | solution.py:37
  47.4 2.6 %shard_map.130 = (bf16[128,512]{1,0:T(8,128)(2,1)}, bf16[128,512]{1,0:T(8,128)(2,1)}) custom-call(s32[1]{0:T(128)S(6)} %copy.14.refs_0_.len_ref, bf16[128,512]{1,0:T(8,128)(2,1)S(1)} %copy-done.3, bf16[128,512]{1,0:T(8,128)(2,1)S(1)} %copy-done.4, bf16[128,512]{1,0:T(8,128)(2,1)S(1)} %copy-done.2, bf16[128,512]{1,0:T(8,128)(2,1)S(1)} %collective-permute-done.6.refs_4_, ...), custom_call_target="tpu_custom_call" | custom-call | flops 268435456 | tf_op jit(solution)/shard_map/pallas_call | solution.py:37
  50.0 0.8 %shard_map.135 = f32[512,256]{1,0:T(8,128)} custom-call(bf16[256,256]{1,0:T(8,128)(2,1)S(1)} %shard_map.134.refs_0_, bf16[256,256]{1,0:T(8,128)(2,1)S(1)} %collective-permute-done.21.refs_1_), custom_call_target="tpu_custom_call" | custom-call | tf_op jit(solution)/shard_map/pallas_call | solution.py:37
  (37 shorter events, 0.1 us)
Async XLA Ops:
  0.6 8.3 %collective-permute-start.1 = (bf16[128,512]{1,0:T(8,128)(2,1)}, bf16[128,512]{1,0:T(8,128)(2,1)S(1)}, u32[]{:S(2)}, u32[]{:S(2)}) collective-permute-start(bf16[128,512]{1,0:T(8,128)(2,1)} %refs_1_.3), channel_id=1, source_target_pairs={{0,2},{1,3},{2,0},{3,1},{4,6},{5,7},{6,4},{7,5},{8,10},{9,11},{10,... | collective-permute-start | bytes 393224 | tf_op jit(solution)/shard_map/ppermute | solution.py:70
  3.7 6.9 %collective-permute-start.4 = (bf16[128,512]{1,0:T(8,128)(2,1)}, bf16[128,512]{1,0:T(8,128)(2,1)S(1)}, u32[]{:S(2)}, u32[]{:S(2)}) collective-permute-start(bf16[128,512]{1,0:T(8,128)(2,1)} %refs_2_.3), channel_id=1, source_target_pairs={{0,2},{1,3},{2,0},{3,1},{4,6},{5,7},{6,4},{7,5},{8,10},{9,11},{10,... | collective-permute-start | bytes 393224 | tf_op jit(solution)/shard_map/ppermute | solution.py:70
  3.7 7.5 %collective-permute-start = (bf16[128,512]{1,0:T(8,128)(2,1)}, bf16[128,512]{1,0:T(8,128)(2,1)S(1)}, u32[]{:S(2)}, u32[]{:S(2)}) collective-permute-start(bf16[128,512]{1,0:T(8,128)(2,1)} %refs_1_.3), channel_id=1, source_target_pairs={{0,1},{1,0},{2,3},{3,2},{4,5},{5,4},{6,7},{7,6},{8,9},{9,8},{10,11... | collective-permute-start | bytes 393224 | tf_op jit(solution)/shard_map/ppermute | solution.py:70
  3.7 9.2 %collective-permute-start.3 = (bf16[128,512]{1,0:T(8,128)(2,1)}, bf16[128,512]{1,0:T(8,128)(2,1)S(1)}, u32[]{:S(2)}, u32[]{:S(2)}) collective-permute-start(bf16[128,512]{1,0:T(8,128)(2,1)} %refs_2_.3), channel_id=1, source_target_pairs={{0,1},{1,0},{2,3},{3,2},{4,5},{5,4},{6,7},{7,6},{8,9},{9,8},{10,11... | collective-permute-start | bytes 393224 | tf_op jit(solution)/shard_map/ppermute | solution.py:70
  4.3 1.2 %copy-start = (bf16[512,1024]{1,0:T(8,128)(2,1)S(1)}, bf16[512,1024]{1,0:T(8,128)(2,1)}, u32[]{:S(2)}) copy-start(bf16[512,1024]{1,0:T(8,128)(2,1)} %w_ref.3) | copy-start | bytes 3145732
  5.5 0.9 %copy-start.5 = (bf16[128,1024]{1,0:T(8,128)(2,1)S(1)}, bf16[128,1024]{1,0:T(8,128)(2,1)}, u32[]{:S(2)}) copy-start(bf16[128,1024]{1,0:T(8,128)(2,1)} %og_ref.1) | copy-start | bytes 786436
  6.4 6.6 %copy-start.2 = (bf16[128,512]{1,0:T(8,128)(2,1)S(1)}, bf16[128,512]{1,0:T(8,128)(2,1)}, u32[]{:S(2)}) copy-start(bf16[128,512]{1,0:T(8,128)(2,1)} %refs_3_.1) | copy-start | bytes 393220
  6.4 6.6 %copy-start.3 = (bf16[128,512]{1,0:T(8,128)(2,1)S(1)}, bf16[128,512]{1,0:T(8,128)(2,1)}, u32[]{:S(2)}) copy-start(bf16[128,512]{1,0:T(8,128)(2,1)} %refs_1_.3) | copy-start | bytes 393220
  6.4 6.6 %copy-start.4 = (bf16[128,512]{1,0:T(8,128)(2,1)S(1)}, bf16[128,512]{1,0:T(8,128)(2,1)}, u32[]{:S(2)}) copy-start(bf16[128,512]{1,0:T(8,128)(2,1)} %refs_2_.3) | copy-start | bytes 393220
  6.4 6.6 %copy-start.6 = (bf16[128,512]{1,0:T(8,128)(2,1)S(1)}, bf16[128,512]{1,0:T(8,128)(2,1)}, u32[]{:S(2)}) copy-start(bf16[128,512]{1,0:T(8,128)(2,1)} %refs_10_.1) | copy-start | bytes 393220
  6.9 6.1 %collective-permute-start.16 = (bf16[128,512]{1,0:T(8,128)(2,1)S(1)}, bf16[128,512]{1,0:T(8,128)(2,1)S(1)}, u32[]{:S(2)}, u32[]{:S(2)}) collective-permute-start(bf16[128,512]{1,0:T(8,128)(2,1)S(1)} %get-tuple-element.33), channel_id=1, source_target_pairs={{0,2},{1,3},{2,0},{3,1},{4,6},{5,7},{6,4},{7,5},{8,10},{9,11},{10,... | collective-permute-start | bytes 393224 | tf_op jit(solution)/shard_map/ppermute | solution.py:70
  8.9 4.1 %collective-permute-start.2 = (bf16[128,512]{1,0:T(8,128)(2,1)S(1)}, bf16[128,512]{1,0:T(8,128)(2,1)S(1)}, u32[]{:S(2)}, u32[]{:S(2)}) collective-permute-start(bf16[128,512]{1,0:T(8,128)(2,1)S(1)} %collective-permute-done.1.refs_4_), channel_id=1, source_target_pairs={{0,1},{1,0},{2,3},{3,2},{4,5},{5,4},{6,7},{7,6},{8,9},{9,8},{10,11... | collective-permute-start | bytes 393224 | tf_op jit(solution)/shard_map/ppermute | solution.py:70
  10.6 2.5 %collective-permute-start.5 = (bf16[128,512]{1,0:T(8,128)(2,1)S(1)}, bf16[128,512]{1,0:T(8,128)(2,1)S(1)}, u32[]{:S(2)}, u32[]{:S(2)}) collective-permute-start(bf16[128,512]{1,0:T(8,128)(2,1)S(1)} %collective-permute-done.4.refs_8_), channel_id=1, source_target_pairs={{0,1},{1,0},{2,3},{3,2},{4,5},{5,4},{6,7},{7,6},{8,9},{9,8},{10,11... | collective-permute-start | bytes 393224 | tf_op jit(solution)/shard_map/ppermute | solution.py:70
  11.2 1.8 %copy-start.7 = (f32[512]{0:T(512)S(1)}, f32[512]{0:T(512)}, u32[]{:S(2)}) copy-start(f32[512]{0:T(512)} %param.14) | copy-start | bytes 6148
  11.2 6.1 %collective-permute-start.15 = (bf16[128,512]{1,0:T(8,128)(2,1)S(1)}, bf16[128,512]{1,0:T(8,128)(2,1)S(1)}, u32[]{:S(2)}, u32[]{:S(2)}) collective-permute-start(bf16[128,512]{1,0:T(8,128)(2,1)S(1)} %get-tuple-element.32.refs_4_), channel_id=1, source_target_pairs={{0,1},{1,0},{2,3},{3,2},{4,5},{5,4},{6,7},{7,6},{8,9},{9,8},{10,11... | collective-permute-start | bytes 393224 | tf_op jit(solution)/shard_map/ppermute | solution.py:70
  13.0 4.3 %collective-permute-start.17 = (bf16[128,512]{1,0:T(8,128)(2,1)S(1)}, bf16[128,512]{1,0:T(8,128)(2,1)S(1)}, u32[]{:S(2)}, u32[]{:S(2)}) collective-permute-start(bf16[128,512]{1,0:T(8,128)(2,1)S(1)} %collective-permute-done.16.refs_6_), channel_id=1, source_target_pairs={{0,1},{1,0},{2,3},{3,2},{4,5},{5,4},{6,7},{7,6},{8,9},{9,8},{10,11... | collective-permute-start | bytes 393224 | tf_op jit(solution)/shard_map/ppermute | solution.py:70
  15.1 30.0 %copy-start.1 = (bf16[512,1024]{1,0:T(8,128)(2,1)S(1)}, bf16[512,1024]{1,0:T(8,128)(2,1)}, u32[]{:S(2)}) copy-start(bf16[512,1024]{1,0:T(8,128)(2,1)} %w_ref.3) | copy-start | bytes 3145732
  15.1 2.3 %collective-permute-start.12 = (bf16[512,128]{1,0:T(8,128)(2,1)S(1)}, bf16[512,128]{1,0:T(8,128)(2,1)S(1)}, u32[]{:S(2)}, u32[]{:S(2)}) collective-permute-start(bf16[512,128]{1,0:T(8,128)(2,1)S(1)} %get-tuple-element.31.refs_0_), channel_id=1, source_target_pairs={{0,1},{1,0},{2,3},{3,2},{4,5},{5,4},{6,7},{7,6},{8,9},{9,8},{10,11... | collective-permute-start | bytes 393224 | tf_op jit(solution)/shard_map/ppermute | solution.py:70
  15.6 6.1 %collective-permute-start.13 = (bf16[512,128]{1,0:T(8,128)(2,1)S(1)}, bf16[512,128]{1,0:T(8,128)(2,1)S(1)}, u32[]{:S(2)}, u32[]{:S(2)}) collective-permute-start(bf16[512,128]{1,0:T(8,128)(2,1)S(1)} %get-tuple-element.31.refs_0_), channel_id=1, source_target_pairs={{0,2},{1,3},{2,0},{3,1},{4,6},{5,7},{6,4},{7,5},{8,10},{9,11},{10,... | collective-permute-start | bytes 393224 | tf_op jit(solution)/shard_map/ppermute | solution.py:70
  17.3 5.8 %collective-permute-start.14 = (bf16[512,128]{1,0:T(8,128)(2,1)S(1)}, bf16[512,128]{1,0:T(8,128)(2,1)S(1)}, u32[]{:S(2)}, u32[]{:S(2)}) collective-permute-start(bf16[512,128]{1,0:T(8,128)(2,1)S(1)} %get-tuple-element.31.refs_0_), channel_id=1, source_target_pairs={{0,3},{1,2},{2,1},{3,0},{4,7},{5,6},{6,5},{7,4},{8,11},{9,10},{10,... | collective-permute-start | bytes 393224 | tf_op jit(solution)/shard_map/ppermute | solution.py:70
  23.5 6.1 %collective-permute-start.18 = (bf16[256,256]{1,0:T(8,128)(2,1)S(1)}, bf16[256,256]{1,0:T(8,128)(2,1)S(1)}, u32[]{:S(2)}, u32[]{:S(2)}) collective-permute-start(bf16[256,256]{1,0:T(8,128)(2,1)S(1)} %get-tuple-element.35), channel_id=1, source_target_pairs={{0,4},{4,0},{8,12},{12,8},{16,20},{20,16},{24,28},{28,24},{1,5},{5... | collective-permute-start | bytes 393224 | tf_op jit(solution)/shard_map/ppermute | solution.py:89
  29.5 5.4 %collective-permute-start.19 = (bf16[256,256]{1,0:T(8,128)(2,1)S(1)}, bf16[256,256]{1,0:T(8,128)(2,1)S(1)}, u32[]{:S(2)}, u32[]{:S(2)}) collective-permute-start(bf16[256,256]{1,0:T(8,128)(2,1)S(1)} %shard_map.132.refs_0_), channel_id=1, source_target_pairs={{0,8},{4,12},{8,0},{12,4},{16,24},{20,28},{24,16},{28,20},{1,9},{5... | collective-permute-start | bytes 393224 | tf_op jit(solution)/shard_map/ppermute | solution.py:89
  31.4 6.5 %collective-permute-start.7 = (bf16[128,512]{1,0:T(8,128)(2,1)S(1)}, bf16[128,512]{1,0:T(8,128)(2,1)S(1)}, u32[]{:S(2)}, u32[]{:S(2)}) collective-permute-start(bf16[128,512]{1,0:T(8,128)(2,1)S(1)} %copy-done.2), channel_id=1, source_target_pairs={{0,2},{1,3},{2,0},{3,1},{4,6},{5,7},{6,4},{7,5},{8,10},{9,11},{10,... | collective-permute-start | bytes 393224 | tf_op jit(solution)/shard_map/ppermute | solution.py:70
  32.9 6.3 %collective-permute-start.10 = (bf16[128,512]{1,0:T(8,128)(2,1)S(1)}, bf16[128,512]{1,0:T(8,128)(2,1)S(1)}, u32[]{:S(2)}, u32[]{:S(2)}) collective-permute-start(bf16[128,512]{1,0:T(8,128)(2,1)S(1)} %get-tuple-element.24.ag_ref.refs_7_), channel_id=1, source_target_pairs={{0,2},{1,3},{2,0},{3,1},{4,6},{5,7},{6,4},{7,5},{8,10},{9,11},{10,... | collective-permute-start | bytes 393224 | tf_op jit(solution)/shard_map/ppermute | solution.py:70
  35.0 8.3 %collective-permute-start.20 = (bf16[256,256]{1,0:T(8,128)(2,1)S(1)}, bf16[256,256]{1,0:T(8,128)(2,1)S(1)}, u32[]{:S(2)}, u32[]{:S(2)}) collective-permute-start(bf16[256,256]{1,0:T(8,128)(2,1)S(1)} %shard_map.133.refs_0_), channel_id=1, source_target_pairs={{0,16},{4,20},{8,24},{12,28},{16,0},{20,4},{24,8},{28,12},{1,17},{... | collective-permute-start | bytes 393224 | tf_op jit(solution)/shard_map/ppermute | solution.py:89
  37.8 9.6 %collective-permute-start.6 = (bf16[128,512]{1,0:T(8,128)(2,1)S(1)}, bf16[128,512]{1,0:T(8,128)(2,1)S(1)}, u32[]{:S(2)}, u32[]{:S(2)}) collective-permute-start(bf16[128,512]{1,0:T(8,128)(2,1)S(1)} %copy-done.2), channel_id=1, source_target_pairs={{0,1},{1,0},{2,3},{3,2},{4,5},{5,4},{6,7},{7,6},{8,9},{9,8},{10,11... | collective-permute-start | bytes 393224 | tf_op jit(solution)/shard_map/ppermute | solution.py:70
  37.8 9.6 %collective-permute-start.8 = (bf16[128,512]{1,0:T(8,128)(2,1)S(1)}, bf16[128,512]{1,0:T(8,128)(2,1)S(1)}, u32[]{:S(2)}, u32[]{:S(2)}) collective-permute-start(bf16[128,512]{1,0:T(8,128)(2,1)S(1)} %collective-permute-done.7.refs_5_), channel_id=1, source_target_pairs={{0,1},{1,0},{2,3},{3,2},{4,5},{5,4},{6,7},{7,6},{8,9},{9,8},{10,11... | collective-permute-start | bytes 393224 | tf_op jit(solution)/shard_map/ppermute | solution.py:70
  38.4 9.1 %collective-permute-start.9 = (bf16[128,512]{1,0:T(8,128)(2,1)S(1)}, bf16[128,512]{1,0:T(8,128)(2,1)S(1)}, u32[]{:S(2)}, u32[]{:S(2)}) collective-permute-start(bf16[128,512]{1,0:T(8,128)(2,1)S(1)} %get-tuple-element.24.ag_ref.refs_7_), channel_id=1, source_target_pairs={{0,1},{1,0},{2,3},{3,2},{4,5},{5,4},{6,7},{7,6},{8,9},{9,8},{10,11... | collective-permute-start | bytes 393224 | tf_op jit(solution)/shard_map/ppermute | solution.py:70
  39.2 8.2 %collective-permute-start.11 = (bf16[128,512]{1,0:T(8,128)(2,1)S(1)}, bf16[128,512]{1,0:T(8,128)(2,1)S(1)}, u32[]{:S(2)}, u32[]{:S(2)}) collective-permute-start(bf16[128,512]{1,0:T(8,128)(2,1)S(1)} %collective-permute-done.10.refs_9_), channel_id=1, source_target_pairs={{0,1},{1,0},{2,3},{3,2},{4,5},{5,4},{6,7},{7,6},{8,9},{9,8},{10,11... | collective-permute-start | bytes 393224 | tf_op jit(solution)/shard_map/ppermute | solution.py:70
  43.4 6.6 %collective-permute-start.21 = (bf16[256,256]{1,0:T(8,128)(2,1)S(1)}, bf16[256,256]{1,0:T(8,128)(2,1)S(1)}, u32[]{:S(2)}, u32[]{:S(2)}) collective-permute-start(bf16[256,256]{1,0:T(8,128)(2,1)S(1)} %shard_map.134.refs_0_), channel_id=1, source_target_pairs={{0,4},{4,0},{8,12},{12,8},{16,20},{20,16},{24,28},{28,24},{1,5},{5... | collective-permute-start | bytes 393224 | tf_op jit(solution)/shard_map/ppermute | solution.py:89

commit v3 on v2

--- a/solution.py
+++ b/solution.py
@@ -72,9 +72,10 @@
 
 def digits(groups):
     out, stride = [], 1
-    while groups // stride % 2 == 0:
-        out.append((stride, 2))
-        stride *= 2
+    for size in [4] + [2] * groups:
+        if groups // stride % size == 0:
+            out.append((stride, size))
+            stride *= size
     if groups // stride > 1:
         out.append((stride, groups // stride))
     return out
@@ -184,7 +185,8 @@
         - jnp.mean(normed_grad, axis=1, keepdims=True)
         - normed * jnp.mean(normed_grad * normed, axis=1, keepdims=True)
     )
-    ag_ref[...] = grad.astype(BF16)
+    ag_ref[:, :feats] = grad.astype(BF16)
+    ag_ref[:, feats:] = q_ref[...]
 
 
 def query_kernel(len_ref, q_ref, kall, vall, ag_ref, mixed_ref, w_ref, lo_ref, dq_ref):
@@ -217,15 +219,12 @@
 def key_kernel(lanes, *refs):
     count = lanes
     len_ref, k_ref, v_ref = refs[:3]
-    q_refs = refs[3 : 3 + count]
-    g_refs = refs[3 + count : 3 + 2 * count]
-    dk_ref, dv_ref, qall, gall = refs[3 + 2 * count :]
+    dk_ref, dv_ref, gqall = refs[3 + count :]
     length = len_ref[0]
     rows, feats = k_ref.shape
-    total = qall.shape[0]
+    total = gqall.shape[0]
     tile = min(total, 512)
-    store_blocks(qall, q_refs, lanes)
-    store_blocks(gall, g_refs, lanes)
+    store_blocks(gqall, refs[3 : 3 + count], lanes)
     pos = lax.axis_index("blk")
     mine = lax.rem(lax.broadcasted_iota(jnp.int32, (2 * rows, tile), 0), rows) + pos * rows
     query = lax.broadcasted_iota(jnp.int32, (2 * rows, tile), 1)
@@ -234,19 +233,21 @@
         lhs = two_heads(k_ref[:, cols] * BF16(HEAD ** -0.5 / 2))
         val = two_heads(v_ref[:, cols])
 
-        def step(t, carry, lhs=lhs, val=val, cols=cols):
+        q_cols = slice(feats + p * PAIR, feats + (p + 1) * PAIR)
+
+        def step(t, carry, lhs=lhs, val=val, cols=cols, q_cols=q_cols):
             dk, dv = carry
             at = pl.ds(pl.multiple_of(t * tile, tile), tile)
-            half = dot(lhs, qall[at, cols], NT)
-            prob_grad = dot(val, gall[at, cols], NT)
+            half = dot(lhs, gqall[at, q_cols], NT)
+            prob_grad = dot(val, gqall[at, cols], NT)
             where = query + t * tile
             live = (mine <= where) & (where < length)
             th = jnp.tanh(half)
             weight = jnp.where(live, half + half * th, 0.0)
             slope = (0.5 + 0.5 * th) * (1.0 + half * (1.0 - th))
             score_grad = jnp.where(live, prob_grad * slope, 0.0)
-            dk = dk + dot(score_grad.astype(BF16), qall[at, cols])
-            dv = dv + dot(weight.astype(BF16), gall[at, cols])
+            dk = dk + dot(score_grad.astype(BF16), gqall[at, q_cols])
+            dv = dv + dot(weight.astype(BF16), gqall[at, cols])
             return dk, dv
 
         zero = jnp.zeros((2 * rows, PAIR), F32)
@@ -344,15 +345,14 @@
     )
     moved = [over_blk(columns[k], lanes, k, 0) for k in steps]
     columns = cores([columns[0]] + moved)
-    queries = cores([query] + cross(query))
 
     attention_flops = 4 * rows * total * feats
-    mixed, mixed_t, att_grad, grad_gate, kall, vall = call(
+    mixed, mixed_t, grads_queries, grad_gate, kall, vall = call(
         functools.partial(forward_kernel, lanes),
         [
             ((rows, feats), BF16),
             ((feats, rows), BF16),
-            ((rows, feats), BF16),
+            ((rows, 2 * feats), BF16),
             ((rows, feats), BF16),
             ((total, feats), BF16),
             ((total, feats), BF16),
@@ -368,10 +368,8 @@
         scratch=[pltpu.VMEM((rows, feats), F32)],
         flops=attention_flops,
     )
-    mixes = [mixed_t]
-    for n in range(1, lanes):
-        mixes.append(over_blk(mixed_t, lanes, n // CORES, n % CORES))
-    grads = cores([att_grad] + cross(att_grad))
+    mixes = cores([mixed_t] + cross(mixed_t))
+    grads = cores([grads_queries] + cross(grads_queries))
 
     stages = digits(groups)
     size = feats
@@ -388,7 +386,7 @@
         query,
         kall,
         vall,
-        att_grad,
+        grads_queries,
         mixed,
         out_weight,
         scalars=1,
@@ -400,10 +398,9 @@
         lengths,
         key,
         value,
-        *queries,
         *grads,
         scalars=1,
-        scratch=[pltpu.VMEM((total, feats), BF16), pltpu.VMEM((total, feats), BF16)],
+        scratch=[pltpu.VMEM((total, 2 * feats), BF16)],
         flops=2 * attention_flops,
     )
 

time: 51.1 us -> 57 us (1.12)
  waiting for transfers between devices: 19.5 us -> 25.6 us
  starting transfers between devices: 18.9 us -> 18.2 us
  local copies, waits for them, and re-layouts: 2.2 us -> 2.87 us
    ppermute x18 -> x15, waiting for transfers between devices: 9.43 us -> 16.8 us  [over_blk(): return lax.ppermute(x, 'blk', pairs)]
    ppermute x18 -> x15, starting transfers between devices: 11 us -> 8.49 us  [over_blk(): return lax.ppermute(x, 'blk', pairs)]
    ppermute x4 -> x7, starting transfers between devices: 7.95 us -> 9.75 us  [over_digit(): return lax.ppermute(x, 'grp', pairs)]
    ppermute x4 -> x7, waiting for transfers between devices: 10.1 us -> 8.81 us  [over_digit(): return lax.ppermute(x, 'grp', pairs)]
    unnamed x16, local copies, waits for them, and re-layouts: 2.2 us -> 2.87 us
    pallas_call x9 -> x8, Pallas kernels: 8.76 us -> 8.71 us  [call(): pl.pallas_call(kernel, out_shape=[jax.ShapeDtypeStruct(s, d) for s, d in...]
  transfers between devices with their start and end apart: 22 -> 22, of which waited for: 8 -> 10; matrix products, arithmetic and copies ran while one was open for 0% -> 0% of each run, Pallas kernels for 15% -> 7%
where the time goes in v3:
time: 57 us; the launch traced here: 56.8 us
  waiting for transfers between devices  25.6 us (45%)
  starting transfers between devices  18.2 us (32%)
  Pallas kernels  8.71 us (15%)
  local copies, waits for them, and re-layouts  2.87 us (5%)
  between operations  1.39 us (2%)
    ppermute x15, waiting for transfers between devices, over_blk(): return lax.ppermute(x, 'blk', pairs)  16.8 us
    ppermute x7, starting transfers between devices, over_digit(): return lax.ppermute(x, 'grp', pairs)  9.75 us
    ppermute x7, waiting for transfers between devices, over_digit(): return lax.ppermute(x, 'grp', pairs)  8.81 us
    pallas_call x8, Pallas kernels, call(): pl.pallas_call(kernel, out_shape=[jax.ShapeDtypeStruct(s, d) for s, d in...  8.71 us
    ppermute x15, starting transfers between devices, over_blk(): return lax.ppermute(x, 'blk', pairs)  8.49 us
    unnamed x16, local copies, waits for them, and re-layouts  2.87 us
  transfers between devices with their start and end apart: 22, of which 10 were waited for; matrix products, arithmetic and copies ran while one was open for 0% of the time, Pallas kernels for 7%

profile of v3, /device:TPU:0, one launch (start us, length us, event | category | flops | bytes accessed | tf_op | source)
XLA Modules:
  0.0 56.8 jit_solution(11739058110091138426)
XLA Ops:
  0.6 3.0 %collective-permute-start.1 = (bf16[128,512]{1,0:T(8,128)(2,1)}, bf16[128,512]{1,0:T(8,128)(2,1)S(1)}, u32[]{:S(2)}, u32[]{:S(2)}) collective-permute-start(bf16[128,512]{1,0:T(8,128)(2,1)} %refs_1_.3), channel_id=1, source_target_pairs={{0,2},{1,3},{2,0},{3,1},{4,6},{5,7},{6,4},{7,5},{8,10},{9,11},{10,... | collective-permute-start | bytes 393224 | tf_op jit(solution)/shard_map/ppermute | solution.py:70
  3.7 0.5 collective-permute-start.3
  4.3 4.0 %collective-permute-done.1.refs_4_ = bf16[128,512]{1,0:T(8,128)(2,1)S(1)} collective-permute-done((bf16[128,512]{1,0:T(8,128)(2,1)}, bf16[128,512]{1,0:T(8,128)(2,1)S(1)}, u32[]{:S(2)}, u32[]{:S(2)}) %collective-permute-start.1) | collective-permute-done | bytes 131104 | tf_op jit(solution)/shard_map/ppermute | solution.py:70
  8.2 2.0 %collective-permute-done.4.refs_8_ = bf16[128,512]{1,0:T(8,128)(2,1)S(1)} collective-permute-done((bf16[128,512]{1,0:T(8,128)(2,1)}, bf16[128,512]{1,0:T(8,128)(2,1)S(1)}, u32[]{:S(2)}, u32[]{:S(2)}) %collective-permute-start.4) | collective-permute-done | bytes 131104 | tf_op jit(solution)/shard_map/ppermute | solution.py:70
  10.8 1.2 %copy-done = bf16[512,1024]{1,0:T(8,128)(2,1)S(1)} copy-done((bf16[512,1024]{1,0:T(8,128)(2,1)S(1)}, bf16[512,1024]{1,0:T(8,128)(2,1)}, u32[]{:S(2)}) %copy-start) | copy-done | bytes 1048600
  12.1 0.9 %copy-done.5 = bf16[128,1024]{1,0:T(8,128)(2,1)S(1)} copy-done((bf16[128,1024]{1,0:T(8,128)(2,1)S(1)}, bf16[128,1024]{1,0:T(8,128)(2,1)}, u32[]{:S(2)}) %copy-start.5) | copy-done | bytes 262168
  13.0 0.5 shard_map.127
  13.6 0.3 copy-done.2
  14.3 2.0 %shard_map.128 = (bf16[128,512]{1,0:T(8,128)(2,1)S(1)}, bf16[512,128]{1,0:T(8,128)(2,1)S(1)}, bf16[128,1024]{1,0:T(8,128)(2,1)S(1)}, bf16[128,512]{1,0:T(8,128)(...) custom-call(s32[1]{0:T(128)S(6)} %copy.14.refs_0_.len_ref, bf16[128,512]{1,0:T(8,128)(2,1)S(1)} %copy-done.2, ...), custom_call_target="tpu_custom_call" | custom-call | flops 134217728 | tf_op jit(solution)/shard_map/pallas_call | solution.py:37
  16.3 1.7 %collective-permute-start.7 = (bf16[128,1024]{1,0:T(8,128)(2,1)S(1)}, bf16[128,1024]{1,0:T(8,128)(2,1)S(1)}, u32[]{:S(2)}, u32[]{:S(2)}) collective-permute-start(bf16[128,1024]{1,0:T(8,128)(2,1)S(1)} %get-tuple-element.26.ag_ref.refs_3_), channel_id=1, source_target_pairs={{0,2},{1,3},{2,0},{3,1},{4,6},{5,7},{6,4},{7,5},{8,10},{9,11},{10,... | collective-permute-start | bytes 786440 | tf_op jit(solution)/shard_map/ppermute | solution.py:70
  18.0 0.3 collective-permute-start.13
  18.3 1.7 %collective-permute-start.10 = (bf16[512,128]{1,0:T(8,128)(2,1)S(1)}, bf16[512,128]{1,0:T(8,128)(2,1)S(1)}, u32[]{:S(2)}, u32[]{:S(2)}) collective-permute-start(bf16[512,128]{1,0:T(8,128)(2,1)S(1)} %get-tuple-element.33.refs_0_), channel_id=1, source_target_pairs={{0,2},{1,3},{2,0},{3,1},{4,6},{5,7},{6,4},{7,5},{8,10},{9,11},{10,... | collective-permute-start | bytes 393224 | tf_op jit(solution)/shard_map/ppermute | solution.py:70
  20.0 8.2 %collective-permute-done.13.refs_6_ = bf16[128,512]{1,0:T(8,128)(2,1)S(1)} collective-permute-done((bf16[128,512]{1,0:T(8,128)(2,1)S(1)}, bf16[128,512]{1,0:T(8,128)(2,1)S(1)}, u32[]{:S(2)}, u32[]{:S(2)}) %collective-permute-start.13) | collective-permute-done | bytes 131104 | tf_op jit(solution)/shard_map/ppermute | solution.py:70
  28.3 0.5 collective-permute-start.9
  28.8 1.8 %collective-permute-done.10.refs_2_ = bf16[512,128]{1,0:T(8,128)(2,1)S(1)} collective-permute-done((bf16[512,128]{1,0:T(8,128)(2,1)S(1)}, bf16[512,128]{1,0:T(8,128)(2,1)S(1)}, u32[]{:S(2)}, u32[]{:S(2)}) %collective-permute-start.10) | collective-permute-done | bytes 131104 | tf_op jit(solution)/shard_map/ppermute | solution.py:70
  30.6 0.5 collective-permute-start.6
  31.2 0.8 %collective-permute-done.11.refs_3_ = bf16[512,128]{1,0:T(8,128)(2,1)S(1)} collective-permute-done((bf16[512,128]{1,0:T(8,128)(2,1)S(1)}, bf16[512,128]{1,0:T(8,128)(2,1)S(1)}, u32[]{:S(2)}, u32[]{:S(2)}) %collective-permute-start.11) | collective-permute-done | bytes 131104 | tf_op jit(solution)/shard_map/ppermute | solution.py:70
  32.0 0.4 shard_map.131
  32.3 1.8 %collective-permute-start.15 = (bf16[128,256]{1,0:T(8,128)(2,1)S(1)}, bf16[128,256]{1,0:T(8,128)(2,1)S(1)}, u32[]{:S(2)}, u32[]{:S(2)}) collective-permute-start(bf16[128,256]{1,0:T(8,128)(2,1)S(1)} %get-tuple-element.37), channel_id=1, source_target_pairs={{0,4},{4,0},{8,12},{12,8},{16,20},{20,16},{24,28},{28,24},{1,5},{5... | collective-permute-start | bytes 196616 | tf_op jit(solution)/shard_map/ppermute | solution.py:90
  34.2 1.6 %collective-permute-start.16 = (bf16[128,256]{1,0:T(8,128)(2,1)S(1)}, bf16[128,256]{1,0:T(8,128)(2,1)S(1)}, u32[]{:S(2)}, u32[]{:S(2)}) collective-permute-start(bf16[128,256]{1,0:T(8,128)(2,1)S(1)} %get-tuple-element.38), channel_id=1, source_target_pairs={{0,8},{4,12},{8,0},{12,4},{16,24},{20,28},{24,16},{28,20},{1,9},{5... | collective-permute-start | bytes 196616 | tf_op jit(solution)/shard_map/ppermute | solution.py:90
  35.9 0.8 %collective-permute-done.15.refs_1_ = bf16[128,256]{1,0:T(8,128)(2,1)S(1)} collective-permute-done((bf16[128,256]{1,0:T(8,128)(2,1)S(1)}, bf16[128,256]{1,0:T(8,128)(2,1)S(1)}, u32[]{:S(2)}, u32[]{:S(2)}) %collective-permute-start.15) | collective-permute-done | bytes 65568 | tf_op jit(solution)/shard_map/ppermute | solution.py:90
  36.7 2.3 %collective-permute-done.16.refs_2_ = bf16[128,256]{1,0:T(8,128)(2,1)S(1)} collective-permute-done((bf16[128,256]{1,0:T(8,128)(2,1)S(1)}, bf16[128,256]{1,0:T(8,128)(2,1)S(1)}, u32[]{:S(2)}, u32[]{:S(2)}) %collective-permute-start.16) | collective-permute-done | bytes 65568 | tf_op jit(solution)/shard_map/ppermute | solution.py:90
  39.0 1.9 %collective-permute-done.17.refs_3_ = bf16[128,256]{1,0:T(8,128)(2,1)S(1)} collective-permute-done((bf16[128,256]{1,0:T(8,128)(2,1)S(1)}, bf16[128,256]{1,0:T(8,128)(2,1)S(1)}, u32[]{:S(2)}, u32[]{:S(2)}) %collective-permute-start.17) | collective-permute-done | bytes 65568 | tf_op jit(solution)/shard_map/ppermute | solution.py:90
  41.0 2.6 %collective-permute-start.18 = (bf16[128,256]{1,0:T(8,128)(2,1)S(1)}, bf16[128,256]{1,0:T(8,128)(2,1)S(1)}, u32[]{:S(2)}, u32[]{:S(2)}) collective-permute-start(bf16[128,256]{1,0:T(8,128)(2,1)S(1)} %shard_map.132.refs_0_), channel_id=1, source_target_pairs={{0,16},{4,20},{8,24},{12,28},{16,0},{20,4},{24,8},{28,12},{1,17},{... | collective-permute-start | bytes 196616 | tf_op jit(solution)/shard_map/ppermute | solution.py:90
  43.6 3.2 %collective-permute-done.18.refs_1_ = bf16[128,256]{1,0:T(8,128)(2,1)S(1)} collective-permute-done((bf16[128,256]{1,0:T(8,128)(2,1)S(1)}, bf16[128,256]{1,0:T(8,128)(2,1)S(1)}, u32[]{:S(2)}, u32[]{:S(2)}) %collective-permute-start.18) | collective-permute-done | bytes 65568 | tf_op jit(solution)/shard_map/ppermute | solution.py:90
  46.8 0.7 %collective-permute-start.19 = (bf16[128,256]{1,0:T(8,128)(2,1)S(1)}, bf16[128,256]{1,0:T(8,128)(2,1)S(1)}, u32[]{:S(2)}, u32[]{:S(2)}) collective-permute-start(bf16[128,256]{1,0:T(8,128)(2,1)S(1)} %shard_map.133.refs_0_), channel_id=1, source_target_pairs={{0,4},{4,0},{8,12},{12,8},{16,20},{20,16},{24,28},{28,24},{1,5},{5... | collective-permute-start | bytes 196616 | tf_op jit(solution)/shard_map/ppermute | solution.py:90
  47.5 0.5 collective-permute-start.20
  48.0 2.4 %collective-permute-start.21 = (bf16[128,256]{1,0:T(8,128)(2,1)S(1)}, bf16[128,256]{1,0:T(8,128)(2,1)S(1)}, u32[]{:S(2)}, u32[]{:S(2)}) collective-permute-start(bf16[128,256]{1,0:T(8,128)(2,1)S(1)} %shard_map.133.refs_0_), channel_id=1, source_target_pairs={{0,12},{4,8},{8,4},{12,0},{16,28},{20,24},{24,20},{28,16},{1,13},{... | collective-permute-start | bytes 196616 | tf_op jit(solution)/shard_map/ppermute | solution.py:90
  50.4 2.3 %shard_map.129 = (bf16[128,1024]{1,0:T(8,128)(2,1)}, bf16[128,512]{1,0:T(8,128)(2,1)}) custom-call(s32[1]{0:T(128)S(6)} %copy.14.refs_0_.len_ref, bf16[128,512]{1,0:T(8,128)(2,1)S(1)} %copy-done.2, bf16[512,512]{1,0:T(8,128)(2,1)S(1)} %get-tuple-element.24.kall, bf16[512,512]{1,0:T(8,128)(2,1)S(1)} %get-tuple-element.25.vall, ...), custom_call_target="tpu_custom_call" | custom-call | flops 134217728 | tf_op jit(solution)/shard_map/pallas_call | solution.py:37
  52.7 0.6 %collective-permute-done.21.refs_3_ = bf16[128,256]{1,0:T(8,128)(2,1)S(1)} collective-permute-done((bf16[128,256]{1,0:T(8,128)(2,1)S(1)}, bf16[128,256]{1,0:T(8,128)(2,1)S(1)}, u32[]{:S(2)}, u32[]{:S(2)}) %collective-permute-start.21) | collective-permute-done | bytes 65568 | tf_op jit(solution)/shard_map/ppermute | solution.py:90
  53.3 0.8 %shard_map.134 = f32[512,256]{1,0:T(8,128)} custom-call(bf16[128,256]{1,0:T(8,128)(2,1)S(1)} %shard_map.133.refs_0_, bf16[128,256]{1,0:T(8,128)(2,1)S(1)} %collective-permute-done.19.refs_1_, bf16[128,256]{1,0:T(8,128)(2,1)S(1)} %collective-permute-done.20.refs_2_, bf16[128,256]{1,0:T(8,128)(2,1)S(1)} %collective-permute-done.21.refs_3_), custom_call_target="tpu_custom_call" | custom-call | tf_op jit(solution)/shard_map/pallas_call | solution.py:37
  54.1 2.6 %shard_map.130 = (bf16[128,512]{1,0:T(8,128)(2,1)}, bf16[128,512]{1,0:T(8,128)(2,1)}) custom-call(s32[1]{0:T(128)S(6)} %copy.14.refs_0_.len_ref, bf16[128,512]{1,0:T(8,128)(2,1)S(1)} %copy-done.3, bf16[128,512]{1,0:T(8,128)(2,1)S(1)} %copy-done.4, bf16[128,1024]{1,0:T(8,128)(2,1)S(1)} %get-tuple-element.26.ag_ref.refs_3_, ...), custom_call_target="tpu_custom_call" | custom-call | flops 268435456 | tf_op jit(solution)/shard_map/pallas_call | solution.py:37
  (36 shorter events, 0.8 us)
Async XLA Ops:
  0.6 7.6 %collective-permute-start.1 = (bf16[128,512]{1,0:T(8,128)(2,1)}, bf16[128,512]{1,0:T(8,128)(2,1)S(1)}, u32[]{:S(2)}, u32[]{:S(2)}) collective-permute-start(bf16[128,512]{1,0:T(8,128)(2,1)} %refs_1_.3), channel_id=1, source_target_pairs={{0,2},{1,3},{2,0},{3,1},{4,6},{5,7},{6,4},{7,5},{8,10},{9,11},{10,... | collective-permute-start | bytes 393224 | tf_op jit(solution)/shard_map/ppermute | solution.py:70
  3.7 6.5 %collective-permute-start.4 = (bf16[128,512]{1,0:T(8,128)(2,1)}, bf16[128,512]{1,0:T(8,128)(2,1)S(1)}, u32[]{:S(2)}, u32[]{:S(2)}) collective-permute-start(bf16[128,512]{1,0:T(8,128)(2,1)} %refs_2_.3), channel_id=1, source_target_pairs={{0,2},{1,3},{2,0},{3,1},{4,6},{5,7},{6,4},{7,5},{8,10},{9,11},{10,... | collective-permute-start | bytes 393224 | tf_op jit(solution)/shard_map/ppermute | solution.py:70
  3.7 9.8 %collective-permute-start = (bf16[128,512]{1,0:T(8,128)(2,1)}, bf16[128,512]{1,0:T(8,128)(2,1)S(1)}, u32[]{:S(2)}, u32[]{:S(2)}) collective-permute-start(bf16[128,512]{1,0:T(8,128)(2,1)} %refs_1_.3), channel_id=1, source_target_pairs={{0,1},{1,0},{2,3},{3,2},{4,5},{5,4},{6,7},{7,6},{8,9},{9,8},{10,11... | collective-permute-start | bytes 393224 | tf_op jit(solution)/shard_map/ppermute | solution.py:70
  3.7 9.8 %collective-permute-start.3 = (bf16[128,512]{1,0:T(8,128)(2,1)}, bf16[128,512]{1,0:T(8,128)(2,1)S(1)}, u32[]{:S(2)}, u32[]{:S(2)}) collective-permute-start(bf16[128,512]{1,0:T(8,128)(2,1)} %refs_2_.3), channel_id=1, source_target_pairs={{0,1},{1,0},{2,3},{3,2},{4,5},{5,4},{6,7},{7,6},{8,9},{9,8},{10,11... | collective-permute-start | bytes 393224 | tf_op jit(solution)/shard_map/ppermute | solution.py:70
  8.2 5.3 %collective-permute-start.2 = (bf16[128,512]{1,0:T(8,128)(2,1)S(1)}, bf16[128,512]{1,0:T(8,128)(2,1)S(1)}, u32[]{:S(2)}, u32[]{:S(2)}) collective-permute-start(bf16[128,512]{1,0:T(8,128)(2,1)S(1)} %collective-permute-done.1.refs_4_), channel_id=1, source_target_pairs={{0,1},{1,0},{2,3},{3,2},{4,5},{5,4},{6,7},{7,6},{8,9},{9,8},{10,11... | collective-permute-start | bytes 393224 | tf_op jit(solution)/shard_map/ppermute | solution.py:70
  10.2 3.4 %collective-permute-start.5 = (bf16[128,512]{1,0:T(8,128)(2,1)S(1)}, bf16[128,512]{1,0:T(8,128)(2,1)S(1)}, u32[]{:S(2)}, u32[]{:S(2)}) collective-permute-start(bf16[128,512]{1,0:T(8,128)(2,1)S(1)} %collective-permute-done.4.refs_8_), channel_id=1, source_target_pairs={{0,1},{1,0},{2,3},{3,2},{4,5},{5,4},{6,7},{7,6},{8,9},{9,8},{10,11... | collective-permute-start | bytes 393224 | tf_op jit(solution)/shard_map/ppermute | solution.py:70
  10.8 1.2 %copy-start = (bf16[512,1024]{1,0:T(8,128)(2,1)S(1)}, bf16[512,1024]{1,0:T(8,128)(2,1)}, u32[]{:S(2)}) copy-start(bf16[512,1024]{1,0:T(8,128)(2,1)} %w_ref.3) | copy-start | bytes 3145732
  12.1 0.9 %copy-start.5 = (bf16[128,1024]{1,0:T(8,128)(2,1)S(1)}, bf16[128,1024]{1,0:T(8,128)(2,1)}, u32[]{:S(2)}) copy-start(bf16[128,1024]{1,0:T(8,128)(2,1)} %og_ref.1) | copy-start | bytes 786436
  13.0 0.9 %copy-start.2 = (bf16[128,512]{1,0:T(8,128)(2,1)S(1)}, bf16[128,512]{1,0:T(8,128)(2,1)}, u32[]{:S(2)}) copy-start(bf16[128,512]{1,0:T(8,128)(2,1)} %q_ref.1) | copy-start | bytes 393220
  13.0 1.0 %copy-start.3 = (bf16[128,512]{1,0:T(8,128)(2,1)S(1)}, bf16[128,512]{1,0:T(8,128)(2,1)}, u32[]{:S(2)}) copy-start(bf16[128,512]{1,0:T(8,128)(2,1)} %refs_1_.3) | copy-start | bytes 393220
  13.0 1.0 %copy-start.4 = (bf16[128,512]{1,0:T(8,128)(2,1)S(1)}, bf16[128,512]{1,0:T(8,128)(2,1)}, u32[]{:S(2)}) copy-start(bf16[128,512]{1,0:T(8,128)(2,1)} %refs_2_.3) | copy-start | bytes 393220
  13.0 1.1 %copy-start.6 = (bf16[128,512]{1,0:T(8,128)(2,1)S(1)}, bf16[128,512]{1,0:T(8,128)(2,1)}, u32[]{:S(2)}) copy-start(bf16[128,512]{1,0:T(8,128)(2,1)} %refs_10_.1) | copy-start | bytes 393220
  13.5 0.7 %copy-start.7 = (f32[512]{0:T(512)S(1)}, f32[512]{0:T(512)}, u32[]{:S(2)}) copy-start(f32[512]{0:T(512)} %param.14) | copy-start | bytes 6148
  16.3 34.1 %copy-start.1 = (bf16[512,1024]{1,0:T(8,128)(2,1)S(1)}, bf16[512,1024]{1,0:T(8,128)(2,1)}, u32[]{:S(2)}) copy-start(bf16[512,1024]{1,0:T(8,128)(2,1)} %w_ref.3) | copy-start | bytes 3145732
  16.3 14.9 %collective-permute-start.7 = (bf16[128,1024]{1,0:T(8,128)(2,1)S(1)}, bf16[128,1024]{1,0:T(8,128)(2,1)S(1)}, u32[]{:S(2)}, u32[]{:S(2)}) collective-permute-start(bf16[128,1024]{1,0:T(8,128)(2,1)S(1)} %get-tuple-element.26.ag_ref.refs_3_), channel_id=1, source_target_pairs={{0,2},{1,3},{2,0},{3,1},{4,6},{5,7},{6,4},{7,5},{8,10},{9,11},{10,... | collective-permute-start | bytes 786440 | tf_op jit(solution)/shard_map/ppermute | solution.py:70
  18.0 10.2 %collective-permute-start.13 = (bf16[128,512]{1,0:T(8,128)(2,1)S(1)}, bf16[128,512]{1,0:T(8,128)(2,1)S(1)}, u32[]{:S(2)}, u32[]{:S(2)}) collective-permute-start(bf16[128,512]{1,0:T(8,128)(2,1)S(1)} %get-tuple-element.35), channel_id=1, source_target_pairs={{0,2},{1,3},{2,0},{3,1},{4,6},{5,7},{6,4},{7,5},{8,10},{9,11},{10,... | collective-permute-start | bytes 393224 | tf_op jit(solution)/shard_map/ppermute | solution.py:70
  18.3 12.3 %collective-permute-start.10 = (bf16[512,128]{1,0:T(8,128)(2,1)S(1)}, bf16[512,128]{1,0:T(8,128)(2,1)S(1)}, u32[]{:S(2)}, u32[]{:S(2)}) collective-permute-start(bf16[512,128]{1,0:T(8,128)(2,1)S(1)} %get-tuple-element.33.refs_0_), channel_id=1, source_target_pairs={{0,2},{1,3},{2,0},{3,1},{4,6},{5,7},{6,4},{7,5},{8,10},{9,11},{10,... | collective-permute-start | bytes 393224 | tf_op jit(solution)/shard_map/ppermute | solution.py:70
  20.0 10.6 %collective-permute-start.12 = (bf16[128,512]{1,0:T(8,128)(2,1)S(1)}, bf16[128,512]{1,0:T(8,128)(2,1)S(1)}, u32[]{:S(2)}, u32[]{:S(2)}) collective-permute-start(bf16[128,512]{1,0:T(8,128)(2,1)S(1)} %get-tuple-element.34.refs_4_), channel_id=1, source_target_pairs={{0,1},{1,0},{2,3},{3,2},{4,5},{5,4},{6,7},{7,6},{8,9},{9,8},{10,11... | collective-permute-start | bytes 393224 | tf_op jit(solution)/shard_map/ppermute | solution.py:70
  28.3 2.9 %collective-permute-start.14 = (bf16[128,512]{1,0:T(8,128)(2,1)S(1)}, bf16[128,512]{1,0:T(8,128)(2,1)S(1)}, u32[]{:S(2)}, u32[]{:S(2)}) collective-permute-start(bf16[128,512]{1,0:T(8,128)(2,1)S(1)} %collective-permute-done.13.refs_6_), channel_id=1, source_target_pairs={{0,1},{1,0},{2,3},{3,2},{4,5},{5,4},{6,7},{7,6},{8,9},{9,8},{10,11... | collective-permute-start | bytes 393224 | tf_op jit(solution)/shard_map/ppermute | solution.py:70
  28.3 2.9 %collective-permute-start.9 = (bf16[512,128]{1,0:T(8,128)(2,1)S(1)}, bf16[512,128]{1,0:T(8,128)(2,1)S(1)}, u32[]{:S(2)}, u32[]{:S(2)}) collective-permute-start(bf16[512,128]{1,0:T(8,128)(2,1)S(1)} %get-tuple-element.33.refs_0_), channel_id=1, source_target_pairs={{0,1},{1,0},{2,3},{3,2},{4,5},{5,4},{6,7},{7,6},{8,9},{9,8},{10,11... | collective-permute-start | bytes 393224 | tf_op jit(solution)/shard_map/ppermute | solution.py:70
  30.6 1.3 %collective-permute-start.11 = (bf16[512,128]{1,0:T(8,128)(2,1)S(1)}, bf16[512,128]{1,0:T(8,128)(2,1)S(1)}, u32[]{:S(2)}, u32[]{:S(2)}) collective-permute-start(bf16[512,128]{1,0:T(8,128)(2,1)S(1)} %collective-permute-done.10.refs_2_), channel_id=1, source_target_pairs={{0,1},{1,0},{2,3},{3,2},{4,5},{5,4},{6,7},{7,6},{8,9},{9,8},{10,11... | collective-permute-start | bytes 393224 | tf_op jit(solution)/shard_map/ppermute | solution.py:70
  30.6 23.5 %collective-permute-start.6 = (bf16[128,1024]{1,0:T(8,128)(2,1)S(1)}, bf16[128,1024]{1,0:T(8,128)(2,1)S(1)}, u32[]{:S(2)}, u32[]{:S(2)}) collective-permute-start(bf16[128,1024]{1,0:T(8,128)(2,1)S(1)} %get-tuple-element.26.ag_ref.refs_3_), channel_id=1, source_target_pairs={{0,1},{1,0},{2,3},{3,2},{4,5},{5,4},{6,7},{7,6},{8,9},{9,8},{10,11... | collective-permute-start | bytes 786440 | tf_op jit(solution)/shard_map/ppermute | solution.py:70
  31.1 23.0 %collective-permute-start.8 = (bf16[128,1024]{1,0:T(8,128)(2,1)S(1)}, bf16[128,1024]{1,0:T(8,128)(2,1)S(1)}, u32[]{:S(2)}, u32[]{:S(2)}) collective-permute-start(bf16[128,1024]{1,0:T(8,128)(2,1)S(1)} %collective-permute-done.7.refs_5_), channel_id=1, source_target_pairs={{0,1},{1,0},{2,3},{3,2},{4,5},{5,4},{6,7},{7,6},{8,9},{9,8},{10,11... | collective-permute-start | bytes 786440 | tf_op jit(solution)/shard_map/ppermute | solution.py:70
  32.3 4.3 %collective-permute-start.15 = (bf16[128,256]{1,0:T(8,128)(2,1)S(1)}, bf16[128,256]{1,0:T(8,128)(2,1)S(1)}, u32[]{:S(2)}, u32[]{:S(2)}) collective-permute-start(bf16[128,256]{1,0:T(8,128)(2,1)S(1)} %get-tuple-element.37), channel_id=1, source_target_pairs={{0,4},{4,0},{8,12},{12,8},{16,20},{20,16},{24,28},{28,24},{1,5},{5... | collective-permute-start | bytes 196616 | tf_op jit(solution)/shard_map/ppermute | solution.py:90
  34.2 4.8 %collective-permute-start.16 = (bf16[128,256]{1,0:T(8,128)(2,1)S(1)}, bf16[128,256]{1,0:T(8,128)(2,1)S(1)}, u32[]{:S(2)}, u32[]{:S(2)}) collective-permute-start(bf16[128,256]{1,0:T(8,128)(2,1)S(1)} %get-tuple-element.38), channel_id=1, source_target_pairs={{0,8},{4,12},{8,0},{12,4},{16,24},{20,28},{24,16},{28,20},{1,9},{5... | collective-permute-start | bytes 196616 | tf_op jit(solution)/shard_map/ppermute | solution.py:90
  35.8 5.2 %collective-permute-start.17 = (bf16[128,256]{1,0:T(8,128)(2,1)S(1)}, bf16[128,256]{1,0:T(8,128)(2,1)S(1)}, u32[]{:S(2)}, u32[]{:S(2)}) collective-permute-start(bf16[128,256]{1,0:T(8,128)(2,1)S(1)} %get-tuple-element.39), channel_id=1, source_target_pairs={{0,12},{4,8},{8,4},{12,0},{16,28},{20,24},{24,20},{28,16},{1,13},{... | collective-permute-start | bytes 196616 | tf_op jit(solution)/shard_map/ppermute | solution.py:90
  41.0 5.8 %collective-permute-start.18 = (bf16[128,256]{1,0:T(8,128)(2,1)S(1)}, bf16[128,256]{1,0:T(8,128)(2,1)S(1)}, u32[]{:S(2)}, u32[]{:S(2)}) collective-permute-start(bf16[128,256]{1,0:T(8,128)(2,1)S(1)} %shard_map.132.refs_0_), channel_id=1, source_target_pairs={{0,16},{4,20},{8,24},{12,28},{16,0},{20,4},{24,8},{28,12},{1,17},{... | collective-permute-start | bytes 196616 | tf_op jit(solution)/shard_map/ppermute | solution.py:90
  46.8 5.9 %collective-permute-start.19 = (bf16[128,256]{1,0:T(8,128)(2,1)S(1)}, bf16[128,256]{1,0:T(8,128)(2,1)S(1)}, u32[]{:S(2)}, u32[]{:S(2)}) collective-permute-start(bf16[128,256]{1,0:T(8,128)(2,1)S(1)} %shard_map.133.refs_0_), channel_id=1, source_target_pairs={{0,4},{4,0},{8,12},{12,8},{16,20},{20,16},{24,28},{28,24},{1,5},{5... | collective-permute-start | bytes 196616 | tf_op jit(solution)/shard_map/ppermute | solution.py:90
  47.5 5.2 %collective-permute-start.20 = (bf16[128,256]{1,0:T(8,128)(2,1)S(1)}, bf16[128,256]{1,0:T(8,128)(2,1)S(1)}, u32[]{:S(2)}, u32[]{:S(2)}) collective-permute-start(bf16[128,256]{1,0:T(8,128)(2,1)S(1)} %shard_map.133.refs_0_), channel_id=1, source_target_pairs={{0,8},{4,12},{8,0},{12,4},{16,24},{20,28},{24,16},{28,20},{1,9},{5... | collective-permute-start | bytes 196616 | tf_op jit(solution)/shard_map/ppermute | solution.py:90
  48.0 5.3 %collective-permute-start.21 = (bf16[128,256]{1,0:T(8,128)(2,1)S(1)}, bf16[128,256]{1,0:T(8,128)(2,1)S(1)}, u32[]{:S(2)}, u32[]{:S(2)}) collective-permute-start(bf16[128,256]{1,0:T(8,128)(2,1)S(1)} %shard_map.133.refs_0_), channel_id=1, source_target_pairs={{0,12},{4,8},{8,4},{12,0},{16,28},{20,24},{24,20},{28,16},{1,13},{... | collective-permute-start | bytes 196616 | tf_op jit(solution)/shard_map/ppermute | solution.py:90

commit v4 on v3

v4 whole, which is shorter than its diff:
```python
import functools
import math

import jax
import jax.numpy as jnp
from jax import lax
from jax.experimental import pallas as pl
from jax.experimental.pallas import tpu as pltpu
from jax.sharding import PartitionSpec as P


HEAD = 64
PAIR = 2 * HEAD
EPS = 1e-05
F32 = jnp.float32
BF16 = jnp.bfloat16
CORES = 2
WORK_BYTES = 8 << 20

NT = (((1,), (1,)), ((), ()))
NN = (((1,), (0,)), ((), ()))


def dot(a, b, dims=NN):
    return lax.dot_general(a, b, dims, preferred_element_type=F32)


def nbytes(shape, dtype):
    return math.prod(shape) * jnp.dtype(dtype).itemsize


def call(kernel, outs, *args, scalars=0, scratch=(), flops=0, space=pltpu.VMEM):
    smem = pl.BlockSpec(memory_space=pltpu.SMEM)
    vmem = pl.BlockSpec(memory_space=pltpu.VMEM)
    inputs = pl.BlockSpec(memory_space=space)
    held = sum(nbytes(x.shape, x.dtype) for x in args) + sum(nbytes(*o) for o in outs)
    held += sum(nbytes(x.shape, x.dtype) for x in scratch if x.memory_space == pltpu.VMEM)
    return pl.pallas_call(
        kernel,
        out_shape=[jax.ShapeDtypeStruct(s, d) for s, d in outs],
        in_specs=[smem] * scalars + [inputs] * (len(args) - scalars),
        out_specs=[vmem] * len(outs),
        scratch_shapes=list(scratch),
        cost_estimate=pl.CostEstimate(flops=flops, transcendentals=0, bytes_accessed=0),
        compiler_params=pltpu.CompilerParams(vmem_limit_bytes=held + WORK_BYTES),
    )(*args)


def is_pow2(size):
    return size & (size - 1) == 0


def target(index, k, size):
    if is_pow2(size):
        return index ^ k
    return (index + k) % size if isinstance(index, int) else lax.rem(index + k, size)


def source(index, k, size):
    if is_pow2(size):
        return index ^ k
    return (index - k) % size if isinstance(index, int) else lax.rem(index + size - k, size)


def over_blk(x, lanes, step, other):
    chips = lanes // CORES
    pairs = []
    for i in range(lanes):
        chip, core = divmod(i, CORES)
        pairs.append((i, target(chip, step, chips) * CORES + (core + other) % CORES))
    return lax.ppermute(x, "blk", pairs)


def digits(groups):
    out, stride = [], 1
    for size in [4] + [2] * groups:
        if groups // stride % size == 0:
            out.append((stride, size))
            stride *= size
    if groups // stride > 1:
        out.append((stride, groups // stride))
    return out


def over_digit(x, groups, digit, k):
    stride, size = digit
    pairs = []
    for i in range(groups):
        d = (i // stride) % size
        pairs.append((i, i + (target(d, k, size) - d) * stride))
    return lax.ppermute(x, "grp", pairs)


def digit_of(digit):
    stride, size = digit
    return lax.rem(lax.div(lax.axis_index("grp"), jnp.int32(stride)), jnp.int32(size))


def low_lanes(shape):
    return lax.broadcasted_iota(jnp.int32, shape, 1) < HEAD


def two_heads(x):
    low = low_lanes(x.shape)
    zero = jnp.zeros_like(x)
    return jnp.concatenate([jnp.where(low, x, zero), jnp.where(low, zero, x)], axis=0)


def one_pair(x):
    rows = x.shape[0] // 2
    top, bottom = x[:rows], x[rows:]
    return jnp.where(low_lanes(top.shape), top, bottom)


def block_at(n, lanes):
    chips = lanes // CORES
    pos = lax.axis_index("blk")
    chip, core = lax.div(pos, CORES), lax.rem(pos, CORES)
    return source(chip, n // CORES, chips) * CORES + lax.rem(core + n % CORES, CORES)


def tiles(blocks, size=4):
    return [blocks[n : n + size] for n in range(0, len(blocks), size)]


def places(blocks, lanes, rows):
    lane = lax.broadcasted_iota(jnp.int32, (1, rows), 1)
    return jnp.concatenate([block_at(n, lanes) * rows + lane for n in blocks], axis=1)


def limits(length, rows):
    pos = lax.axis_index("blk")
    local = lax.rem(lax.broadcasted_iota(jnp.int32, (CORES * rows, 1), 0), rows)
    row = local + pos * rows
    return jnp.where(row < length, row, -1)


def stack(refs, blocks, cols):
    return jnp.concatenate([refs[n][:, cols] for n in blocks], axis=0)


def pair_slices(feats):
    return [slice(p * PAIR, (p + 1) * PAIR) for p in range(feats // PAIR)]


HALF_SCALE = HEAD ** -0.5 / 2


def fetch_kernel(chips, og_ref, *refs):
    count = (len(refs) - chips - 1) // 2
    sources, outs, sem = list(refs[:count]), refs[count:-1], refs[-1]
    chip = lax.div(lax.axis_index("blk"), CORES)
    width = outs[-1].shape[1]
    for k in range(chips):
        at = pl.multiple_of(target(chip, k, chips) * width, width)
        sources.append(og_ref.at[:, pl.ds(at, width)])
    copies = [
        pltpu.make_async_copy(src, dst, sem.at[n]) for n, (src, dst) in enumerate(zip(sources, outs))
    ]
    for copy in copies:
        copy.start()
    for copy in copies:
        copy.wait()


def attend(lanes, length, q_ref, k_refs, v_refs, blocks, cols):
    rows = q_ref.shape[0]
    lhs = two_heads(q_ref[:, cols] * BF16(HALF_SCALE))
    limit = limits(length, rows)
    acc = None
    for some in tiles(blocks):
        half = dot(lhs, stack(k_refs, some, cols), NT)
        live = places(some, lanes, rows) <= limit
        weight = jnp.where(live, half + half * jnp.tanh(half), 0.0).astype(BF16)
        part = dot(weight, stack(v_refs, some, cols))
        acc = part if acc is None else acc + part
    return one_pair(acc)


def partial_kernel(lanes, blocks, *refs):
    len_ref, q_ref = refs[:2]
    k_refs = dict(zip(blocks, refs[2 : 2 + len(blocks)]))
    v_refs = dict(zip(blocks, refs[2 + len(blocks) :]))
    before, out_ref = refs[2 + 2 * len(blocks) : -1], refs[-1]
    length = len_ref[0]
    for cols in pair_slices(q_ref.shape[1]):
        part = attend(lanes, length, q_ref, k_refs, v_refs, blocks, cols)
        for ref in before:
            part = part + ref[:, cols]
        out_ref[:, cols] = part


def forward_kernel(lanes, blocks, *refs):
    len_ref, q_ref = refs[:2]
    count = len(blocks)
    k_refs = dict(zip(blocks, refs[2 : 2 + count]))
    v_refs = dict(zip(blocks, refs[2 + count :]))
    near_ref, gate_ref, gain_ref = refs[2 + 2 * count : 5 + 2 * count]
    mixed_ref, mixed_t_ref, normed_ref, inv_ref, att = refs[5 + 2 * count :]
    length = len_ref[0]
    for cols in pair_slices(q_ref.shape[1]):
        att[:, cols] = near_ref[:, cols] + attend(
            lanes, length, q_ref, k_refs, v_refs, blocks, cols
        )
    attended = att[...]
    centre = attended - jnp.mean(attended, axis=1, keepdims=True)
    inv_std = lax.rsqrt(jnp.mean(centre * centre, axis=1, keepdims=True) + EPS)
    normed = centre * inv_std
    mixed = (normed * gain_ref[...] * gate_ref[...].astype(F32)).astype(BF16)
    mixed_t_ref[...] = mixed.T
    mixed_ref[...] = mixed
    normed_ref[...] = normed
    inv_ref[...] = jnp.broadcast_to(inv_std, inv_ref.shape)


def query_kernel(lanes, *refs):
    len_ref, q_ref = refs[:2]
    k_refs, v_refs = refs[2 : 2 + lanes], refs[2 + lanes : 2 + 2 * lanes]
    gate_ref, gain_ref, og_ref, normed_ref, inv_ref, mixed_ref, w_ref = refs[2 + 2 * lanes : 9 + 2 * lanes]
    lo_ref, dq_ref, gg_ref, gq_ref = refs[9 + 2 * lanes :]
    length = len_ref[0]
    rows, feats = q_ref.shape
    gain = gain_ref[...]
    normed = normed_ref[...]
    mixed_grad = dot(og_ref[...], w_ref[...], NT)
    gg_ref[...] = (mixed_grad * (normed * gain)).astype(BF16)
    normed_grad = mixed_grad * gate_ref[...].astype(F32) * gain
    grad = inv_ref[:, :1] * (
        normed_grad
        - jnp.mean(normed_grad, axis=1, keepdims=True)
        - normed * jnp.mean(normed_grad * normed, axis=1, keepdims=True)
    )
    gq_ref[:, :feats] = grad.astype(BF16)
    gq_ref[:, feats:] = q_ref[...]
    lo_ref[...] = dot(mixed_ref[...], w_ref[...]).astype(BF16)
    limit = limits(length, rows)
    for cols in pair_slices(feats):
        lhs = two_heads(q_ref[:, cols] * BF16(HALF_SCALE))
        grads = two_heads(gq_ref[:, cols])
        acc = None
        for blocks in tiles(range(lanes)):
            keys = stack(k_refs, blocks, cols)
            half = dot(lhs, keys, NT)
            prob_grad = dot(grads, stack(v_refs, blocks, cols), NT)
            th = jnp.tanh(half)
            slope = (0.5 + 0.5 * th) * (1.0 + half * (1.0 - th))
            live = places(blocks, lanes, rows) <= limit
            score_grad = jnp.where(live, prob_grad * slope, 0.0).astype(BF16)
            part = dot(score_grad, keys)
            acc = part if acc is None else acc + part
        dq_ref[:, cols] = (one_pair(acc) * HEAD ** -0.5).astype(BF16)


def key_kernel(lanes, *refs):
    len_ref, k_ref, v_ref = refs[:3]
    gq_refs = refs[3 : 3 + lanes]
    dk_ref, dv_ref = refs[3 + lanes :]
    length = len_ref[0]
    rows, feats = k_ref.shape
    pos = lax.axis_index("blk")
    mine = lax.rem(lax.broadcasted_iota(jnp.int32, (CORES * rows, 1), 0), rows) + pos * rows
    for p, cols in enumerate(pair_slices(feats)):
        lhs = two_heads(k_ref[:, cols] * BF16(HALF_SCALE))
        val = two_heads(v_ref[:, cols])
        q_cols = slice(feats + p * PAIR, feats + (p + 1) * PAIR)
        dk = dv = None
        for blocks in tiles(range(lanes)):
            queries = stack(gq_refs, blocks, q_cols)
            grads = stack(gq_refs, blocks, cols)
            half = dot(lhs, queries, NT)
            prob_grad = dot(val, grads, NT)
            where = places(blocks, lanes, rows)
            where = jnp.where(where < length, where, -1)
            live = mine <= where
            th = jnp.tanh(half)
            weight = jnp.where(live, half + half * th, 0.0).astype(BF16)
            slope = (0.5 + 0.5 * th) * (1.0 + half * (1.0 - th))
            score_grad = jnp.where(live, prob_grad * slope, 0.0).astype(BF16)
            part_k, part_v = dot(score_grad, queries), dot(weight, grads)
            dk = part_k if dk is None else dk + part_k
            dv = part_v if dv is None else dv + part_v
        dk_ref[:, cols] = (one_pair(dk) * HEAD ** -0.5).astype(BF16)
        dv_ref[:, cols] = one_pair(dv).astype(BF16)


def split(total_ref, digit, keep_ref, send_refs):
    size = 1 + len(send_refs)
    part = keep_ref.shape[0]
    mine = digit_of(digit)
    keep_ref[...] = total_ref[pl.ds(pl.multiple_of(mine * part, part), part), :]
    for k, ref in enumerate(send_refs, 1):
        at = target(mine, k, size)
        ref[...] = total_ref[pl.ds(pl.multiple_of(at * part, part), part), :].astype(BF16)


def product_kernel(lanes, digit, *refs):
    m_refs, o_refs = refs[:lanes], refs[lanes : 2 * lanes]
    outs, acc = refs[2 * lanes : -1], refs[-1]
    width = acc.shape[1]
    first = lax.rem(lax.axis_index("blk"), CORES) == 0
    total = None
    for n in range(0, lanes, CORES):
        lhs = jnp.concatenate([m[...] for m in m_refs[n : n + CORES]], axis=1)
        rhs = jnp.concatenate([o[...] for o in o_refs[n : n + CORES]], axis=0)
        rhs = jnp.where(first, rhs[:, :width], rhs[:, width:])
        part = dot(lhs, rhs)
        total = part if total is None else total + part
    acc[...] = total
    split(acc, digit, outs[0], outs[1:])


def sum_split_kernel(count, whole, digit, *refs):
    outs, acc = refs[1 + count : -1], refs[-1]
    if whole is None:
        total = refs[0][...]
        for ref in refs[1 : 1 + count]:
            total = total + ref[...].astype(F32)
    else:
        mine, size = digit_of(whole), whole[1]
        rows = refs[0].shape[0]
        for k, ref in enumerate(refs[: 1 + count]):
            at = source(mine, k, size) * rows
            acc[pl.ds(pl.multiple_of(at, rows), rows), :] = ref[...].astype(F32)
        total = acc[:rows, :]
        for k in range(1, size):
            total = total + acc[k * rows : (k + 1) * rows, :]
        acc = acc.at[:rows, :]
    acc[...] = total
    if digit is None:
        outs[0][...] = total.astype(outs[0].dtype)
    else:
        split(acc, digit, outs[0], outs[1:])


def join_kernel(digit, *refs):
    parts, out = refs[:-1], refs[-1]
    size, part = len(parts), parts[0].shape[0]
    mine = digit_of(digit)
    for k, ref in enumerate(parts):
        at = source(mine, k, size)
        out[pl.ds(pl.multiple_of(at * part, part), part), :] = ref[...].astype(out.dtype)


def layer(query, key, value, gate_u, out_grad, lengths, norm_gain, out_weight):
    rows, feats = query.shape
    model = out_grad.shape[1]
    lanes = lax.axis_size("blk")
    groups = lax.axis_size("grp")
    chips = lanes // CORES
    total = rows * lanes
    width = model // lanes
    steps = range(1, chips)

    def cross(x):
        return [over_blk(x, lanes, k, 0) for k in steps]

    def cores(pieces):
        out = []
        for x in pieces:
            out += [x, over_blk(x, lanes, 0, 1)]
        return out

    keys = cores([key] + cross(key))
    values = cores([value] + cross(value))
    query_here, key_here, value_here, gates, *columns = call(
        functools.partial(fetch_kernel, chips),
        [((rows, feats), BF16)] * 4 + [((rows, model // chips), BF16)] * chips,
        *(pltpu.with_memory_space_constraint(x, pltpu.HBM) for x in (out_grad, query, key, value, gate_u)),
        scratch=[pltpu.SemaphoreType.DMA((4 + chips,))],
        space=pltpu.HBM,
    )
    keys[0], values[0] = key_here, value_here
    moved = [over_blk(columns[k], lanes, k, 0) for k in steps]
    columns = cores([columns[0]] + moved)

    attention_flops = 4 * rows * total * feats
    gain = norm_gain.reshape(1, feats)

    def share(blocks, *before):
        return call(
            functools.partial(partial_kernel, lanes, blocks),
            [((rows, feats), F32)],
            lengths,
            query_here,
            *(keys[n] for n in blocks),
            *(values[n] for n in blocks),
            *before,
            scalars=1,
            flops=attention_flops * len(blocks) // lanes,
        )

    attended = share(list(range(CORES)))
    last = list(range(CORES + 1, lanes, CORES))
    if last:
        attended = share(list(range(CORES, lanes, CORES)), *attended)
    mixed, mixed_t, normed, inv_std = call(
        functools.partial(forward_kernel, lanes, last),
        [
            ((rows, feats), BF16),
            ((feats, rows), BF16),
            ((rows, feats), F32),
            ((rows, PAIR), F32),
        ],
        lengths,
        query_here,
        *(keys[n] for n in last),
        *(values[n] for n in last),
        *attended,
        gates,
        gain,
        scalars=1,
        scratch=[pltpu.VMEM((rows, feats), F32)],
        flops=attention_flops * len(last) // lanes,
    )
    mixes = cores([mixed_t] + cross(mixed_t))
    layer_out, grad_query, grad_gate, grads_queries = call(
        functools.partial(query_kernel, lanes),
        [
            ((rows, model), BF16),
            ((rows, feats), BF16),
            ((rows, feats), BF16),
            ((rows, 2 * feats), BF16),
        ],
        lengths,
        query_here,
        *keys,
        *values,
        gates,
        gain,
        out_grad,
        normed,
        inv_std,
        mixed,
        out_weight,
        scalars=1,
        flops=attention_flops + 4 * rows * feats * model,
    )
    grads = cores([grads_queries] + cross(grads_queries))
    grad_key, grad_value = call(
        functools.partial(key_kernel, lanes),
        [((rows, feats), BF16), ((rows, feats), BF16)],
        lengths,
        key_here,
        value_here,
        *grads,
        scalars=1,
        flops=2 * attention_flops,
    )

    stages = digits(groups)
    size = feats
    plan = []
    for n, digit in enumerate(stages):
        parts = digit[1] if n == 0 and size % (16 * digit[1]) == 0 else 1
        size //= parts
        plan.append((digit, parts, size))

    def pieces_of(parts, part):
        return [((part, width), F32)] + [((part, width), BF16)] * (parts - 1)

    held = call(
        functools.partial(product_kernel, lanes, plan[0][0]),
        pieces_of(plan[0][1], plan[0][2]),
        *mixes,
        *columns,
        scratch=[pltpu.VMEM((feats, width), F32)],
        flops=2 * total * feats * width,
    )
    for n, (digit, parts, part) in enumerate(plan):
        if parts > 1:
            received = [over_digit(held[k], groups, digit, k) for k in range(1, parts)]
        else:
            held = [held[0].astype(BF16)]
            received = [over_digit(held[0], groups, digit, k) for k in range(1, digit[1])]
        last = n + 1 == len(plan)
        nxt = None if last else plan[n + 1]
        split_next = not last and nxt[1] > 1
        held = call(
            functools.partial(
                sum_split_kernel,
                len(received),
                None if parts > 1 else digit,
                nxt[0] if split_next else None,
            ),
            [((part, width), BF16)] if not split_next else pieces_of(nxt[1], nxt[2]),
            held[0],
            *received,
            scratch=[pltpu.VMEM((part if parts > 1 else part * digit[1], width), F32)],
        )
    piece = held[0]
    gathers = [entry for entry in plan[::-1] if entry[1] > 1]
    for n, (digit, parts, part) in enumerate(gathers):
        received = [over_digit(piece, groups, digit, k) for k in range(1, parts)]
        (piece,) = call(
            functools.partial(join_kernel, digit),
            [((part * parts, width), F32 if n + 1 == len(gathers) else BF16)],
            piece,
            *received,
        )
    return (layer_out, grad_query, grad_key, grad_value, grad_gate, piece.astype(F32))


def solution(mesh):
    rows = P(("grp", "blk"), None)
    return jax.shard_map(
        layer,
        mesh=mesh,
        in_specs=(rows, rows, rows, rows, rows, P("grp"), P(), P()),
        out_specs=(rows, rows, rows, rows, rows, P(None, "blk")),
        check_vma=False,
    )
```

time: 57 us -> 57.7 us (1.012)
  local copies, waits for them, and re-layouts: 2.87 us -> 0.22 us
  waiting for transfers between devices: 25.6 us -> 27.9 us
  Pallas kernels: 8.71 us -> 9.79 us
    unnamed x16 -> x6, local copies, waits for them, and re-layouts: 2.87 us -> 0.22 us
    ppermute x7, waiting for transfers between devices: 8.81 us -> 11.1 us  [over_digit(): return lax.ppermute(x, 'grp', pairs)]
    pallas_call x8 -> x10, Pallas kernels: 8.71 us -> 9.79 us  [call(): pl.pallas_call(kernel, out_shape=[jax.ShapeDtypeStruct(s, d) for s, d in...]
  transfers between devices with their start and end apart: 22 -> 22, of which waited for: 10 -> 12; matrix products, arithmetic and copies ran while one was open for 0% -> 0% of each run, Pallas kernels for 7% -> 6%
where the time goes in v4:
time: 57.7 us; the launch traced here: 57.6 us
  waiting for transfers between devices  27.9 us (48%)
  starting transfers between devices  18.2 us (32%)
  Pallas kernels  9.79 us (17%)
  between operations  1.42 us (2%)
    ppermute x15, waiting for transfers between devices, over_blk(): return lax.ppermute(x, 'blk', pairs)  16.7 us
    ppermute x7, waiting for transfers between devices, over_digit(): return lax.ppermute(x, 'grp', pairs)  11.1 us
    pallas_call x10, Pallas kernels, call(): pl.pallas_call(kernel, out_shape=[jax.ShapeDtypeStruct(s, d) for s, d in...  9.79 us
    ppermute x7, starting transfers between devices, over_digit(): return lax.ppermute(x, 'grp', pairs)  9.76 us
    ppermute x15, starting transfers between devices, over_blk(): return lax.ppermute(x, 'blk', pairs)  8.49 us
  transfers between devices with their start and end apart: 22, of which 12 were waited for; matrix products, arithmetic and copies ran while one was open for 0% of the time, Pallas kernels for 6%

profile of v4, /device:TPU:0, one launch (start us, length us, event | category | flops | bytes accessed | tf_op | source)
XLA Modules:
  0.0 57.6 jit_solution(16786208511971220216)
XLA Ops:
  0.6 3.0 %collective-permute-start.1 = (bf16[128,512]{1,0:T(8,128)(2,1)}, bf16[128,512]{1,0:T(8,128)(2,1)S(1)}, u32[]{:S(2)}, u32[]{:S(2)}) collective-permute-start(bf16[128,512]{1,0:T(8,128)(2,1)} %refs_1_.1), channel_id=1, source_target_pairs={{0,2},{1,3},{2,0},{3,1},{4,6},{5,7},{6,4},{7,5},{8,10},{9,11},{10,... | collective-permute-start | bytes 393224 | tf_op jit(solution)/shard_map/ppermute | solution.py:71
  3.7 0.5 collective-permute-start.3
  4.3 4.0 %collective-permute-done.1.refs_2_.refs_4_ = bf16[128,512]{1,0:T(8,128)(2,1)S(1)} collective-permute-done((bf16[128,512]{1,0:T(8,128)(2,1)}, bf16[128,512]{1,0:T(8,128)(2,1)S(1)}, u32[]{:S(2)}, u32[]{:S(2)}) %collective-permute-start.1) | collective-permute-done | bytes 131104 | tf_op jit(solution)/shard_map/ppermute | solution.py:71
  8.2 2.0 %collective-permute-done.4.refs_3_.refs_8_ = bf16[128,512]{1,0:T(8,128)(2,1)S(1)} collective-permute-done((bf16[128,512]{1,0:T(8,128)(2,1)}, bf16[128,512]{1,0:T(8,128)(2,1)S(1)}, u32[]{:S(2)}, u32[]{:S(2)}) %collective-permute-start.4) | collective-permute-done | bytes 131104 | tf_op jit(solution)/shard_map/ppermute | solution.py:71
  10.8 1.3 %shard_map.127 = (bf16[128,512]{1,0:T(8,128)(2,1)S(1)}, bf16[128,512]{1,0:T(8,128)(2,1)S(1)}, bf16[128,512]{1,0:T(8,128)(2,1)S(1)}, bf16[128,512]{1,0:T(8,128)(2...) custom-call(bf16[128,1024]{1,0:T(8,128)(2,1)} %refs_12_.1, bf16[128,512]{1,0:T(8,128)(2,1)} %refs_0_.6, ...), custom_call_target="tpu_custom_call" | custom-call | tf_op jit(solution)/shard_map/pallas_call | solution.py:38
  12.1 0.7 %shard_map.128.refs_4_ = f32[128,512]{1,0:T(8,128)S(1)} custom-call(s32[1]{0:T(128)S(6)} %copy.14.refs_0_, bf16[128,512]{1,0:T(8,128)(2,1)S(1)} %get-tuple-element.26.refs_1_, bf16[128,512]{1,0:T(8,128)(2,1)S(1)} %get-tuple-element.27.refs_2_.refs_1_, bf16[128,512]{1,0:T(8,128)(2,1)S(1)} %collective-permute-done.refs_3_, ...), custom_call_target="tpu_custom_call" | custom-call | flops 67108864 | tf_op jit(solution)/shard_map/pallas_call | solution.py:38
  12.8 0.5 shard_map.129.refs_4_
  13.4 0.8 %shard_map.130 = (bf16[128,512]{1,0:T(8,128)(2,1)S(1)}, bf16[512,128]{1,0:T(8,128)(2,1)S(1)}, f32[128,512]{1,0:T(8,128)S(1)}, f32[128,128]{1,0:T(8,128)S(1)}) custom-call(s32[1]{0:T(128)S(6)} %copy.14.refs_0_, bf16[128,512]{1,0:T(8,128)(2,1)S(1)} %get-tuple-element.26.refs_1_, bf16[128,512]{1,0:T(8,128)(2,1)S(1)} %collective-permute-done.2.refs_2_.refs_5_, ...), custom_call_target="tpu_custom_call" | custom-call | flops 33554432 | tf_op jit(solution)/shard_map/pallas_call | solution.py:38
  14.4 2.7 %shard_map.131 = (bf16[128,1024]{1,0:T(8,128)(2,1)}, bf16[128,512]{1,0:T(8,128)(2,1)}, bf16[128,512]{1,0:T(8,128)(2,1)}, bf16[128,1024]{1,0:T(8,128)(2,1)S(1)}) custom-call(s32[1]{0:T(128)S(6)} %copy.14.refs_0_, bf16[128,512]{1,0:T(8,128)(2,1)S(1)} %get-tuple-element.26.refs_1_, bf16[128,512]{1,0:T(8,128)(2,1)S(1)} %get-tuple-element.27.refs_2_.refs_1_, ...), custom_call_target="tpu_custom_call" | custom-call | flops 402653184 | tf_op jit(solution)/shard_map/pallas_call | solution.py:38
  17.2 1.7 %collective-permute-start.7 = (bf16[128,1024]{1,0:T(8,128)(2,1)S(1)}, bf16[128,1024]{1,0:T(8,128)(2,1)S(1)}, u32[]{:S(2)}, u32[]{:S(2)}) collective-permute-start(bf16[128,1024]{1,0:T(8,128)(2,1)S(1)} %get-tuple-element.35.refs_3_), channel_id=1, source_target_pairs={{0,2},{1,3},{2,0},{3,1},{4,6},{5,7},{6,4},{7,5},{8,10},{9,11},{10,... | collective-permute-start | bytes 786440 | tf_op jit(solution)/shard_map/ppermute | solution.py:71
  19.2 1.7 %collective-permute-start.10 = (bf16[512,128]{1,0:T(8,128)(2,1)S(1)}, bf16[512,128]{1,0:T(8,128)(2,1)S(1)}, u32[]{:S(2)}, u32[]{:S(2)}) collective-permute-start(bf16[512,128]{1,0:T(8,128)(2,1)S(1)} %get-tuple-element.39.refs_0_), channel_id=1, source_target_pairs={{0,2},{1,3},{2,0},{3,1},{4,6},{5,7},{6,4},{7,5},{8,10},{9,11},{10,... | collective-permute-start | bytes 393224 | tf_op jit(solution)/shard_map/ppermute | solution.py:71
  21.0 8.2 %collective-permute-done.13.refs_6_ = bf16[128,512]{1,0:T(8,128)(2,1)S(1)} collective-permute-done((bf16[128,512]{1,0:T(8,128)(2,1)S(1)}, bf16[128,512]{1,0:T(8,128)(2,1)S(1)}, u32[]{:S(2)}, u32[]{:S(2)}) %collective-permute-start.13) | collective-permute-done | bytes 131104 | tf_op jit(solution)/shard_map/ppermute | solution.py:71
  29.2 0.5 collective-permute-start.9
  29.7 1.8 %collective-permute-done.10.refs_2_ = bf16[512,128]{1,0:T(8,128)(2,1)S(1)} collective-permute-done((bf16[512,128]{1,0:T(8,128)(2,1)S(1)}, bf16[512,128]{1,0:T(8,128)(2,1)S(1)}, u32[]{:S(2)}, u32[]{:S(2)}) %collective-permute-start.10) | collective-permute-done | bytes 131104 | tf_op jit(solution)/shard_map/ppermute | solution.py:71
  31.5 0.5 collective-permute-start.6
  32.1 0.8 %collective-permute-done.11.refs_3_ = bf16[512,128]{1,0:T(8,128)(2,1)S(1)} collective-permute-done((bf16[512,128]{1,0:T(8,128)(2,1)S(1)}, bf16[512,128]{1,0:T(8,128)(2,1)S(1)}, u32[]{:S(2)}, u32[]{:S(2)}) %collective-permute-start.11) | collective-permute-done | bytes 131104 | tf_op jit(solution)/shard_map/ppermute | solution.py:71
  32.9 0.4 shard_map.133
  33.2 1.8 %collective-permute-start.15 = (bf16[128,256]{1,0:T(8,128)(2,1)S(1)}, bf16[128,256]{1,0:T(8,128)(2,1)S(1)}, u32[]{:S(2)}, u32[]{:S(2)}) collective-permute-start(bf16[128,256]{1,0:T(8,128)(2,1)S(1)} %get-tuple-element.43), channel_id=1, source_target_pairs={{0,4},{4,0},{8,12},{12,8},{16,20},{20,16},{24,28},{28,24},{1,5},{5... | collective-permute-start | bytes 196616 | tf_op jit(solution)/shard_map/ppermute | solution.py:91
  35.1 1.6 %collective-permute-start.16 = (bf16[128,256]{1,0:T(8,128)(2,1)S(1)}, bf16[128,256]{1,0:T(8,128)(2,1)S(1)}, u32[]{:S(2)}, u32[]{:S(2)}) collective-permute-start(bf16[128,256]{1,0:T(8,128)(2,1)S(1)} %get-tuple-element.44), channel_id=1, source_target_pairs={{0,8},{4,12},{8,0},{12,4},{16,24},{20,28},{24,16},{28,20},{1,9},{5... | collective-permute-start | bytes 196616 | tf_op jit(solution)/shard_map/ppermute | solution.py:91
  36.8 0.8 %collective-permute-done.15.refs_1_ = bf16[128,256]{1,0:T(8,128)(2,1)S(1)} collective-permute-done((bf16[128,256]{1,0:T(8,128)(2,1)S(1)}, bf16[128,256]{1,0:T(8,128)(2,1)S(1)}, u32[]{:S(2)}, u32[]{:S(2)}) %collective-permute-start.15) | collective-permute-done | bytes 65568 | tf_op jit(solution)/shard_map/ppermute | solution.py:91
  37.6 2.3 %collective-permute-done.16.refs_2_ = bf16[128,256]{1,0:T(8,128)(2,1)S(1)} collective-permute-done((bf16[128,256]{1,0:T(8,128)(2,1)S(1)}, bf16[128,256]{1,0:T(8,128)(2,1)S(1)}, u32[]{:S(2)}, u32[]{:S(2)}) %collective-permute-start.16) | collective-permute-done | bytes 65568 | tf_op jit(solution)/shard_map/ppermute | solution.py:91
  39.9 1.9 %collective-permute-done.17.refs_3_ = bf16[128,256]{1,0:T(8,128)(2,1)S(1)} collective-permute-done((bf16[128,256]{1,0:T(8,128)(2,1)S(1)}, bf16[128,256]{1,0:T(8,128)(2,1)S(1)}, u32[]{:S(2)}, u32[]{:S(2)}) %collective-permute-start.17) | collective-permute-done | bytes 65568 | tf_op jit(solution)/shard_map/ppermute | solution.py:91
  41.9 2.7 %collective-permute-start.18 = (bf16[128,256]{1,0:T(8,128)(2,1)S(1)}, bf16[128,256]{1,0:T(8,128)(2,1)S(1)}, u32[]{:S(2)}, u32[]{:S(2)}) collective-permute-start(bf16[128,256]{1,0:T(8,128)(2,1)S(1)} %shard_map.134.refs_0_), channel_id=1, source_target_pairs={{0,16},{4,20},{8,24},{12,28},{16,0},{20,4},{24,8},{28,12},{1,17},{... | collective-permute-start | bytes 196616 | tf_op jit(solution)/shard_map/ppermute | solution.py:91
  44.5 3.1 %collective-permute-done.18.refs_1_ = bf16[128,256]{1,0:T(8,128)(2,1)S(1)} collective-permute-done((bf16[128,256]{1,0:T(8,128)(2,1)S(1)}, bf16[128,256]{1,0:T(8,128)(2,1)S(1)}, u32[]{:S(2)}, u32[]{:S(2)}) %collective-permute-start.18) | collective-permute-done | bytes 65568 | tf_op jit(solution)/shard_map/ppermute | solution.py:91
  47.7 0.7 %collective-permute-start.19 = (bf16[128,256]{1,0:T(8,128)(2,1)S(1)}, bf16[128,256]{1,0:T(8,128)(2,1)S(1)}, u32[]{:S(2)}, u32[]{:S(2)}) collective-permute-start(bf16[128,256]{1,0:T(8,128)(2,1)S(1)} %shard_map.135.refs_0_), channel_id=1, source_target_pairs={{0,4},{4,0},{8,12},{12,8},{16,20},{20,16},{24,28},{28,24},{1,5},{5... | collective-permute-start | bytes 196616 | tf_op jit(solution)/shard_map/ppermute | solution.py:91
  48.4 0.5 collective-permute-start.20
  48.9 2.4 %collective-permute-start.21 = (bf16[128,256]{1,0:T(8,128)(2,1)S(1)}, bf16[128,256]{1,0:T(8,128)(2,1)S(1)}, u32[]{:S(2)}, u32[]{:S(2)}) collective-permute-start(bf16[128,256]{1,0:T(8,128)(2,1)S(1)} %shard_map.135.refs_0_), channel_id=1, source_target_pairs={{0,12},{4,8},{8,4},{12,0},{16,28},{20,24},{24,20},{28,16},{1,13},{... | collective-permute-start | bytes 196616 | tf_op jit(solution)/shard_map/ppermute | solution.py:91
  51.3 0.8 %collective-permute-done.19.refs_1_ = bf16[128,256]{1,0:T(8,128)(2,1)S(1)} collective-permute-done((bf16[128,256]{1,0:T(8,128)(2,1)S(1)}, bf16[128,256]{1,0:T(8,128)(2,1)S(1)}, u32[]{:S(2)}, u32[]{:S(2)}) %collective-permute-start.19) | collective-permute-done | bytes 65568 | tf_op jit(solution)/shard_map/ppermute | solution.py:91
  52.0 0.6 %collective-permute-done.20.refs_2_ = bf16[128,256]{1,0:T(8,128)(2,1)S(1)} collective-permute-done((bf16[128,256]{1,0:T(8,128)(2,1)S(1)}, bf16[128,256]{1,0:T(8,128)(2,1)S(1)}, u32[]{:S(2)}, u32[]{:S(2)}) %collective-permute-start.20) | collective-permute-done | bytes 65568 | tf_op jit(solution)/shard_map/ppermute | solution.py:91
  52.7 1.5 %collective-permute-done.21.refs_3_ = bf16[128,256]{1,0:T(8,128)(2,1)S(1)} collective-permute-done((bf16[128,256]{1,0:T(8,128)(2,1)S(1)}, bf16[128,256]{1,0:T(8,128)(2,1)S(1)}, u32[]{:S(2)}, u32[]{:S(2)}) %collective-permute-start.21) | collective-permute-done | bytes 65568 | tf_op jit(solution)/shard_map/ppermute | solution.py:91
  54.2 0.8 %shard_map.136 = f32[512,256]{1,0:T(8,128)} custom-call(bf16[128,256]{1,0:T(8,128)(2,1)S(1)} %shard_map.135.refs_0_, bf16[128,256]{1,0:T(8,128)(2,1)S(1)} %collective-permute-done.19.refs_1_, bf16[128,256]{1,0:T(8,128)(2,1)S(1)} %collective-permute-done.20.refs_2_, bf16[128,256]{1,0:T(8,128)(2,1)S(1)} %collective-permute-done.21.refs_3_), custom_call_target="tpu_custom_call" | custom-call | tf_op jit(solution)/shard_map/pallas_call | solution.py:38
  55.0 2.5 %shard_map.132 = (bf16[128,512]{1,0:T(8,128)(2,1)}, bf16[128,512]{1,0:T(8,128)(2,1)}) custom-call(s32[1]{0:T(128)S(6)} %copy.14.refs_0_, bf16[128,512]{1,0:T(8,128)(2,1)S(1)} %get-tuple-element.27.refs_2_.refs_1_, bf16[128,512]{1,0:T(8,128)(2,1)S(1)} %get-tuple-element.28.refs_4_.refs_6_.refs_2_, bf16[128,1024]{1,0:T(8,128)(2,1)S(1)} %get-tuple-element.35.refs_3_, ...), custom_call_target="tpu_custom_call" | custom-call | flops 268435456 | tf_op jit(solution)/shard_map/pallas_call | solution.py:38
  (28 shorter events, 0.9 us)
Async XLA Ops:
  0.6 7.6 %collective-permute-start.1 = (bf16[128,512]{1,0:T(8,128)(2,1)}, bf16[128,512]{1,0:T(8,128)(2,1)S(1)}, u32[]{:S(2)}, u32[]{:S(2)}) collective-permute-start(bf16[128,512]{1,0:T(8,128)(2,1)} %refs_1_.1), channel_id=1, source_target_pairs={{0,2},{1,3},{2,0},{3,1},{4,6},{5,7},{6,4},{7,5},{8,10},{9,11},{10,... | collective-permute-start | bytes 393224 | tf_op jit(solution)/shard_map/ppermute | solution.py:71
  3.7 6.5 %collective-permute-start.4 = (bf16[128,512]{1,0:T(8,128)(2,1)}, bf16[128,512]{1,0:T(8,128)(2,1)S(1)}, u32[]{:S(2)}, u32[]{:S(2)}) collective-permute-start(bf16[128,512]{1,0:T(8,128)(2,1)} %refs_2_.1), channel_id=1, source_target_pairs={{0,2},{1,3},{2,0},{3,1},{4,6},{5,7},{6,4},{7,5},{8,10},{9,11},{10,... | collective-permute-start | bytes 393224 | tf_op jit(solution)/shard_map/ppermute | solution.py:71
  3.7 8.4 %collective-permute-start = (bf16[128,512]{1,0:T(8,128)(2,1)}, bf16[128,512]{1,0:T(8,128)(2,1)S(1)}, u32[]{:S(2)}, u32[]{:S(2)}) collective-permute-start(bf16[128,512]{1,0:T(8,128)(2,1)} %refs_1_.1), channel_id=1, source_target_pairs={{0,1},{1,0},{2,3},{3,2},{4,5},{5,4},{6,7},{7,6},{8,9},{9,8},{10,11... | collective-permute-start | bytes 393224 | tf_op jit(solution)/shard_map/ppermute | solution.py:71
  3.7 8.4 %collective-permute-start.3 = (bf16[128,512]{1,0:T(8,128)(2,1)}, bf16[128,512]{1,0:T(8,128)(2,1)S(1)}, u32[]{:S(2)}, u32[]{:S(2)}) collective-permute-start(bf16[128,512]{1,0:T(8,128)(2,1)} %refs_2_.1), channel_id=1, source_target_pairs={{0,1},{1,0},{2,3},{3,2},{4,5},{5,4},{6,7},{7,6},{8,9},{9,8},{10,11... | collective-permute-start | bytes 393224 | tf_op jit(solution)/shard_map/ppermute | solution.py:71
  8.2 5.2 %collective-permute-start.2 = (bf16[128,512]{1,0:T(8,128)(2,1)S(1)}, bf16[128,512]{1,0:T(8,128)(2,1)S(1)}, u32[]{:S(2)}, u32[]{:S(2)}) collective-permute-start(bf16[128,512]{1,0:T(8,128)(2,1)S(1)} %collective-permute-done.1.refs_2_.refs_4_), channel_id=1, source_target_pairs={{0,1},{1,0},{2,3},{3,2},{4,5},{5,4},{6,7},{7,6},{8,9},{9,8},{10,11... | collective-permute-start | bytes 393224 | tf_op jit(solution)/shard_map/ppermute | solution.py:71
  10.2 3.2 %collective-permute-start.5 = (bf16[128,512]{1,0:T(8,128)(2,1)S(1)}, bf16[128,512]{1,0:T(8,128)(2,1)S(1)}, u32[]{:S(2)}, u32[]{:S(2)}) collective-permute-start(bf16[128,512]{1,0:T(8,128)(2,1)S(1)} %collective-permute-done.4.refs_3_.refs_8_), channel_id=1, source_target_pairs={{0,1},{1,0},{2,3},{3,2},{4,5},{5,4},{6,7},{7,6},{8,9},{9,8},{10,11... | collective-permute-start | bytes 393224 | tf_op jit(solution)/shard_map/ppermute | solution.py:71
  12.1 1.3 %copy-start.2 = (f32[512]{0:T(512)S(1)}, f32[512]{0:T(512)}, u32[]{:S(2)}) copy-start(f32[512]{0:T(512)} %param.14) | copy-start | bytes 6148
  12.8 1.4 %copy-start = (bf16[512,1024]{1,0:T(8,128)(2,1)S(1)}, bf16[512,1024]{1,0:T(8,128)(2,1)}, u32[]{:S(2)}) copy-start(bf16[512,1024]{1,0:T(8,128)(2,1)} %refs_16_.1) | copy-start | bytes 3145732
  13.4 1.0 %copy-start.1 = (bf16[128,1024]{1,0:T(8,128)(2,1)S(1)}, bf16[128,1024]{1,0:T(8,128)(2,1)}, u32[]{:S(2)}) copy-start(bf16[128,1024]{1,0:T(8,128)(2,1)} %refs_12_.1) | copy-start | bytes 786436
  17.2 14.8 %collective-permute-start.7 = (bf16[128,1024]{1,0:T(8,128)(2,1)S(1)}, bf16[128,1024]{1,0:T(8,128)(2,1)S(1)}, u32[]{:S(2)}, u32[]{:S(2)}) collective-permute-start(bf16[128,1024]{1,0:T(8,128)(2,1)S(1)} %get-tuple-element.35.refs_3_), channel_id=1, source_target_pairs={{0,2},{1,3},{2,0},{3,1},{4,6},{5,7},{6,4},{7,5},{8,10},{9,11},{10,... | collective-permute-start | bytes 786440 | tf_op jit(solution)/shard_map/ppermute | solution.py:71
  18.9 10.2 %collective-permute-start.13 = (bf16[128,512]{1,0:T(8,128)(2,1)S(1)}, bf16[128,512]{1,0:T(8,128)(2,1)S(1)}, u32[]{:S(2)}, u32[]{:S(2)}) collective-permute-start(bf16[128,512]{1,0:T(8,128)(2,1)S(1)} %get-tuple-element.41), channel_id=1, source_target_pairs={{0,2},{1,3},{2,0},{3,1},{4,6},{5,7},{6,4},{7,5},{8,10},{9,11},{10,... | collective-permute-start | bytes 393224 | tf_op jit(solution)/shard_map/ppermute | solution.py:71
  19.2 12.3 %collective-permute-start.10 = (bf16[512,128]{1,0:T(8,128)(2,1)S(1)}, bf16[512,128]{1,0:T(8,128)(2,1)S(1)}, u32[]{:S(2)}, u32[]{:S(2)}) collective-permute-start(bf16[512,128]{1,0:T(8,128)(2,1)S(1)} %get-tuple-element.39.refs_0_), channel_id=1, source_target_pairs={{0,2},{1,3},{2,0},{3,1},{4,6},{5,7},{6,4},{7,5},{8,10},{9,11},{10,... | collective-permute-start | bytes 393224 | tf_op jit(solution)/shard_map/ppermute | solution.py:71
  21.0 10.6 %collective-permute-start.12 = (bf16[128,512]{1,0:T(8,128)(2,1)S(1)}, bf16[128,512]{1,0:T(8,128)(2,1)S(1)}, u32[]{:S(2)}, u32[]{:S(2)}) collective-permute-start(bf16[128,512]{1,0:T(8,128)(2,1)S(1)} %get-tuple-element.40.refs_4_), channel_id=1, source_target_pairs={{0,1},{1,0},{2,3},{3,2},{4,5},{5,4},{6,7},{7,6},{8,9},{9,8},{10,11... | collective-permute-start | bytes 393224 | tf_op jit(solution)/shard_map/ppermute | solution.py:71
  29.2 2.9 %collective-permute-start.14 = (bf16[128,512]{1,0:T(8,128)(2,1)S(1)}, bf16[128,512]{1,0:T(8,128)(2,1)S(1)}, u32[]{:S(2)}, u32[]{:S(2)}) collective-permute-start(bf16[128,512]{1,0:T(8,128)(2,1)S(1)} %collective-permute-done.13.refs_6_), channel_id=1, source_target_pairs={{0,1},{1,0},{2,3},{3,2},{4,5},{5,4},{6,7},{7,6},{8,9},{9,8},{10,11... | collective-permute-start | bytes 393224 | tf_op jit(solution)/shard_map/ppermute | solution.py:71
  29.2 2.9 %collective-permute-start.9 = (bf16[512,128]{1,0:T(8,128)(2,1)S(1)}, bf16[512,128]{1,0:T(8,128)(2,1)S(1)}, u32[]{:S(2)}, u32[]{:S(2)}) collective-permute-start(bf16[512,128]{1,0:T(8,128)(2,1)S(1)} %get-tuple-element.39.refs_0_), channel_id=1, source_target_pairs={{0,1},{1,0},{2,3},{3,2},{4,5},{5,4},{6,7},{7,6},{8,9},{9,8},{10,11... | collective-permute-start | bytes 393224 | tf_op jit(solution)/shard_map/ppermute | solution.py:71
  31.5 1.3 %collective-permute-start.11 = (bf16[512,128]{1,0:T(8,128)(2,1)S(1)}, bf16[512,128]{1,0:T(8,128)(2,1)S(1)}, u32[]{:S(2)}, u32[]{:S(2)}) collective-permute-start(bf16[512,128]{1,0:T(8,128)(2,1)S(1)} %collective-permute-done.10.refs_2_), channel_id=1, source_target_pairs={{0,1},{1,0},{2,3},{3,2},{4,5},{5,4},{6,7},{7,6},{8,9},{9,8},{10,11... | collective-permute-start | bytes 393224 | tf_op jit(solution)/shard_map/ppermute | solution.py:71
  31.5 23.5 %collective-permute-start.6 = (bf16[128,1024]{1,0:T(8,128)(2,1)S(1)}, bf16[128,1024]{1,0:T(8,128)(2,1)S(1)}, u32[]{:S(2)}, u32[]{:S(2)}) collective-permute-start(bf16[128,1024]{1,0:T(8,128)(2,1)S(1)} %get-tuple-element.35.refs_3_), channel_id=1, source_target_pairs={{0,1},{1,0},{2,3},{3,2},{4,5},{5,4},{6,7},{7,6},{8,9},{9,8},{10,11... | collective-permute-start | bytes 786440 | tf_op jit(solution)/shard_map/ppermute | solution.py:71
  32.0 23.0 %collective-permute-start.8 = (bf16[128,1024]{1,0:T(8,128)(2,1)S(1)}, bf16[128,1024]{1,0:T(8,128)(2,1)S(1)}, u32[]{:S(2)}, u32[]{:S(2)}) collective-permute-start(bf16[128,1024]{1,0:T(8,128)(2,1)S(1)} %collective-permute-done.7.refs_5_), channel_id=1, source_target_pairs={{0,1},{1,0},{2,3},{3,2},{4,5},{5,4},{6,7},{7,6},{8,9},{9,8},{10,11... | collective-permute-start | bytes 786440 | tf_op jit(solution)/shard_map/ppermute | solution.py:71
  33.2 4.3 %collective-permute-start.15 = (bf16[128,256]{1,0:T(8,128)(2,1)S(1)}, bf16[128,256]{1,0:T(8,128)(2,1)S(1)}, u32[]{:S(2)}, u32[]{:S(2)}) collective-permute-start(bf16[128,256]{1,0:T(8,128)(2,1)S(1)} %get-tuple-element.43), channel_id=1, source_target_pairs={{0,4},{4,0},{8,12},{12,8},{16,20},{20,16},{24,28},{28,24},{1,5},{5... | collective-permute-start | bytes 196616 | tf_op jit(solution)/shard_map/ppermute | solution.py:91
  35.1 4.8 %collective-permute-start.16 = (bf16[128,256]{1,0:T(8,128)(2,1)S(1)}, bf16[128,256]{1,0:T(8,128)(2,1)S(1)}, u32[]{:S(2)}, u32[]{:S(2)}) collective-permute-start(bf16[128,256]{1,0:T(8,128)(2,1)S(1)} %get-tuple-element.44), channel_id=1, source_target_pairs={{0,8},{4,12},{8,0},{12,4},{16,24},{20,28},{24,16},{28,20},{1,9},{5... | collective-permute-start | bytes 196616 | tf_op jit(solution)/shard_map/ppermute | solution.py:91
  36.7 5.2 %collective-permute-start.17 = (bf16[128,256]{1,0:T(8,128)(2,1)S(1)}, bf16[128,256]{1,0:T(8,128)(2,1)S(1)}, u32[]{:S(2)}, u32[]{:S(2)}) collective-permute-start(bf16[128,256]{1,0:T(8,128)(2,1)S(1)} %get-tuple-element.45), channel_id=1, source_target_pairs={{0,12},{4,8},{8,4},{12,0},{16,28},{20,24},{24,20},{28,16},{1,13},{... | collective-permute-start | bytes 196616 | tf_op jit(solution)/shard_map/ppermute | solution.py:91
  41.9 5.8 %collective-permute-start.18 = (bf16[128,256]{1,0:T(8,128)(2,1)S(1)}, bf16[128,256]{1,0:T(8,128)(2,1)S(1)}, u32[]{:S(2)}, u32[]{:S(2)}) collective-permute-start(bf16[128,256]{1,0:T(8,128)(2,1)S(1)} %shard_map.134.refs_0_), channel_id=1, source_target_pairs={{0,16},{4,20},{8,24},{12,28},{16,0},{20,4},{24,8},{28,12},{1,17},{... | collective-permute-start | bytes 196616 | tf_op jit(solution)/shard_map/ppermute | solution.py:91
  47.7 4.3 %collective-permute-start.19 = (bf16[128,256]{1,0:T(8,128)(2,1)S(1)}, bf16[128,256]{1,0:T(8,128)(2,1)S(1)}, u32[]{:S(2)}, u32[]{:S(2)}) collective-permute-start(bf16[128,256]{1,0:T(8,128)(2,1)S(1)} %shard_map.135.refs_0_), channel_id=1, source_target_pairs={{0,4},{4,0},{8,12},{12,8},{16,20},{20,16},{24,28},{28,24},{1,5},{5... | collective-permute-start | bytes 196616 | tf_op jit(solution)/shard_map/ppermute | solution.py:91
  48.4 4.3 %collective-permute-start.20 = (bf16[128,256]{1,0:T(8,128)(2,1)S(1)}, bf16[128,256]{1,0:T(8,128)(2,1)S(1)}, u32[]{:S(2)}, u32[]{:S(2)}) collective-permute-start(bf16[128,256]{1,0:T(8,128)(2,1)S(1)} %shard_map.135.refs_0_), channel_id=1, source_target_pairs={{0,8},{4,12},{8,0},{12,4},{16,24},{20,28},{24,16},{28,20},{1,9},{5... | collective-permute-start | bytes 196616 | tf_op jit(solution)/shard_map/ppermute | solution.py:91
  48.9 5.3 %collective-permute-start.21 = (bf16[128,256]{1,0:T(8,128)(2,1)S(1)}, bf16[128,256]{1,0:T(8,128)(2,1)S(1)}, u32[]{:S(2)}, u32[]{:S(2)}) collective-permute-start(bf16[128,256]{1,0:T(8,128)(2,1)S(1)} %shard_map.135.refs_0_), channel_id=1, source_target_pairs={{0,12},{4,8},{8,4},{12,0},{16,28},{20,24},{24,20},{28,16},{1,13},{... | collective-permute-start | bytes 196616 | tf_op jit(solution)/shard_map/ppermute | solution.py:91

commit v5 on v4

--- a/solution.py
+++ b/solution.py
@@ -161,6 +161,12 @@
         copy.start()
     for copy in copies:
         copy.wait()
+
+
+def weight_and_slope(half, live):
+    u = jnp.where(live, 1.0 + jnp.tanh(half), 0.0)
+    weight = half * u
+    return weight, u + weight * (2.0 - u)
 
 
 def attend(lanes, length, q_ref, k_refs, v_refs, blocks, cols):
@@ -242,13 +248,12 @@
             keys = stack(k_refs, blocks, cols)
             half = dot(lhs, keys, NT)
             prob_grad = dot(grads, stack(v_refs, blocks, cols), NT)
-            th = jnp.tanh(half)
-            slope = (0.5 + 0.5 * th) * (1.0 + half * (1.0 - th))
             live = places(blocks, lanes, rows) <= limit
-            score_grad = jnp.where(live, prob_grad * slope, 0.0).astype(BF16)
+            slope = weight_and_slope(half, live)[1]
+            score_grad = (prob_grad * slope).astype(BF16)
             part = dot(score_grad, keys)
             acc = part if acc is None else acc + part
-        dq_ref[:, cols] = (one_pair(acc) * HEAD ** -0.5).astype(BF16)
+        dq_ref[:, cols] = (one_pair(acc) * HALF_SCALE).astype(BF16)
 
 
 def key_kernel(lanes, *refs):
@@ -272,14 +277,12 @@
             where = places(blocks, lanes, rows)
             where = jnp.where(where < length, where, -1)
             live = mine <= where
-            th = jnp.tanh(half)
-            weight = jnp.where(live, half + half * th, 0.0).astype(BF16)
-            slope = (0.5 + 0.5 * th) * (1.0 + half * (1.0 - th))
-            score_grad = jnp.where(live, prob_grad * slope, 0.0).astype(BF16)
-            part_k, part_v = dot(score_grad, queries), dot(weight, grads)
+            weight, slope = weight_and_slope(half, live)
+            score_grad = (prob_grad * slope).astype(BF16)
+            part_k, part_v = dot(score_grad, queries), dot(weight.astype(BF16), grads)
             dk = part_k if dk is None else dk + part_k
             dv = part_v if dv is None else dv + part_v
-        dk_ref[:, cols] = (one_pair(dk) * HEAD ** -0.5).astype(BF16)
+        dk_ref[:, cols] = (one_pair(dk) * HALF_SCALE).astype(BF16)
         dv_ref[:, cols] = one_pair(dv).astype(BF16)
 
 

time: 57.7 us -> 57.6 us (level)
  transfers between devices with their start and end apart: 22 -> 22, of which waited for: 12 -> 12; matrix products, arithmetic and copies ran while one was open for 0% -> 0% of each run, Pallas kernels for 6% -> 7%
where the time goes in v5:
time: 57.6 us; the launch traced here: 57.4 us
  waiting for transfers between devices  27.9 us (48%)
  starting transfers between devices  18.2 us (32%)
  Pallas kernels  9.65 us (17%)
  between operations  1.42 us (2%)
    ppermute x15, waiting for transfers between devices, over_blk(): return lax.ppermute(x, 'blk', pairs)  16.7 us
    ppermute x7, waiting for transfers between devices, over_digit(): return lax.ppermute(x, 'grp', pairs)  11.1 us
    ppermute x7, starting transfers between devices, over_digit(): return lax.ppermute(x, 'grp', pairs)  9.76 us
    pallas_call x10, Pallas kernels, call(): pl.pallas_call(kernel, out_shape=[jax.ShapeDtypeStruct(s, d) for s, d in...  9.65 us
    ppermute x15, starting transfers between devices, over_blk(): return lax.ppermute(x, 'blk', pairs)  8.48 us
  transfers between devices with their start and end apart: 22, of which 12 were waited for; matrix products, arithmetic and copies ran while one was open for 0% of the time, Pallas kernels for 7%

profile of v5, /device:TPU:0, one launch (start us, length us, event | category | flops | bytes accessed | tf_op | source)
XLA Modules:
  0.0 57.4 jit_solution(15114668028456562883)
XLA Ops:
  0.6 3.0 %collective-permute-start.1 = (bf16[128,512]{1,0:T(8,128)(2,1)}, bf16[128,512]{1,0:T(8,128)(2,1)S(1)}, u32[]{:S(2)}, u32[]{:S(2)}) collective-permute-start(bf16[128,512]{1,0:T(8,128)(2,1)} %refs_1_.1), channel_id=1, source_target_pairs={{0,2},{1,3},{2,0},{3,1},{4,6},{5,7},{6,4},{7,5},{8,10},{9,11},{10,... | collective-permute-start | bytes 393224 | tf_op jit(solution)/shard_map/ppermute | solution.py:71
  3.7 0.5 collective-permute-start.3
  4.3 4.0 %collective-permute-done.1.refs_2_.refs_4_ = bf16[128,512]{1,0:T(8,128)(2,1)S(1)} collective-permute-done((bf16[128,512]{1,0:T(8,128)(2,1)}, bf16[128,512]{1,0:T(8,128)(2,1)S(1)}, u32[]{:S(2)}, u32[]{:S(2)}) %collective-permute-start.1) | collective-permute-done | bytes 131104 | tf_op jit(solution)/shard_map/ppermute | solution.py:71
  8.2 2.0 %collective-permute-done.4.refs_3_.refs_8_ = bf16[128,512]{1,0:T(8,128)(2,1)S(1)} collective-permute-done((bf16[128,512]{1,0:T(8,128)(2,1)}, bf16[128,512]{1,0:T(8,128)(2,1)S(1)}, u32[]{:S(2)}, u32[]{:S(2)}) %collective-permute-start.4) | collective-permute-done | bytes 131104 | tf_op jit(solution)/shard_map/ppermute | solution.py:71
  10.8 1.3 %shard_map.127 = (bf16[128,512]{1,0:T(8,128)(2,1)S(1)}, bf16[128,512]{1,0:T(8,128)(2,1)S(1)}, bf16[128,512]{1,0:T(8,128)(2,1)S(1)}, bf16[128,512]{1,0:T(8,128)(2...) custom-call(bf16[128,1024]{1,0:T(8,128)(2,1)} %refs_12_.1, bf16[128,512]{1,0:T(8,128)(2,1)} %refs_0_.6, ...), custom_call_target="tpu_custom_call" | custom-call | tf_op jit(solution)/shard_map/pallas_call | solution.py:38
  12.1 0.7 %shard_map.128.refs_4_ = f32[128,512]{1,0:T(8,128)S(1)} custom-call(s32[1]{0:T(128)S(6)} %copy.14.refs_0_, bf16[128,512]{1,0:T(8,128)(2,1)S(1)} %get-tuple-element.26.refs_1_, bf16[128,512]{1,0:T(8,128)(2,1)S(1)} %get-tuple-element.27.refs_2_.refs_1_, bf16[128,512]{1,0:T(8,128)(2,1)S(1)} %collective-permute-done.refs_3_, ...), custom_call_target="tpu_custom_call" | custom-call | flops 67108864 | tf_op jit(solution)/shard_map/pallas_call | solution.py:38
  12.8 0.5 shard_map.129.refs_4_
  13.4 0.8 %shard_map.130 = (bf16[128,512]{1,0:T(8,128)(2,1)S(1)}, bf16[512,128]{1,0:T(8,128)(2,1)S(1)}, f32[128,512]{1,0:T(8,128)S(1)}, f32[128,128]{1,0:T(8,128)S(1)}) custom-call(s32[1]{0:T(128)S(6)} %copy.14.refs_0_, bf16[128,512]{1,0:T(8,128)(2,1)S(1)} %get-tuple-element.26.refs_1_, bf16[128,512]{1,0:T(8,128)(2,1)S(1)} %collective-permute-done.2.refs_2_.refs_5_, ...), custom_call_target="tpu_custom_call" | custom-call | flops 33554432 | tf_op jit(solution)/shard_map/pallas_call | solution.py:38
  14.4 2.7 %shard_map.131 = (bf16[128,1024]{1,0:T(8,128)(2,1)}, bf16[128,512]{1,0:T(8,128)(2,1)}, bf16[128,512]{1,0:T(8,128)(2,1)}, bf16[128,1024]{1,0:T(8,128)(2,1)S(1)}) custom-call(s32[1]{0:T(128)S(6)} %copy.14.refs_0_, bf16[128,512]{1,0:T(8,128)(2,1)S(1)} %get-tuple-element.26.refs_1_, bf16[128,512]{1,0:T(8,128)(2,1)S(1)} %get-tuple-element.27.refs_2_.refs_1_, ...), custom_call_target="tpu_custom_call" | custom-call | flops 402653184 | tf_op jit(solution)/shard_map/pallas_call | solution.py:38
  17.2 1.7 %collective-permute-start.7 = (bf16[128,1024]{1,0:T(8,128)(2,1)S(1)}, bf16[128,1024]{1,0:T(8,128)(2,1)S(1)}, u32[]{:S(2)}, u32[]{:S(2)}) collective-permute-start(bf16[128,1024]{1,0:T(8,128)(2,1)S(1)} %get-tuple-element.35.refs_3_), channel_id=1, source_target_pairs={{0,2},{1,3},{2,0},{3,1},{4,6},{5,7},{6,4},{7,5},{8,10},{9,11},{10,... | collective-permute-start | bytes 786440 | tf_op jit(solution)/shard_map/ppermute | solution.py:71
  19.2 1.7 %collective-permute-start.10 = (bf16[512,128]{1,0:T(8,128)(2,1)S(1)}, bf16[512,128]{1,0:T(8,128)(2,1)S(1)}, u32[]{:S(2)}, u32[]{:S(2)}) collective-permute-start(bf16[512,128]{1,0:T(8,128)(2,1)S(1)} %get-tuple-element.39.refs_0_), channel_id=1, source_target_pairs={{0,2},{1,3},{2,0},{3,1},{4,6},{5,7},{6,4},{7,5},{8,10},{9,11},{10,... | collective-permute-start | bytes 393224 | tf_op jit(solution)/shard_map/ppermute | solution.py:71
  20.9 8.2 %collective-permute-done.13.refs_6_ = bf16[128,512]{1,0:T(8,128)(2,1)S(1)} collective-permute-done((bf16[128,512]{1,0:T(8,128)(2,1)S(1)}, bf16[128,512]{1,0:T(8,128)(2,1)S(1)}, u32[]{:S(2)}, u32[]{:S(2)}) %collective-permute-start.13) | collective-permute-done | bytes 131104 | tf_op jit(solution)/shard_map/ppermute | solution.py:71
  29.1 0.5 collective-permute-start.9
  29.7 1.8 %collective-permute-done.10.refs_2_ = bf16[512,128]{1,0:T(8,128)(2,1)S(1)} collective-permute-done((bf16[512,128]{1,0:T(8,128)(2,1)S(1)}, bf16[512,128]{1,0:T(8,128)(2,1)S(1)}, u32[]{:S(2)}, u32[]{:S(2)}) %collective-permute-start.10) | collective-permute-done | bytes 131104 | tf_op jit(solution)/shard_map/ppermute | solution.py:71
  31.5 0.5 collective-permute-start.6
  32.1 0.8 %collective-permute-done.11.refs_3_ = bf16[512,128]{1,0:T(8,128)(2,1)S(1)} collective-permute-done((bf16[512,128]{1,0:T(8,128)(2,1)S(1)}, bf16[512,128]{1,0:T(8,128)(2,1)S(1)}, u32[]{:S(2)}, u32[]{:S(2)}) %collective-permute-start.11) | collective-permute-done | bytes 131104 | tf_op jit(solution)/shard_map/ppermute | solution.py:71
  32.8 0.3 shard_map.133
  33.2 1.8 %collective-permute-start.15 = (bf16[128,256]{1,0:T(8,128)(2,1)S(1)}, bf16[128,256]{1,0:T(8,128)(2,1)S(1)}, u32[]{:S(2)}, u32[]{:S(2)}) collective-permute-start(bf16[128,256]{1,0:T(8,128)(2,1)S(1)} %get-tuple-element.43), channel_id=1, source_target_pairs={{0,4},{4,0},{8,12},{12,8},{16,20},{20,16},{24,28},{28,24},{1,5},{5... | collective-permute-start | bytes 196616 | tf_op jit(solution)/shard_map/ppermute | solution.py:91
  35.0 1.6 %collective-permute-start.16 = (bf16[128,256]{1,0:T(8,128)(2,1)S(1)}, bf16[128,256]{1,0:T(8,128)(2,1)S(1)}, u32[]{:S(2)}, u32[]{:S(2)}) collective-permute-start(bf16[128,256]{1,0:T(8,128)(2,1)S(1)} %get-tuple-element.44), channel_id=1, source_target_pairs={{0,8},{4,12},{8,0},{12,4},{16,24},{20,28},{24,16},{28,20},{1,9},{5... | collective-permute-start | bytes 196616 | tf_op jit(solution)/shard_map/ppermute | solution.py:91
  36.7 0.8 %collective-permute-done.15.refs_1_ = bf16[128,256]{1,0:T(8,128)(2,1)S(1)} collective-permute-done((bf16[128,256]{1,0:T(8,128)(2,1)S(1)}, bf16[128,256]{1,0:T(8,128)(2,1)S(1)}, u32[]{:S(2)}, u32[]{:S(2)}) %collective-permute-start.15) | collective-permute-done | bytes 65568 | tf_op jit(solution)/shard_map/ppermute | solution.py:91
  37.5 2.3 %collective-permute-done.16.refs_2_ = bf16[128,256]{1,0:T(8,128)(2,1)S(1)} collective-permute-done((bf16[128,256]{1,0:T(8,128)(2,1)S(1)}, bf16[128,256]{1,0:T(8,128)(2,1)S(1)}, u32[]{:S(2)}, u32[]{:S(2)}) %collective-permute-start.16) | collective-permute-done | bytes 65568 | tf_op jit(solution)/shard_map/ppermute | solution.py:91
  39.9 1.9 %collective-permute-done.17.refs_3_ = bf16[128,256]{1,0:T(8,128)(2,1)S(1)} collective-permute-done((bf16[128,256]{1,0:T(8,128)(2,1)S(1)}, bf16[128,256]{1,0:T(8,128)(2,1)S(1)}, u32[]{:S(2)}, u32[]{:S(2)}) %collective-permute-start.17) | collective-permute-done | bytes 65568 | tf_op jit(solution)/shard_map/ppermute | solution.py:91
  41.8 2.7 %collective-permute-start.18 = (bf16[128,256]{1,0:T(8,128)(2,1)S(1)}, bf16[128,256]{1,0:T(8,128)(2,1)S(1)}, u32[]{:S(2)}, u32[]{:S(2)}) collective-permute-start(bf16[128,256]{1,0:T(8,128)(2,1)S(1)} %shard_map.134.refs_0_), channel_id=1, source_target_pairs={{0,16},{4,20},{8,24},{12,28},{16,0},{20,4},{24,8},{28,12},{1,17},{... | collective-permute-start | bytes 196616 | tf_op jit(solution)/shard_map/ppermute | solution.py:91
  44.5 3.1 %collective-permute-done.18.refs_1_ = bf16[128,256]{1,0:T(8,128)(2,1)S(1)} collective-permute-done((bf16[128,256]{1,0:T(8,128)(2,1)S(1)}, bf16[128,256]{1,0:T(8,128)(2,1)S(1)}, u32[]{:S(2)}, u32[]{:S(2)}) %collective-permute-start.18) | collective-permute-done | bytes 65568 | tf_op jit(solution)/shard_map/ppermute | solution.py:91
  47.7 0.7 %collective-permute-start.19 = (bf16[128,256]{1,0:T(8,128)(2,1)S(1)}, bf16[128,256]{1,0:T(8,128)(2,1)S(1)}, u32[]{:S(2)}, u32[]{:S(2)}) collective-permute-start(bf16[128,256]{1,0:T(8,128)(2,1)S(1)} %shard_map.135.refs_0_), channel_id=1, source_target_pairs={{0,4},{4,0},{8,12},{12,8},{16,20},{20,16},{24,28},{28,24},{1,5},{5... | collective-permute-start | bytes 196616 | tf_op jit(solution)/shard_map/ppermute | solution.py:91
  48.4 0.5 collective-permute-start.20
  48.8 2.4 %collective-permute-start.21 = (bf16[128,256]{1,0:T(8,128)(2,1)S(1)}, bf16[128,256]{1,0:T(8,128)(2,1)S(1)}, u32[]{:S(2)}, u32[]{:S(2)}) collective-permute-start(bf16[128,256]{1,0:T(8,128)(2,1)S(1)} %shard_map.135.refs_0_), channel_id=1, source_target_pairs={{0,12},{4,8},{8,4},{12,0},{16,28},{20,24},{24,20},{28,16},{1,13},{... | collective-permute-start | bytes 196616 | tf_op jit(solution)/shard_map/ppermute | solution.py:91
  51.2 0.8 %collective-permute-done.19.refs_1_ = bf16[128,256]{1,0:T(8,128)(2,1)S(1)} collective-permute-done((bf16[128,256]{1,0:T(8,128)(2,1)S(1)}, bf16[128,256]{1,0:T(8,128)(2,1)S(1)}, u32[]{:S(2)}, u32[]{:S(2)}) %collective-permute-start.19) | collective-permute-done | bytes 65568 | tf_op jit(solution)/shard_map/ppermute | solution.py:91
  52.0 0.6 %collective-permute-done.20.refs_2_ = bf16[128,256]{1,0:T(8,128)(2,1)S(1)} collective-permute-done((bf16[128,256]{1,0:T(8,128)(2,1)S(1)}, bf16[128,256]{1,0:T(8,128)(2,1)S(1)}, u32[]{:S(2)}, u32[]{:S(2)}) %collective-permute-start.20) | collective-permute-done | bytes 65568 | tf_op jit(solution)/shard_map/ppermute | solution.py:91
  52.6 1.5 %collective-permute-done.21.refs_3_ = bf16[128,256]{1,0:T(8,128)(2,1)S(1)} collective-permute-done((bf16[128,256]{1,0:T(8,128)(2,1)S(1)}, bf16[128,256]{1,0:T(8,128)(2,1)S(1)}, u32[]{:S(2)}, u32[]{:S(2)}) %collective-permute-start.21) | collective-permute-done | bytes 65568 | tf_op jit(solution)/shard_map/ppermute | solution.py:91
  54.2 0.8 %shard_map.136 = f32[512,256]{1,0:T(8,128)} custom-call(bf16[128,256]{1,0:T(8,128)(2,1)S(1)} %shard_map.135.refs_0_, bf16[128,256]{1,0:T(8,128)(2,1)S(1)} %collective-permute-done.19.refs_1_, bf16[128,256]{1,0:T(8,128)(2,1)S(1)} %collective-permute-done.20.refs_2_, bf16[128,256]{1,0:T(8,128)(2,1)S(1)} %collective-permute-done.21.refs_3_), custom_call_target="tpu_custom_call" | custom-call | tf_op jit(solution)/shard_map/pallas_call | solution.py:38
  55.0 2.4 %shard_map.132 = (bf16[128,512]{1,0:T(8,128)(2,1)}, bf16[128,512]{1,0:T(8,128)(2,1)}) custom-call(s32[1]{0:T(128)S(6)} %copy.14.refs_0_, bf16[128,512]{1,0:T(8,128)(2,1)S(1)} %get-tuple-element.27.refs_2_.refs_1_, bf16[128,512]{1,0:T(8,128)(2,1)S(1)} %get-tuple-element.28.refs_4_.refs_6_.refs_2_, bf16[128,1024]{1,0:T(8,128)(2,1)S(1)} %get-tuple-element.35.refs_3_, ...), custom_call_target="tpu_custom_call" | custom-call | flops 268435456 | tf_op jit(solution)/shard_map/pallas_call | solution.py:38
  (28 shorter events, 0.9 us)
Async XLA Ops:
  0.6 7.6 %collective-permute-start.1 = (bf16[128,512]{1,0:T(8,128)(2,1)}, bf16[128,512]{1,0:T(8,128)(2,1)S(1)}, u32[]{:S(2)}, u32[]{:S(2)}) collective-permute-start(bf16[128,512]{1,0:T(8,128)(2,1)} %refs_1_.1), channel_id=1, source_target_pairs={{0,2},{1,3},{2,0},{3,1},{4,6},{5,7},{6,4},{7,5},{8,10},{9,11},{10,... | collective-permute-start | bytes 393224 | tf_op jit(solution)/shard_map/ppermute | solution.py:71
  3.7 6.5 %collective-permute-start.4 = (bf16[128,512]{1,0:T(8,128)(2,1)}, bf16[128,512]{1,0:T(8,128)(2,1)S(1)}, u32[]{:S(2)}, u32[]{:S(2)}) collective-permute-start(bf16[128,512]{1,0:T(8,128)(2,1)} %refs_2_.1), channel_id=1, source_target_pairs={{0,2},{1,3},{2,0},{3,1},{4,6},{5,7},{6,4},{7,5},{8,10},{9,11},{10,... | collective-permute-start | bytes 393224 | tf_op jit(solution)/shard_map/ppermute | solution.py:71
  3.7 8.4 %collective-permute-start = (bf16[128,512]{1,0:T(8,128)(2,1)}, bf16[128,512]{1,0:T(8,128)(2,1)S(1)}, u32[]{:S(2)}, u32[]{:S(2)}) collective-permute-start(bf16[128,512]{1,0:T(8,128)(2,1)} %refs_1_.1), channel_id=1, source_target_pairs={{0,1},{1,0},{2,3},{3,2},{4,5},{5,4},{6,7},{7,6},{8,9},{9,8},{10,11... | collective-permute-start | bytes 393224 | tf_op jit(solution)/shard_map/ppermute | solution.py:71
  3.7 8.4 %collective-permute-start.3 = (bf16[128,512]{1,0:T(8,128)(2,1)}, bf16[128,512]{1,0:T(8,128)(2,1)S(1)}, u32[]{:S(2)}, u32[]{:S(2)}) collective-permute-start(bf16[128,512]{1,0:T(8,128)(2,1)} %refs_2_.1), channel_id=1, source_target_pairs={{0,1},{1,0},{2,3},{3,2},{4,5},{5,4},{6,7},{7,6},{8,9},{9,8},{10,11... | collective-permute-start | bytes 393224 | tf_op jit(solution)/shard_map/ppermute | solution.py:71
  8.2 5.2 %collective-permute-start.2 = (bf16[128,512]{1,0:T(8,128)(2,1)S(1)}, bf16[128,512]{1,0:T(8,128)(2,1)S(1)}, u32[]{:S(2)}, u32[]{:S(2)}) collective-permute-start(bf16[128,512]{1,0:T(8,128)(2,1)S(1)} %collective-permute-done.1.refs_2_.refs_4_), channel_id=1, source_target_pairs={{0,1},{1,0},{2,3},{3,2},{4,5},{5,4},{6,7},{7,6},{8,9},{9,8},{10,11... | collective-permute-start | bytes 393224 | tf_op jit(solution)/shard_map/ppermute | solution.py:71
  10.2 3.2 %collective-permute-start.5 = (bf16[128,512]{1,0:T(8,128)(2,1)S(1)}, bf16[128,512]{1,0:T(8,128)(2,1)S(1)}, u32[]{:S(2)}, u32[]{:S(2)}) collective-permute-start(bf16[128,512]{1,0:T(8,128)(2,1)S(1)} %collective-permute-done.4.refs_3_.refs_8_), channel_id=1, source_target_pairs={{0,1},{1,0},{2,3},{3,2},{4,5},{5,4},{6,7},{7,6},{8,9},{9,8},{10,11... | collective-permute-start | bytes 393224 | tf_op jit(solution)/shard_map/ppermute | solution.py:71
  12.1 1.3 %copy-start.2 = (f32[512]{0:T(512)S(1)}, f32[512]{0:T(512)}, u32[]{:S(2)}) copy-start(f32[512]{0:T(512)} %param.14) | copy-start | bytes 6148
  12.8 1.4 %copy-start = (bf16[512,1024]{1,0:T(8,128)(2,1)S(1)}, bf16[512,1024]{1,0:T(8,128)(2,1)}, u32[]{:S(2)}) copy-start(bf16[512,1024]{1,0:T(8,128)(2,1)} %refs_16_.1) | copy-start | bytes 3145732
  13.4 1.0 %copy-start.1 = (bf16[128,1024]{1,0:T(8,128)(2,1)S(1)}, bf16[128,1024]{1,0:T(8,128)(2,1)}, u32[]{:S(2)}) copy-start(bf16[128,1024]{1,0:T(8,128)(2,1)} %refs_12_.1) | copy-start | bytes 786436
  17.2 14.8 %collective-permute-start.7 = (bf16[128,1024]{1,0:T(8,128)(2,1)S(1)}, bf16[128,1024]{1,0:T(8,128)(2,1)S(1)}, u32[]{:S(2)}, u32[]{:S(2)}) collective-permute-start(bf16[128,1024]{1,0:T(8,128)(2,1)S(1)} %get-tuple-element.35.refs_3_), channel_id=1, source_target_pairs={{0,2},{1,3},{2,0},{3,1},{4,6},{5,7},{6,4},{7,5},{8,10},{9,11},{10,... | collective-permute-start | bytes 786440 | tf_op jit(solution)/shard_map/ppermute | solution.py:71
  18.9 10.2 %collective-permute-start.13 = (bf16[128,512]{1,0:T(8,128)(2,1)S(1)}, bf16[128,512]{1,0:T(8,128)(2,1)S(1)}, u32[]{:S(2)}, u32[]{:S(2)}) collective-permute-start(bf16[128,512]{1,0:T(8,128)(2,1)S(1)} %get-tuple-element.41), channel_id=1, source_target_pairs={{0,2},{1,3},{2,0},{3,1},{4,6},{5,7},{6,4},{7,5},{8,10},{9,11},{10,... | collective-permute-start | bytes 393224 | tf_op jit(solution)/shard_map/ppermute | solution.py:71
  19.2 12.3 %collective-permute-start.10 = (bf16[512,128]{1,0:T(8,128)(2,1)S(1)}, bf16[512,128]{1,0:T(8,128)(2,1)S(1)}, u32[]{:S(2)}, u32[]{:S(2)}) collective-permute-start(bf16[512,128]{1,0:T(8,128)(2,1)S(1)} %get-tuple-element.39.refs_0_), channel_id=1, source_target_pairs={{0,2},{1,3},{2,0},{3,1},{4,6},{5,7},{6,4},{7,5},{8,10},{9,11},{10,... | collective-permute-start | bytes 393224 | tf_op jit(solution)/shard_map/ppermute | solution.py:71
  20.9 10.6 %collective-permute-start.12 = (bf16[128,512]{1,0:T(8,128)(2,1)S(1)}, bf16[128,512]{1,0:T(8,128)(2,1)S(1)}, u32[]{:S(2)}, u32[]{:S(2)}) collective-permute-start(bf16[128,512]{1,0:T(8,128)(2,1)S(1)} %get-tuple-element.40.refs_4_), channel_id=1, source_target_pairs={{0,1},{1,0},{2,3},{3,2},{4,5},{5,4},{6,7},{7,6},{8,9},{9,8},{10,11... | collective-permute-start | bytes 393224 | tf_op jit(solution)/shard_map/ppermute | solution.py:71
  29.1 2.9 %collective-permute-start.14 = (bf16[128,512]{1,0:T(8,128)(2,1)S(1)}, bf16[128,512]{1,0:T(8,128)(2,1)S(1)}, u32[]{:S(2)}, u32[]{:S(2)}) collective-permute-start(bf16[128,512]{1,0:T(8,128)(2,1)S(1)} %collective-permute-done.13.refs_6_), channel_id=1, source_target_pairs={{0,1},{1,0},{2,3},{3,2},{4,5},{5,4},{6,7},{7,6},{8,9},{9,8},{10,11... | collective-permute-start | bytes 393224 | tf_op jit(solution)/shard_map/ppermute | solution.py:71
  29.1 2.9 %collective-permute-start.9 = (bf16[512,128]{1,0:T(8,128)(2,1)S(1)}, bf16[512,128]{1,0:T(8,128)(2,1)S(1)}, u32[]{:S(2)}, u32[]{:S(2)}) collective-permute-start(bf16[512,128]{1,0:T(8,128)(2,1)S(1)} %get-tuple-element.39.refs_0_), channel_id=1, source_target_pairs={{0,1},{1,0},{2,3},{3,2},{4,5},{5,4},{6,7},{7,6},{8,9},{9,8},{10,11... | collective-permute-start | bytes 393224 | tf_op jit(solution)/shard_map/ppermute | solution.py:71
  31.5 1.3 %collective-permute-start.11 = (bf16[512,128]{1,0:T(8,128)(2,1)S(1)}, bf16[512,128]{1,0:T(8,128)(2,1)S(1)}, u32[]{:S(2)}, u32[]{:S(2)}) collective-permute-start(bf16[512,128]{1,0:T(8,128)(2,1)S(1)} %collective-permute-done.10.refs_2_), channel_id=1, source_target_pairs={{0,1},{1,0},{2,3},{3,2},{4,5},{5,4},{6,7},{7,6},{8,9},{9,8},{10,11... | collective-permute-start | bytes 393224 | tf_op jit(solution)/shard_map/ppermute | solution.py:71
  31.5 23.5 %collective-permute-start.6 = (bf16[128,1024]{1,0:T(8,128)(2,1)S(1)}, bf16[128,1024]{1,0:T(8,128)(2,1)S(1)}, u32[]{:S(2)}, u32[]{:S(2)}) collective-permute-start(bf16[128,1024]{1,0:T(8,128)(2,1)S(1)} %get-tuple-element.35.refs_3_), channel_id=1, source_target_pairs={{0,1},{1,0},{2,3},{3,2},{4,5},{5,4},{6,7},{7,6},{8,9},{9,8},{10,11... | collective-permute-start | bytes 786440 | tf_op jit(solution)/shard_map/ppermute | solution.py:71
  32.0 23.0 %collective-permute-start.8 = (bf16[128,1024]{1,0:T(8,128)(2,1)S(1)}, bf16[128,1024]{1,0:T(8,128)(2,1)S(1)}, u32[]{:S(2)}, u32[]{:S(2)}) collective-permute-start(bf16[128,1024]{1,0:T(8,128)(2,1)S(1)} %collective-permute-done.7.refs_5_), channel_id=1, source_target_pairs={{0,1},{1,0},{2,3},{3,2},{4,5},{5,4},{6,7},{7,6},{8,9},{9,8},{10,11... | collective-permute-start | bytes 786440 | tf_op jit(solution)/shard_map/ppermute | solution.py:71
  33.2 4.3 %collective-permute-start.15 = (bf16[128,256]{1,0:T(8,128)(2,1)S(1)}, bf16[128,256]{1,0:T(8,128)(2,1)S(1)}, u32[]{:S(2)}, u32[]{:S(2)}) collective-permute-start(bf16[128,256]{1,0:T(8,128)(2,1)S(1)} %get-tuple-element.43), channel_id=1, source_target_pairs={{0,4},{4,0},{8,12},{12,8},{16,20},{20,16},{24,28},{28,24},{1,5},{5... | collective-permute-start | bytes 196616 | tf_op jit(solution)/shard_map/ppermute | solution.py:91
  35.0 4.8 %collective-permute-start.16 = (bf16[128,256]{1,0:T(8,128)(2,1)S(1)}, bf16[128,256]{1,0:T(8,128)(2,1)S(1)}, u32[]{:S(2)}, u32[]{:S(2)}) collective-permute-start(bf16[128,256]{1,0:T(8,128)(2,1)S(1)} %get-tuple-element.44), channel_id=1, source_target_pairs={{0,8},{4,12},{8,0},{12,4},{16,24},{20,28},{24,16},{28,20},{1,9},{5... | collective-permute-start | bytes 196616 | tf_op jit(solution)/shard_map/ppermute | solution.py:91
  36.6 5.2 %collective-permute-start.17 = (bf16[128,256]{1,0:T(8,128)(2,1)S(1)}, bf16[128,256]{1,0:T(8,128)(2,1)S(1)}, u32[]{:S(2)}, u32[]{:S(2)}) collective-permute-start(bf16[128,256]{1,0:T(8,128)(2,1)S(1)} %get-tuple-element.45), channel_id=1, source_target_pairs={{0,12},{4,8},{8,4},{12,0},{16,28},{20,24},{24,20},{28,16},{1,13},{... | collective-permute-start | bytes 196616 | tf_op jit(solution)/shard_map/ppermute | solution.py:91
  41.8 5.8 %collective-permute-start.18 = (bf16[128,256]{1,0:T(8,128)(2,1)S(1)}, bf16[128,256]{1,0:T(8,128)(2,1)S(1)}, u32[]{:S(2)}, u32[]{:S(2)}) collective-permute-start(bf16[128,256]{1,0:T(8,128)(2,1)S(1)} %shard_map.134.refs_0_), channel_id=1, source_target_pairs={{0,16},{4,20},{8,24},{12,28},{16,0},{20,4},{24,8},{28,12},{1,17},{... | collective-permute-start | bytes 196616 | tf_op jit(solution)/shard_map/ppermute | solution.py:91
  47.7 4.3 %collective-permute-start.19 = (bf16[128,256]{1,0:T(8,128)(2,1)S(1)}, bf16[128,256]{1,0:T(8,128)(2,1)S(1)}, u32[]{:S(2)}, u32[]{:S(2)}) collective-permute-start(bf16[128,256]{1,0:T(8,128)(2,1)S(1)} %shard_map.135.refs_0_), channel_id=1, source_target_pairs={{0,4},{4,0},{8,12},{12,8},{16,20},{20,16},{24,28},{28,24},{1,5},{5... | collective-permute-start | bytes 196616 | tf_op jit(solution)/shard_map/ppermute | solution.py:91
  48.4 4.3 %collective-permute-start.20 = (bf16[128,256]{1,0:T(8,128)(2,1)S(1)}, bf16[128,256]{1,0:T(8,128)(2,1)S(1)}, u32[]{:S(2)}, u32[]{:S(2)}) collective-permute-start(bf16[128,256]{1,0:T(8,128)(2,1)S(1)} %shard_map.135.refs_0_), channel_id=1, source_target_pairs={{0,8},{4,12},{8,0},{12,4},{16,24},{20,28},{24,16},{28,20},{1,9},{5... | collective-permute-start | bytes 196616 | tf_op jit(solution)/shard_map/ppermute | solution.py:91
  48.8 5.3 %collective-permute-start.21 = (bf16[128,256]{1,0:T(8,128)(2,1)S(1)}, bf16[128,256]{1,0:T(8,128)(2,1)S(1)}, u32[]{:S(2)}, u32[]{:S(2)}) collective-permute-start(bf16[128,256]{1,0:T(8,128)(2,1)S(1)} %shard_map.135.refs_0_), channel_id=1, source_target_pairs={{0,12},{4,8},{8,4},{12,0},{16,28},{20,24},{24,20},{28,16},{1,13},{... | collective-permute-start | bytes 196616 | tf_op jit(solution)/shard_map/ppermute | solution.py:91

commit v6 on v5

--- a/solution.py
+++ b/solution.py
@@ -256,10 +256,11 @@
         dq_ref[:, cols] = (one_pair(acc) * HALF_SCALE).astype(BF16)
 
 
-def key_kernel(lanes, *refs):
+def key_kernel(lanes, blocks, *refs):
     len_ref, k_ref, v_ref = refs[:3]
-    gq_refs = refs[3 : 3 + lanes]
-    dk_ref, dv_ref = refs[3 + lanes :]
+    count = len(blocks)
+    gq_refs = dict(zip(blocks, refs[3 : 3 + count]))
+    before, outs = refs[3 + count : -2], refs[-2:]
     length = len_ref[0]
     rows, feats = k_ref.shape
     pos = lax.axis_index("blk")
@@ -269,21 +270,23 @@
         val = two_heads(v_ref[:, cols])
         q_cols = slice(feats + p * PAIR, feats + (p + 1) * PAIR)
         dk = dv = None
-        for blocks in tiles(range(lanes)):
-            queries = stack(gq_refs, blocks, q_cols)
-            grads = stack(gq_refs, blocks, cols)
+        for some in tiles(blocks):
+            queries = stack(gq_refs, some, q_cols)
+            grads = stack(gq_refs, some, cols)
             half = dot(lhs, queries, NT)
             prob_grad = dot(val, grads, NT)
-            where = places(blocks, lanes, rows)
-            where = jnp.where(where < length, where, -1)
-            live = mine <= where
+            where = places(some, lanes, rows)
+            live = mine <= jnp.where(where < length, where, -1)
             weight, slope = weight_and_slope(half, live)
             score_grad = (prob_grad * slope).astype(BF16)
             part_k, part_v = dot(score_grad, queries), dot(weight.astype(BF16), grads)
             dk = part_k if dk is None else dk + part_k
             dv = part_v if dv is None else dv + part_v
-        dk_ref[:, cols] = (one_pair(dk) * HALF_SCALE).astype(BF16)
-        dv_ref[:, cols] = one_pair(dv).astype(BF16)
+        for out, grad, ref, scale in zip(outs, (dk, dv), before or (None, None), (HALF_SCALE, 1.0)):
+            grad = one_pair(grad)
+            if ref is not None:
+                grad = grad + ref[:, cols]
+            out[:, cols] = grad if out.dtype == F32 else (grad * scale).astype(out.dtype)
 
 
 def split(total_ref, digit, keep_ref, send_refs):
@@ -439,16 +442,23 @@
         flops=attention_flops + 4 * rows * feats * model,
     )
     grads = cores([grads_queries] + cross(grads_queries))
-    grad_key, grad_value = call(
-        functools.partial(key_kernel, lanes),
-        [((rows, feats), BF16), ((rows, feats), BF16)],
-        lengths,
-        key_here,
-        value_here,
-        *grads,
-        scalars=1,
-        flops=2 * attention_flops,
-    )
+
+    def key_share(blocks, kind, *before):
+        return call(
+            functools.partial(key_kernel, lanes, blocks),
+            [((rows, feats), kind)] * 2,
+            lengths,
+            key_here,
+            value_here,
+            *(grads[n] for n in blocks),
+            *before,
+            scalars=1,
+            flops=2 * attention_flops * len(blocks) // lanes,
+        )
+
+    here, away = list(range(CORES)), list(range(CORES, lanes))
+    shares = key_share(here, F32) if away else []
+    grad_key, grad_value = key_share(away or here, BF16, *shares)
 
     stages = digits(groups)
     size = feats

time: 57.6 us -> 56.9 us (0.988)
  waiting for transfers between devices: 27.9 us -> 26.8 us
    ppermute x7, waiting for transfers between devices: 11.1 us -> 10 us  [over_digit(): return lax.ppermute(x, 'grp', pairs)]
    pallas_call x10 -> x11, Pallas kernels: 9.65 us -> 10.1 us  [call(): pl.pallas_call(kernel, out_shape=[jax.ShapeDtypeStruct(s, d) for s, d in...]
  transfers between devices with their start and end apart: 22 -> 22, of which waited for: 12 -> 11; matrix products, arithmetic and copies ran while one was open for 0% -> 0% of each run, Pallas kernels for 7% -> 8%
where the time goes in v6:
time: 56.9 us; the launch traced here: 56.8 us
  waiting for transfers between devices  26.8 us (47%)
  starting transfers between devices  18.2 us (32%)
  Pallas kernels  10.1 us (18%)
  between operations  1.44 us (3%)
    ppermute x15, waiting for transfers between devices, over_blk(): return lax.ppermute(x, 'blk', pairs)  16.8 us
    pallas_call x11, Pallas kernels, call(): pl.pallas_call(kernel, out_shape=[jax.ShapeDtypeStruct(s, d) for s, d in...  10.1 us
    ppermute x7, waiting for transfers between devices, over_digit(): return lax.ppermute(x, 'grp', pairs)  10 us
    ppermute x7, starting transfers between devices, over_digit(): return lax.ppermute(x, 'grp', pairs)  9.76 us
    ppermute x15, starting transfers between devices, over_blk(): return lax.ppermute(x, 'blk', pairs)  8.49 us
  transfers between devices with their start and end apart: 22, of which 11 were waited for; matrix products, arithmetic and copies ran while one was open for 0% of the time, Pallas kernels for 8%

profile of v6, /device:TPU:0, one launch (start us, length us, event | category | flops | bytes accessed | tf_op | source)
XLA Modules:
  0.0 56.8 jit_solution(5502621691417000580)
XLA Ops:
  0.6 3.0 %collective-permute-start.1 = (bf16[128,512]{1,0:T(8,128)(2,1)}, bf16[128,512]{1,0:T(8,128)(2,1)S(1)}, u32[]{:S(2)}, u32[]{:S(2)}) collective-permute-start(bf16[128,512]{1,0:T(8,128)(2,1)} %refs_1_.1), channel_id=1, source_target_pairs={{0,2},{1,3},{2,0},{3,1},{4,6},{5,7},{6,4},{7,5},{8,10},{9,11},{10,... | collective-permute-start | bytes 393224 | tf_op jit(solution)/shard_map/ppermute | solution.py:71
  3.7 0.5 collective-permute-start.3
  4.3 4.0 %collective-permute-done.1.refs_2_.refs_4_ = bf16[128,512]{1,0:T(8,128)(2,1)S(1)} collective-permute-done((bf16[128,512]{1,0:T(8,128)(2,1)}, bf16[128,512]{1,0:T(8,128)(2,1)S(1)}, u32[]{:S(2)}, u32[]{:S(2)}) %collective-permute-start.1) | collective-permute-done | bytes 131104 | tf_op jit(solution)/shard_map/ppermute | solution.py:71
  8.2 2.0 %collective-permute-done.4.refs_3_.refs_8_ = bf16[128,512]{1,0:T(8,128)(2,1)S(1)} collective-permute-done((bf16[128,512]{1,0:T(8,128)(2,1)}, bf16[128,512]{1,0:T(8,128)(2,1)S(1)}, u32[]{:S(2)}, u32[]{:S(2)}) %collective-permute-start.4) | collective-permute-done | bytes 131104 | tf_op jit(solution)/shard_map/ppermute | solution.py:71
  10.8 1.3 %shard_map.127 = (bf16[128,512]{1,0:T(8,128)(2,1)S(1)}, bf16[128,512]{1,0:T(8,128)(2,1)S(1)}, bf16[128,512]{1,0:T(8,128)(2,1)S(1)}, bf16[128,512]{1,0:T(8,128)(2...) custom-call(bf16[128,1024]{1,0:T(8,128)(2,1)} %refs_12_.1, bf16[128,512]{1,0:T(8,128)(2,1)} %refs_0_.7, ...), custom_call_target="tpu_custom_call" | custom-call | tf_op jit(solution)/shard_map/pallas_call | solution.py:38
  12.1 0.7 %shard_map.128.refs_4_ = f32[128,512]{1,0:T(8,128)S(1)} custom-call(s32[1]{0:T(128)S(6)} %copy.14.refs_0_, bf16[128,512]{1,0:T(8,128)(2,1)S(1)} %get-tuple-element.28.refs_1_, bf16[128,512]{1,0:T(8,128)(2,1)S(1)} %get-tuple-element.29.refs_2_.refs_1_, bf16[128,512]{1,0:T(8,128)(2,1)S(1)} %collective-permute-done.refs_3_, ...), custom_call_target="tpu_custom_call" | custom-call | flops 67108864 | tf_op jit(solution)/shard_map/pallas_call | solution.py:38
  12.8 0.5 shard_map.129.refs_4_
  13.4 0.8 %shard_map.130 = (bf16[128,512]{1,0:T(8,128)(2,1)S(1)}, bf16[512,128]{1,0:T(8,128)(2,1)S(1)}, f32[128,512]{1,0:T(8,128)S(1)}, f32[128,128]{1,0:T(8,128)S(1)}) custom-call(s32[1]{0:T(128)S(6)} %copy.14.refs_0_, bf16[128,512]{1,0:T(8,128)(2,1)S(1)} %get-tuple-element.28.refs_1_, bf16[128,512]{1,0:T(8,128)(2,1)S(1)} %collective-permute-done.2.refs_2_.refs_5_, ...), custom_call_target="tpu_custom_call" | custom-call | flops 33554432 | tf_op jit(solution)/shard_map/pallas_call | solution.py:38
  14.4 2.7 %shard_map.131 = (bf16[128,1024]{1,0:T(8,128)(2,1)}, bf16[128,512]{1,0:T(8,128)(2,1)}, bf16[128,512]{1,0:T(8,128)(2,1)}, bf16[128,1024]{1,0:T(8,128)(2,1)S(1)}) custom-call(s32[1]{0:T(128)S(6)} %copy.14.refs_0_, bf16[128,512]{1,0:T(8,128)(2,1)S(1)} %get-tuple-element.28.refs_1_, bf16[128,512]{1,0:T(8,128)(2,1)S(1)} %get-tuple-element.29.refs_2_.refs_1_, ...), custom_call_target="tpu_custom_call" | custom-call | flops 402653184 | tf_op jit(solution)/shard_map/pallas_call | solution.py:38
  17.1 1.7 %collective-permute-start.6 = (bf16[128,1024]{1,0:T(8,128)(2,1)S(1)}, bf16[128,1024]{1,0:T(8,128)(2,1)S(1)}, u32[]{:S(2)}, u32[]{:S(2)}) collective-permute-start(bf16[128,1024]{1,0:T(8,128)(2,1)S(1)} %get-tuple-element.37.refs_3_), channel_id=1, source_target_pairs={{0,2},{1,3},{2,0},{3,1},{4,6},{5,7},{6,4},{7,5},{8,10},{9,11},{10,... | collective-permute-start | bytes 786440 | tf_op jit(solution)/shard_map/ppermute | solution.py:71
  19.2 1.7 %collective-permute-start.10 = (bf16[512,128]{1,0:T(8,128)(2,1)S(1)}, bf16[512,128]{1,0:T(8,128)(2,1)S(1)}, u32[]{:S(2)}, u32[]{:S(2)}) collective-permute-start(bf16[512,128]{1,0:T(8,128)(2,1)S(1)} %get-tuple-element.43.refs_0_), channel_id=1, source_target_pairs={{0,2},{1,3},{2,0},{3,1},{4,6},{5,7},{6,4},{7,5},{8,10},{9,11},{10,... | collective-permute-start | bytes 393224 | tf_op jit(solution)/shard_map/ppermute | solution.py:71
  20.9 8.2 %collective-permute-done.13.refs_6_ = bf16[128,512]{1,0:T(8,128)(2,1)S(1)} collective-permute-done((bf16[128,512]{1,0:T(8,128)(2,1)S(1)}, bf16[128,512]{1,0:T(8,128)(2,1)S(1)}, u32[]{:S(2)}, u32[]{:S(2)}) %collective-permute-start.13) | collective-permute-done | bytes 131104 | tf_op jit(solution)/shard_map/ppermute | solution.py:71
  29.1 0.5 collective-permute-start.9
  29.6 1.8 %collective-permute-done.10.refs_2_ = bf16[512,128]{1,0:T(8,128)(2,1)S(1)} collective-permute-done((bf16[512,128]{1,0:T(8,128)(2,1)S(1)}, bf16[512,128]{1,0:T(8,128)(2,1)S(1)}, u32[]{:S(2)}, u32[]{:S(2)}) %collective-permute-start.10) | collective-permute-done | bytes 131104 | tf_op jit(solution)/shard_map/ppermute | solution.py:71
  31.5 0.5 collective-permute-start.8
  32.1 0.8 %collective-permute-done.11.refs_3_ = bf16[512,128]{1,0:T(8,128)(2,1)S(1)} collective-permute-done((bf16[512,128]{1,0:T(8,128)(2,1)S(1)}, bf16[512,128]{1,0:T(8,128)(2,1)S(1)}, u32[]{:S(2)}, u32[]{:S(2)}) %collective-permute-start.11) | collective-permute-done | bytes 131104 | tf_op jit(solution)/shard_map/ppermute | solution.py:71
  32.8 0.3 shard_map.134
  33.2 1.8 %collective-permute-start.15 = (bf16[128,256]{1,0:T(8,128)(2,1)S(1)}, bf16[128,256]{1,0:T(8,128)(2,1)S(1)}, u32[]{:S(2)}, u32[]{:S(2)}) collective-permute-start(bf16[128,256]{1,0:T(8,128)(2,1)S(1)} %get-tuple-element.47), channel_id=1, source_target_pairs={{0,4},{4,0},{8,12},{12,8},{16,20},{20,16},{24,28},{28,24},{1,5},{5... | collective-permute-start | bytes 196616 | tf_op jit(solution)/shard_map/ppermute | solution.py:91
  35.0 1.6 %collective-permute-start.16 = (bf16[128,256]{1,0:T(8,128)(2,1)S(1)}, bf16[128,256]{1,0:T(8,128)(2,1)S(1)}, u32[]{:S(2)}, u32[]{:S(2)}) collective-permute-start(bf16[128,256]{1,0:T(8,128)(2,1)S(1)} %get-tuple-element.48), channel_id=1, source_target_pairs={{0,8},{4,12},{8,0},{12,4},{16,24},{20,28},{24,16},{28,20},{1,9},{5... | collective-permute-start | bytes 196616 | tf_op jit(solution)/shard_map/ppermute | solution.py:91
  36.7 0.8 %collective-permute-done.15.refs_1_ = bf16[128,256]{1,0:T(8,128)(2,1)S(1)} collective-permute-done((bf16[128,256]{1,0:T(8,128)(2,1)S(1)}, bf16[128,256]{1,0:T(8,128)(2,1)S(1)}, u32[]{:S(2)}, u32[]{:S(2)}) %collective-permute-start.15) | collective-permute-done | bytes 65568 | tf_op jit(solution)/shard_map/ppermute | solution.py:91
  37.5 2.3 %collective-permute-done.16.refs_2_ = bf16[128,256]{1,0:T(8,128)(2,1)S(1)} collective-permute-done((bf16[128,256]{1,0:T(8,128)(2,1)S(1)}, bf16[128,256]{1,0:T(8,128)(2,1)S(1)}, u32[]{:S(2)}, u32[]{:S(2)}) %collective-permute-start.16) | collective-permute-done | bytes 65568 | tf_op jit(solution)/shard_map/ppermute | solution.py:91
  39.8 1.9 %collective-permute-done.17.refs_3_ = bf16[128,256]{1,0:T(8,128)(2,1)S(1)} collective-permute-done((bf16[128,256]{1,0:T(8,128)(2,1)S(1)}, bf16[128,256]{1,0:T(8,128)(2,1)S(1)}, u32[]{:S(2)}, u32[]{:S(2)}) %collective-permute-start.17) | collective-permute-done | bytes 65568 | tf_op jit(solution)/shard_map/ppermute | solution.py:91
  41.8 2.7 %collective-permute-start.18 = (bf16[128,256]{1,0:T(8,128)(2,1)S(1)}, bf16[128,256]{1,0:T(8,128)(2,1)S(1)}, u32[]{:S(2)}, u32[]{:S(2)}) collective-permute-start(bf16[128,256]{1,0:T(8,128)(2,1)S(1)} %shard_map.135.refs_0_), channel_id=1, source_target_pairs={{0,16},{4,20},{8,24},{12,28},{16,0},{20,4},{24,8},{28,12},{1,17},{... | collective-permute-start | bytes 196616 | tf_op jit(solution)/shard_map/ppermute | solution.py:91
  44.5 3.1 %collective-permute-done.18.refs_1_ = bf16[128,256]{1,0:T(8,128)(2,1)S(1)} collective-permute-done((bf16[128,256]{1,0:T(8,128)(2,1)S(1)}, bf16[128,256]{1,0:T(8,128)(2,1)S(1)}, u32[]{:S(2)}, u32[]{:S(2)}) %collective-permute-start.18) | collective-permute-done | bytes 65568 | tf_op jit(solution)/shard_map/ppermute | solution.py:91
  47.7 0.7 %collective-permute-start.19 = (bf16[128,256]{1,0:T(8,128)(2,1)S(1)}, bf16[128,256]{1,0:T(8,128)(2,1)S(1)}, u32[]{:S(2)}, u32[]{:S(2)}) collective-permute-start(bf16[128,256]{1,0:T(8,128)(2,1)S(1)} %shard_map.136.refs_0_), channel_id=1, source_target_pairs={{0,4},{4,0},{8,12},{12,8},{16,20},{20,16},{24,28},{28,24},{1,5},{5... | collective-permute-start | bytes 196616 | tf_op jit(solution)/shard_map/ppermute | solution.py:91
  48.3 0.5 collective-permute-start.20
  48.8 2.4 %collective-permute-start.21 = (bf16[128,256]{1,0:T(8,128)(2,1)S(1)}, bf16[128,256]{1,0:T(8,128)(2,1)S(1)}, u32[]{:S(2)}, u32[]{:S(2)}) collective-permute-start(bf16[128,256]{1,0:T(8,128)(2,1)S(1)} %shard_map.136.refs_0_), channel_id=1, source_target_pairs={{0,12},{4,8},{8,4},{12,0},{16,28},{20,24},{24,20},{28,16},{1,13},{... | collective-permute-start | bytes 196616 | tf_op jit(solution)/shard_map/ppermute | solution.py:91
  51.2 1.1 %shard_map.132 = (f32[128,512]{1,0:T(8,128)S(1)}, f32[128,512]{1,0:T(8,128)S(1)}) custom-call(s32[1]{0:T(128)S(6)} %copy.14.refs_0_, bf16[128,512]{1,0:T(8,128)(2,1)S(1)} %get-tuple-element.29.refs_2_.refs_1_, bf16[128,512]{1,0:T(8,128)(2,1)S(1)} %get-tuple-element.30.refs_4_.refs_6_.refs_2_, bf16[128,1024]{1,0:T(8,128)(2,1)S(1)} %get-tuple-element.37.refs_3_, ...), custom_call_target="tpu_custom_call" | custom-call | flops 134217728 | tf_op jit(solution)/shard_map/pallas_call | solution.py:38
  52.3 0.3 collective-permute-done.20.refs_2_
  52.6 1.5 %collective-permute-done.21.refs_3_ = bf16[128,256]{1,0:T(8,128)(2,1)S(1)} collective-permute-done((bf16[128,256]{1,0:T(8,128)(2,1)S(1)}, bf16[128,256]{1,0:T(8,128)(2,1)S(1)}, u32[]{:S(2)}, u32[]{:S(2)}) %collective-permute-start.21) | collective-permute-done | bytes 65568 | tf_op jit(solution)/shard_map/ppermute | solution.py:91
  54.1 0.8 %shard_map.137 = f32[512,256]{1,0:T(8,128)} custom-call(bf16[128,256]{1,0:T(8,128)(2,1)S(1)} %shard_map.136.refs_0_, bf16[128,256]{1,0:T(8,128)(2,1)S(1)} %collective-permute-done.19.refs_1_, bf16[128,256]{1,0:T(8,128)(2,1)S(1)} %collective-permute-done.20.refs_2_, bf16[128,256]{1,0:T(8,128)(2,1)S(1)} %collective-permute-done.21.refs_3_), custom_call_target="tpu_custom_call" | custom-call | tf_op jit(solution)/shard_map/pallas_call | solution.py:38
  55.0 1.8 %shard_map.133 = (bf16[128,512]{1,0:T(8,128)(2,1)}, bf16[128,512]{1,0:T(8,128)(2,1)}) custom-call(s32[1]{0:T(128)S(6)} %copy.14.refs_0_, bf16[128,512]{1,0:T(8,128)(2,1)S(1)} %get-tuple-element.29.refs_2_.refs_1_, bf16[128,512]{1,0:T(8,128)(2,1)S(1)} %get-tuple-element.30.refs_4_.refs_6_.refs_2_, bf16[128,1024]{1,0:T(8,128)(2,1)S(1)} %collective-permute-done.6.refs_3_, ...), custom_call_target="tpu_custom_call" | custom-call | flops 134217728 | tf_op jit(solution)/shard_map/pallas_call | solution.py:38
  (29 shorter events, 0.9 us)
Async XLA Ops:
  0.6 7.6 %collective-permute-start.1 = (bf16[128,512]{1,0:T(8,128)(2,1)}, bf16[128,512]{1,0:T(8,128)(2,1)S(1)}, u32[]{:S(2)}, u32[]{:S(2)}) collective-permute-start(bf16[128,512]{1,0:T(8,128)(2,1)} %refs_1_.1), channel_id=1, source_target_pairs={{0,2},{1,3},{2,0},{3,1},{4,6},{5,7},{6,4},{7,5},{8,10},{9,11},{10,... | collective-permute-start | bytes 393224 | tf_op jit(solution)/shard_map/ppermute | solution.py:71
  3.7 6.5 %collective-permute-start.4 = (bf16[128,512]{1,0:T(8,128)(2,1)}, bf16[128,512]{1,0:T(8,128)(2,1)S(1)}, u32[]{:S(2)}, u32[]{:S(2)}) collective-permute-start(bf16[128,512]{1,0:T(8,128)(2,1)} %refs_2_.1), channel_id=1, source_target_pairs={{0,2},{1,3},{2,0},{3,1},{4,6},{5,7},{6,4},{7,5},{8,10},{9,11},{10,... | collective-permute-start | bytes 393224 | tf_op jit(solution)/shard_map/ppermute | solution.py:71
  3.7 8.4 %collective-permute-start = (bf16[128,512]{1,0:T(8,128)(2,1)}, bf16[128,512]{1,0:T(8,128)(2,1)S(1)}, u32[]{:S(2)}, u32[]{:S(2)}) collective-permute-start(bf16[128,512]{1,0:T(8,128)(2,1)} %refs_1_.1), channel_id=1, source_target_pairs={{0,1},{1,0},{2,3},{3,2},{4,5},{5,4},{6,7},{7,6},{8,9},{9,8},{10,11... | collective-permute-start | bytes 393224 | tf_op jit(solution)/shard_map/ppermute | solution.py:71
  3.7 8.4 %collective-permute-start.3 = (bf16[128,512]{1,0:T(8,128)(2,1)}, bf16[128,512]{1,0:T(8,128)(2,1)S(1)}, u32[]{:S(2)}, u32[]{:S(2)}) collective-permute-start(bf16[128,512]{1,0:T(8,128)(2,1)} %refs_2_.1), channel_id=1, source_target_pairs={{0,1},{1,0},{2,3},{3,2},{4,5},{5,4},{6,7},{7,6},{8,9},{9,8},{10,11... | collective-permute-start | bytes 393224 | tf_op jit(solution)/shard_map/ppermute | solution.py:71
  8.2 5.2 %collective-permute-start.2 = (bf16[128,512]{1,0:T(8,128)(2,1)S(1)}, bf16[128,512]{1,0:T(8,128)(2,1)S(1)}, u32[]{:S(2)}, u32[]{:S(2)}) collective-permute-start(bf16[128,512]{1,0:T(8,128)(2,1)S(1)} %collective-permute-done.1.refs_2_.refs_4_), channel_id=1, source_target_pairs={{0,1},{1,0},{2,3},{3,2},{4,5},{5,4},{6,7},{7,6},{8,9},{9,8},{10,11... | collective-permute-start | bytes 393224 | tf_op jit(solution)/shard_map/ppermute | solution.py:71
  10.2 3.2 %collective-permute-start.5 = (bf16[128,512]{1,0:T(8,128)(2,1)S(1)}, bf16[128,512]{1,0:T(8,128)(2,1)S(1)}, u32[]{:S(2)}, u32[]{:S(2)}) collective-permute-start(bf16[128,512]{1,0:T(8,128)(2,1)S(1)} %collective-permute-done.4.refs_3_.refs_8_), channel_id=1, source_target_pairs={{0,1},{1,0},{2,3},{3,2},{4,5},{5,4},{6,7},{7,6},{8,9},{9,8},{10,11... | collective-permute-start | bytes 393224 | tf_op jit(solution)/shard_map/ppermute | solution.py:71
  12.1 1.3 %copy-start.2 = (f32[512]{0:T(512)S(1)}, f32[512]{0:T(512)}, u32[]{:S(2)}) copy-start(f32[512]{0:T(512)} %param.14) | copy-start | bytes 6148
  12.8 1.4 %copy-start = (bf16[512,1024]{1,0:T(8,128)(2,1)S(1)}, bf16[512,1024]{1,0:T(8,128)(2,1)}, u32[]{:S(2)}) copy-start(bf16[512,1024]{1,0:T(8,128)(2,1)} %refs_16_.1) | copy-start | bytes 3145732
  13.4 1.0 %copy-start.1 = (bf16[128,1024]{1,0:T(8,128)(2,1)S(1)}, bf16[128,1024]{1,0:T(8,128)(2,1)}, u32[]{:S(2)}) copy-start(bf16[128,1024]{1,0:T(8,128)(2,1)} %refs_12_.1) | copy-start | bytes 786436
  17.1 14.9 %collective-permute-start.6 = (bf16[128,1024]{1,0:T(8,128)(2,1)S(1)}, bf16[128,1024]{1,0:T(8,128)(2,1)S(1)}, u32[]{:S(2)}, u32[]{:S(2)}) collective-permute-start(bf16[128,1024]{1,0:T(8,128)(2,1)S(1)} %get-tuple-element.37.refs_3_), channel_id=1, source_target_pairs={{0,2},{1,3},{2,0},{3,1},{4,6},{5,7},{6,4},{7,5},{8,10},{9,11},{10,... | collective-permute-start | bytes 786440 | tf_op jit(solution)/shard_map/ppermute | solution.py:71
  18.9 10.2 %collective-permute-start.13 = (bf16[128,512]{1,0:T(8,128)(2,1)S(1)}, bf16[128,512]{1,0:T(8,128)(2,1)S(1)}, u32[]{:S(2)}, u32[]{:S(2)}) collective-permute-start(bf16[128,512]{1,0:T(8,128)(2,1)S(1)} %get-tuple-element.45), channel_id=1, source_target_pairs={{0,2},{1,3},{2,0},{3,1},{4,6},{5,7},{6,4},{7,5},{8,10},{9,11},{10,... | collective-permute-start | bytes 393224 | tf_op jit(solution)/shard_map/ppermute | solution.py:71
  19.2 12.3 %collective-permute-start.10 = (bf16[512,128]{1,0:T(8,128)(2,1)S(1)}, bf16[512,128]{1,0:T(8,128)(2,1)S(1)}, u32[]{:S(2)}, u32[]{:S(2)}) collective-permute-start(bf16[512,128]{1,0:T(8,128)(2,1)S(1)} %get-tuple-element.43.refs_0_), channel_id=1, source_target_pairs={{0,2},{1,3},{2,0},{3,1},{4,6},{5,7},{6,4},{7,5},{8,10},{9,11},{10,... | collective-permute-start | bytes 393224 | tf_op jit(solution)/shard_map/ppermute | solution.py:71
  20.9 10.6 %collective-permute-start.12 = (bf16[128,512]{1,0:T(8,128)(2,1)S(1)}, bf16[128,512]{1,0:T(8,128)(2,1)S(1)}, u32[]{:S(2)}, u32[]{:S(2)}) collective-permute-start(bf16[128,512]{1,0:T(8,128)(2,1)S(1)} %get-tuple-element.44.refs_4_), channel_id=1, source_target_pairs={{0,1},{1,0},{2,3},{3,2},{4,5},{5,4},{6,7},{7,6},{8,9},{9,8},{10,11... | collective-permute-start | bytes 393224 | tf_op jit(solution)/shard_map/ppermute | solution.py:71
  29.1 2.9 %collective-permute-start.14 = (bf16[128,512]{1,0:T(8,128)(2,1)S(1)}, bf16[128,512]{1,0:T(8,128)(2,1)S(1)}, u32[]{:S(2)}, u32[]{:S(2)}) collective-permute-start(bf16[128,512]{1,0:T(8,128)(2,1)S(1)} %collective-permute-done.13.refs_6_), channel_id=1, source_target_pairs={{0,1},{1,0},{2,3},{3,2},{4,5},{5,4},{6,7},{7,6},{8,9},{9,8},{10,11... | collective-permute-start | bytes 393224 | tf_op jit(solution)/shard_map/ppermute | solution.py:71
  29.1 2.9 %collective-permute-start.9 = (bf16[512,128]{1,0:T(8,128)(2,1)S(1)}, bf16[512,128]{1,0:T(8,128)(2,1)S(1)}, u32[]{:S(2)}, u32[]{:S(2)}) collective-permute-start(bf16[512,128]{1,0:T(8,128)(2,1)S(1)} %get-tuple-element.43.refs_0_), channel_id=1, source_target_pairs={{0,1},{1,0},{2,3},{3,2},{4,5},{5,4},{6,7},{7,6},{8,9},{9,8},{10,11... | collective-permute-start | bytes 393224 | tf_op jit(solution)/shard_map/ppermute | solution.py:71
  31.5 1.3 %collective-permute-start.11 = (bf16[512,128]{1,0:T(8,128)(2,1)S(1)}, bf16[512,128]{1,0:T(8,128)(2,1)S(1)}, u32[]{:S(2)}, u32[]{:S(2)}) collective-permute-start(bf16[512,128]{1,0:T(8,128)(2,1)S(1)} %collective-permute-done.10.refs_2_), channel_id=1, source_target_pairs={{0,1},{1,0},{2,3},{3,2},{4,5},{5,4},{6,7},{7,6},{8,9},{9,8},{10,11... | collective-permute-start | bytes 393224 | tf_op jit(solution)/shard_map/ppermute | solution.py:71
  31.5 19.7 %collective-permute-start.8 = (bf16[128,1024]{1,0:T(8,128)(2,1)S(1)}, bf16[128,1024]{1,0:T(8,128)(2,1)S(1)}, u32[]{:S(2)}, u32[]{:S(2)}) collective-permute-start(bf16[128,1024]{1,0:T(8,128)(2,1)S(1)} %get-tuple-element.37.refs_3_), channel_id=1, source_target_pairs={{0,1},{1,0},{2,3},{3,2},{4,5},{5,4},{6,7},{7,6},{8,9},{9,8},{10,11... | collective-permute-start | bytes 786440 | tf_op jit(solution)/shard_map/ppermute | solution.py:71
  32.0 23.0 %collective-permute-start.7 = (bf16[128,1024]{1,0:T(8,128)(2,1)S(1)}, bf16[128,1024]{1,0:T(8,128)(2,1)S(1)}, u32[]{:S(2)}, u32[]{:S(2)}) collective-permute-start(bf16[128,1024]{1,0:T(8,128)(2,1)S(1)} %collective-permute-done.6.refs_3_), channel_id=1, source_target_pairs={{0,1},{1,0},{2,3},{3,2},{4,5},{5,4},{6,7},{7,6},{8,9},{9,8},{10,11... | collective-permute-start | bytes 786440 | tf_op jit(solution)/shard_map/ppermute | solution.py:71
  33.2 4.3 %collective-permute-start.15 = (bf16[128,256]{1,0:T(8,128)(2,1)S(1)}, bf16[128,256]{1,0:T(8,128)(2,1)S(1)}, u32[]{:S(2)}, u32[]{:S(2)}) collective-permute-start(bf16[128,256]{1,0:T(8,128)(2,1)S(1)} %get-tuple-element.47), channel_id=1, source_target_pairs={{0,4},{4,0},{8,12},{12,8},{16,20},{20,16},{24,28},{28,24},{1,5},{5... | collective-permute-start | bytes 196616 | tf_op jit(solution)/shard_map/ppermute | solution.py:91
  35.0 4.8 %collective-permute-start.16 = (bf16[128,256]{1,0:T(8,128)(2,1)S(1)}, bf16[128,256]{1,0:T(8,128)(2,1)S(1)}, u32[]{:S(2)}, u32[]{:S(2)}) collective-permute-start(bf16[128,256]{1,0:T(8,128)(2,1)S(1)} %get-tuple-element.48), channel_id=1, source_target_pairs={{0,8},{4,12},{8,0},{12,4},{16,24},{20,28},{24,16},{28,20},{1,9},{5... | collective-permute-start | bytes 196616 | tf_op jit(solution)/shard_map/ppermute | solution.py:91
  36.6 5.2 %collective-permute-start.17 = (bf16[128,256]{1,0:T(8,128)(2,1)S(1)}, bf16[128,256]{1,0:T(8,128)(2,1)S(1)}, u32[]{:S(2)}, u32[]{:S(2)}) collective-permute-start(bf16[128,256]{1,0:T(8,128)(2,1)S(1)} %get-tuple-element.49), channel_id=1, source_target_pairs={{0,12},{4,8},{8,4},{12,0},{16,28},{20,24},{24,20},{28,16},{1,13},{... | collective-permute-start | bytes 196616 | tf_op jit(solution)/shard_map/ppermute | solution.py:91
  41.8 5.8 %collective-permute-start.18 = (bf16[128,256]{1,0:T(8,128)(2,1)S(1)}, bf16[128,256]{1,0:T(8,128)(2,1)S(1)}, u32[]{:S(2)}, u32[]{:S(2)}) collective-permute-start(bf16[128,256]{1,0:T(8,128)(2,1)S(1)} %shard_map.135.refs_0_), channel_id=1, source_target_pairs={{0,16},{4,20},{8,24},{12,28},{16,0},{20,4},{24,8},{28,12},{1,17},{... | collective-permute-start | bytes 196616 | tf_op jit(solution)/shard_map/ppermute | solution.py:91
  47.7 4.6 %collective-permute-start.19 = (bf16[128,256]{1,0:T(8,128)(2,1)S(1)}, bf16[128,256]{1,0:T(8,128)(2,1)S(1)}, u32[]{:S(2)}, u32[]{:S(2)}) collective-permute-start(bf16[128,256]{1,0:T(8,128)(2,1)S(1)} %shard_map.136.refs_0_), channel_id=1, source_target_pairs={{0,4},{4,0},{8,12},{12,8},{16,20},{20,16},{24,28},{28,24},{1,5},{5... | collective-permute-start | bytes 196616 | tf_op jit(solution)/shard_map/ppermute | solution.py:91
  48.3 4.3 %collective-permute-start.20 = (bf16[128,256]{1,0:T(8,128)(2,1)S(1)}, bf16[128,256]{1,0:T(8,128)(2,1)S(1)}, u32[]{:S(2)}, u32[]{:S(2)}) collective-permute-start(bf16[128,256]{1,0:T(8,128)(2,1)S(1)} %shard_map.136.refs_0_), channel_id=1, source_target_pairs={{0,8},{4,12},{8,0},{12,4},{16,24},{20,28},{24,16},{28,20},{1,9},{5... | collective-permute-start | bytes 196616 | tf_op jit(solution)/shard_map/ppermute | solution.py:91
  48.8 5.3 %collective-permute-start.21 = (bf16[128,256]{1,0:T(8,128)(2,1)S(1)}, bf16[128,256]{1,0:T(8,128)(2,1)S(1)}, u32[]{:S(2)}, u32[]{:S(2)}) collective-permute-start(bf16[128,256]{1,0:T(8,128)(2,1)S(1)} %shard_map.136.refs_0_), channel_id=1, source_target_pairs={{0,12},{4,8},{8,4},{12,0},{16,28},{20,24},{24,20},{28,16},{1,13},{... | collective-permute-start | bytes 196616 | tf_op jit(solution)/shard_map/ppermute | solution.py:91
